TPU v7x, 32 devices: a whole 2x2x4 slice. The times are simulated.
32 devices in a mesh: dp: 2 (over x), ctx: 4 (over z), tp: 4 (over y, core).
Axes of the slice: x: 2, y: 2, z: 4, core: 2. Of those that a mesh axis runs over, the one named last changes fastest.
Arguments:
- hidden_in: bfloat16 [2, 1024, 1536], P('dp', 'ctx'), may hold values from -6 to 6
- segment_ids: int32 [2, 1024], P('dp', 'ctx'), may hold values from 0 to 2, never falling along the last dimension, each value on 1 to 512 neighbouring positions
- cotangent: bfloat16 [2, 1024, 1536], P('dp', 'ctx'), may hold values from -6 to 6
- norm_gain: bfloat16 [2, 1536], replicated, may hold values from 0.5 to 1.5
- gate_proj: bfloat16 [2, 1536, 3072], P(None, ('dp', 'ctx'), 'tp'), may hold values from -0.15625 to 0.15625
- value_proj: bfloat16 [2, 1536, 3072], P(None, ('dp', 'ctx'), 'tp'), may hold values from -0.15625 to 0.15625
- bc_proj: bfloat16 [2, 1536, 256], P(None, ('dp', 'ctx')), may hold values from -0.15625 to 0.15625
- step_proj: bfloat16 [2, 1536, 48], P(None, ('dp', 'ctx'), 'tp'), may hold values from -0.15625 to 0.15625
- conv_value: bfloat16 [2, 4, 3072], P(None, None, 'tp'), may hold values from -3 to 3
- conv_value_bias: bfloat16 [2, 3072], P(None, 'tp'), may hold values from -3 to 3
- conv_bc: bfloat16 [2, 4, 256], replicated, may hold values from -3 to 3
- conv_bc_bias: bfloat16 [2, 256], replicated, may hold values from -3 to 3
- decay_log: float32 [2, 48], P(None, 'tp'), may hold values from -5 to 1
- step_bias: float32 [2, 48], P(None, 'tp'), may hold values from -6 to 0
- skip_gain: float32 [2, 48], P(None, 'tp'), may hold values from 0.5 to 1.5
- out_gain: bfloat16 [2, 3072], P(None, 'tp'), may hold values from 0.5 to 1.5
- out_proj: bfloat16 [2, 3072, 1536], P(None, 'tp', ('dp', 'ctx')), may hold values from -0.109375 to 0.109375
Outputs:
- hidden_out: bfloat16 [2, 1024, 1536], P('dp', 'ctx')
- grad_hidden: bfloat16 [2, 1024, 1536], P('dp', 'ctx')
- grad_norm_gain: float32 [2, 1536], replicated
- grad_gate_proj: float32 [2, 1536, 3072], P(None, ('dp', 'ctx'), 'tp')
- grad_value_proj: float32 [2, 1536, 3072], P(None, ('dp', 'ctx'), 'tp')
- grad_bc_proj: float32 [2, 1536, 256], P(None, ('dp', 'ctx'))
- grad_step_proj: float32 [2, 1536, 48], P(None, ('dp', 'ctx'), 'tp')
- grad_conv_value: float32 [2, 4, 3072], P(None, None, 'tp')
- grad_conv_value_bias: float32 [2, 3072], P(None, 'tp')
- grad_conv_bc: float32 [2, 4, 256], replicated
- grad_conv_bc_bias: float32 [2, 256], replicated
- grad_decay_log: float32 [2, 48], P(None, 'tp')
- grad_step_bias: float32 [2, 48], P(None, 'tp')
- grad_skip_gain: float32 [2, 48], P(None, 'tp')
- grad_out_gain: float32 [2, 3072], P(None, 'tp')
- grad_out_proj: float32 [2, 3072, 1536], P(None, 'tp', ('dp', 'ctx'))
Inputs may be any that keep to these rules, and one draw needn't show every extreme that they name: `segment_ids`: along each sequence the numbers never fall and every number from 0 to the most occurs; a document is the run of positions with one number.
All inputs are finite; a program needn't handle non-finite values.
Results may differ from a plain program's by a relative error of at most 0.02.
Values may be sent and summed in bfloat16 or wider, within the bound.
A program may use at most 192 MiB of HBM per device.

v0:
```python
from functools import partial

import jax
import jax.numpy as jnp
from jax import lax
from jax.sharding import PartitionSpec as P

HEADDIM = 64
BLOCK = 256
LAYERS = 2
INNER = 3072


epsilon = 1e-05
precise = lax.Precision.HIGH


def from_behind(block, axis, distance):
    devices = range(lax.axis_size(axis))
    route = [(i - distance, i) for i in devices if i - distance in devices]
    return lax.ppermute(block, axis, route)


def round_keep(values):
    return lax.optimization_barrier(values.astype(jnp.bfloat16)).astype(jnp.float32)


def dot_back(left_rows, right_rows):
    return lax.dot_general(
        left_rows, right_rows, (((1,), (1,)), ((), ())), preferred_element_type=jnp.float32
    )


def dot_left(left_rows, right_rows):
    return lax.dot_general(
        left_rows, right_rows, (((0,), (0,)), ((), ())), preferred_element_type=jnp.float32
    )


def conv_local(signal, edge_rows, kernel, conv_bias, segment, edge_segment):
    tap_count = kernel.shape[0]
    length = signal.shape[1]
    padded = jnp.concatenate([edge_rows, signal], axis=1)
    seg_pad = jnp.concatenate([edge_segment, segment], axis=1)
    result = conv_bias + jnp.zeros_like(signal)
    for tap_index in range(tap_count):
        same_doc = (seg_pad[:, tap_index : tap_index + length] == segment).astype(jnp.float32)
        result = (
            result
            + kernel[tap_index] * padded[:, tap_index : tap_index + length] * same_doc[:, :, None]
        )
    return jax.nn.silu(result)


def block_step(decay_rates, carried, block_data):
    states, prev_segment = carried
    values, b_mat, c_mat, step_size, segment = block_data
    length = values.shape[0]
    log_decay = jnp.cumsum(step_size * decay_rates, axis=0)
    positions = jnp.arange(length)
    causal = positions[:, None] >= positions[None, :]
    same_doc = jnp.logical_and(segment[:, None] == segment[None, :], causal)[:, :, None]
    differ = jnp.where(same_doc, log_decay[:, None, :] - log_decay[None, :, :], 0.0)
    weights = jnp.where(same_doc, jnp.exp(differ), 0.0)
    cb_product = jnp.dot(c_mat, b_mat.T, precision=precise)
    scores = cb_product[:, :, None] * weights * step_size[None, :, :]
    intra_out = jnp.einsum("tsh,shp->thp", scores, values, precision=precise)
    alive_mask = (segment == prev_segment).astype(jnp.float32)
    reach = alive_mask[:, None] * jnp.exp(log_decay)
    inter_out = reach[:, :, None] * jnp.einsum("tn,hpn->thp", c_mat, states, precision=precise)
    end_same = (segment == segment[length - 1]).astype(jnp.float32)
    to_end = jnp.exp(log_decay[length - 1][None, :] - log_decay) * end_same[:, None] * step_size
    weighted_values = to_end[:, :, None] * values
    new_states = reach[length - 1][:, None, None] * states + jnp.einsum(
        "shp,sn->hpn", weighted_values, b_mat, precision=precise
    )
    return ((new_states, segment[length - 1]), intra_out + inter_out)


def device_scan(values, b_mat, c_mat, step_size, decay_rates, segment, seg_prev):
    block_count = values.shape[0] // BLOCK
    heads_local = values.shape[1]
    state_dim = b_mat.shape[1]
    blocks = (
        values.reshape(block_count, BLOCK, heads_local, HEADDIM),
        b_mat.reshape(block_count, BLOCK, state_dim),
        c_mat.reshape(block_count, BLOCK, state_dim),
        step_size.reshape(block_count, BLOCK, heads_local),
        segment.reshape(block_count, BLOCK),
    )
    initial = (jnp.zeros((heads_local, HEADDIM, state_dim), jnp.float32), seg_prev)
    final_carry, outputs = lax.scan(partial(block_step, decay_rates), initial, blocks)
    return (outputs.reshape(values.shape), final_carry[0])


def step_terms(step_pre, step_bias, decay_log):
    return (jax.nn.softplus(step_pre + step_bias), -jnp.exp(decay_log))


def mixer_terms(values, bc_conv, step_size, decay_rates, skip_gain, segment, seg_prev):
    seq_count, tokens, inner_local = values.shape
    heads_local = step_size.shape[2]
    heads_in = values.reshape(seq_count, tokens, heads_local, HEADDIM)
    state_dim = bc_conv.shape[2] // 2
    scanner = jax.vmap(device_scan, in_axes=(0, 0, 0, 0, None, 0, 0))
    intra_out, local_states = scanner(
        heads_in,
        bc_conv[:, :, :state_dim],
        bc_conv[:, :, state_dim:],
        step_size,
        decay_rates,
        segment,
        seg_prev,
    )
    alive_last = (segment[:, tokens - 1] == seg_prev).astype(jnp.float32)
    decays = alive_last[:, None] * jnp.exp(jnp.sum(step_size * decay_rates, axis=1))
    return (intra_out + skip_gain[:, None] * heads_in, local_states, decays)


def carried_terms(bc_conv, step_size, decay_rates, entering, segment, seg_prev):
    state_dim = bc_conv.shape[2] // 2
    c_mat = bc_conv[:, :, state_dim:]
    log_decay = jnp.cumsum(step_size * decay_rates, axis=1)
    alive_mask = (segment == seg_prev[:, None]).astype(jnp.float32)
    reach = alive_mask[:, :, None] * jnp.exp(log_decay)
    carried = jnp.einsum("sqn,shpn->sqhp", c_mat, entering, precision=precise)
    return reach[:, :, :, None] * carried


def chain_forward(decays, local_states):

    def handoff(step_index, entering):
        return from_behind(decays[:, :, None, None] * entering + local_states, "ctx", 1)

    return lax.fori_loop(0, lax.axis_size("ctx") - 1, handoff, jnp.zeros_like(local_states))


def chain_backward(decays, grad_entering):

    def handback(step_index, beyond):
        return from_behind(
            (grad_entering + decays[:, :, None, None] * beyond).astype(jnp.bfloat16), "ctx", -1
        ).astype(jnp.float32)

    return lax.fori_loop(0, lax.axis_size("ctx") - 1, handback, jnp.zeros_like(grad_entering))


def layer_forward(hidden, segment, layer_params):
    (
        norm_gain,
        gate_proj,
        value_proj,
        bc_proj,
        step_proj,
        conv_value,
        conv_value_bias,
        conv_bc,
        conv_bc_bias,
        decay_log,
        step_bias,
        skip_gain,
        out_gain,
        out_proj,
    ) = layer_params
    seq_count, tokens, model_width = hidden.shape
    row_count = seq_count * tokens
    tap_count = conv_value.shape[0]
    gathered = (
        lax.all_gather(gate_proj, ("dp", "ctx"), axis=0, tiled=True),
        lax.all_gather(value_proj, ("dp", "ctx"), axis=0, tiled=True),
        lax.all_gather(bc_proj, ("dp", "ctx"), axis=0, tiled=True),
        lax.all_gather(step_proj, ("dp", "ctx"), axis=0, tiled=True),
        lax.all_gather(out_proj, ("dp", "ctx"), axis=1, tiled=True),
    )
    gate_full, value_full, bc_full, step_full, out_full = gathered
    hidden_rows = hidden.reshape(row_count, model_width)
    inv_norm = lax.rsqrt(jnp.mean(hidden_rows * hidden_rows, axis=1, keepdims=True) + epsilon)
    normed = (hidden_rows * inv_norm * norm_gain).astype(jnp.bfloat16)
    gate_pre = jnp.dot(normed, gate_full, preferred_element_type=jnp.float32)
    value_pre = jnp.dot(normed, value_full, preferred_element_type=jnp.float32).reshape(
        seq_count, tokens, -1
    )
    bc_pre = jnp.dot(normed, bc_full, preferred_element_type=jnp.float32).reshape(
        seq_count, tokens, -1
    )
    step_pre = jnp.dot(normed, step_full, preferred_element_type=jnp.float32).reshape(
        seq_count, tokens, -1
    )
    first_edge = tokens - tap_count + 1
    edge_value, edge_bc, edge_segment = from_behind(
        (value_pre[:, first_edge:], bc_pre[:, first_edge:], segment[:, first_edge:]), "ctx", 1
    )
    conv_fn = partial(conv_local, segment=segment, edge_segment=edge_segment)
    value_act, value_pull = jax.vjp(conv_fn, value_pre, edge_value, conv_value, conv_value_bias)
    bc_act, bc_pull = jax.vjp(conv_fn, bc_pre, edge_bc, conv_bc, conv_bc_bias)
    values = round_keep(value_act)
    bc_conv = round_keep(bc_act)
    seg_prev = edge_segment[:, tap_count - 2]
    (step_size, decay_rates), step_pull = jax.vjp(step_terms, step_pre, step_bias, decay_log)
    (local_out, local_states, decays), local_pull = jax.vjp(
        partial(mixer_terms, segment=segment, seg_prev=seg_prev),
        values,
        bc_conv,
        step_size,
        decay_rates,
        skip_gain,
    )
    entering = chain_forward(decays, local_states)
    carried_out, carried_pull = jax.vjp(
        partial(carried_terms, segment=segment, seg_prev=seg_prev),
        bc_conv,
        step_size,
        decay_rates,
        entering,
    )
    mixed = (local_out + carried_out).reshape(row_count, -1)
    gate_act = jax.nn.silu(gate_pre)
    gated = mixed * gate_act
    square_sum = lax.psum(jnp.sum(gated * gated, axis=1), "tp")
    inv_gate = lax.rsqrt(square_sum / INNER + epsilon)[:, None]
    scaled = (gated * inv_gate * out_gain).astype(jnp.bfloat16)
    mixer_sum = lax.psum(jnp.dot(scaled, out_full, preferred_element_type=jnp.float32), "tp")
    kept = {
        "scaled": scaled,
        "gated": gated,
        "inv_gate": inv_gate,
        "gate_pre": gate_pre,
        "gate_act": gate_act,
        "mixed": mixed,
        "carried_pull": carried_pull,
        "local_pull": local_pull,
        "step_pull": step_pull,
        "value_pull": value_pull,
        "bc_pull": bc_pull,
        "decays": decays,
        "entering": entering,
        "hidden_rows": hidden_rows,
        "inv_norm": inv_norm,
        "normed": normed,
    }
    return (hidden + mixer_sum.reshape(seq_count, tokens, model_width), kept)


def layer_backward(grad_hidden, kept, layer_params):
    (
        norm_gain,
        gate_proj,
        value_proj,
        bc_proj,
        step_proj,
        conv_value,
        conv_value_bias,
        conv_bc,
        conv_bc_bias,
        decay_log,
        step_bias,
        skip_gain,
        out_gain,
        out_proj,
    ) = layer_params
    seq_count, tokens, model_width = grad_hidden.shape
    row_count = seq_count * tokens
    tap_count = conv_value.shape[0]
    gate_full, value_full, bc_full, step_full, out_full = (
        lax.all_gather(gate_proj, ("dp", "ctx"), axis=0, tiled=True),
        lax.all_gather(value_proj, ("dp", "ctx"), axis=0, tiled=True),
        lax.all_gather(bc_proj, ("dp", "ctx"), axis=0, tiled=True),
        lax.all_gather(step_proj, ("dp", "ctx"), axis=0, tiled=True),
        lax.all_gather(out_proj, ("dp", "ctx"), axis=1, tiled=True),
    )
    grad_rows = grad_hidden.reshape(row_count, model_width)
    grad_low = grad_rows.astype(jnp.bfloat16)
    grad_scaled = dot_back(grad_low, out_full)
    grad_out_proj = dot_left(kept["scaled"], grad_low)
    gated = kept["gated"]
    inv_gate = kept["inv_gate"]
    weighted = grad_scaled * out_gain
    inner_sum = lax.psum(jnp.sum(weighted * gated, axis=1), "tp")
    grad_gated = inv_gate * weighted - gated * inv_gate**3 * (inner_sum / INNER)[:, None]
    grad_out_gain = jnp.sum(grad_scaled * gated * inv_gate, axis=0)
    gate_pre = kept["gate_pre"]
    sigmoid_gate = jax.nn.sigmoid(gate_pre)
    grad_gate_pre = (
        grad_gated * kept["mixed"] * sigmoid_gate * (1.0 + gate_pre * (1.0 - sigmoid_gate))
    )
    grad_heads = (grad_gated * kept["gate_act"]).reshape(
        seq_count, tokens, step_full.shape[1], HEADDIM
    )
    carried_bc, carried_step, carried_rates, grad_entering = kept["carried_pull"](grad_heads)
    beyond = chain_backward(kept["decays"], grad_entering)
    grad_decays = jnp.sum(beyond * kept["entering"], axis=(2, 3))
    local_values, local_bc, local_step, local_rates, grad_skip = kept["local_pull"](
        (grad_heads, beyond, grad_decays)
    )
    grad_step_pre, grad_step_bias, grad_decay_log = kept["step_pull"](
        (carried_step + local_step, carried_rates + local_rates)
    )
    grad_value_pre, grad_edge_value, grad_conv_value, grad_conv_value_bias = kept["value_pull"](
        local_values
    )
    grad_bc_pre, grad_edge_bc, grad_conv_bc, grad_conv_bc_bias = kept["bc_pull"](
        carried_bc + local_bc
    )
    from_value, from_bc = from_behind((grad_edge_value, grad_edge_bc), "ctx", -1)
    first_edge = tokens - tap_count + 1
    grad_value_pre = grad_value_pre.at[:, first_edge:].add(from_value)
    grad_bc_pre = grad_bc_pre.at[:, first_edge:].add(from_bc)
    grad_gate_low = grad_gate_pre.astype(jnp.bfloat16)
    grad_value_low = grad_value_pre.reshape(row_count, -1).astype(jnp.bfloat16)
    grad_step_low = grad_step_pre.reshape(row_count, -1).astype(jnp.bfloat16)
    input_part = (
        dot_back(grad_gate_low, gate_full)
        + dot_back(grad_value_low, value_full)
        + dot_back(grad_step_low, step_full)
    )
    input_sum, bc_sum, conv_bc_sum, conv_bc_bias_sum = (
        lax.psum(input_part.astype(jnp.bfloat16), "tp").astype(jnp.float32),
        lax.psum(grad_bc_pre.reshape(row_count, -1).astype(jnp.bfloat16), "tp").astype(jnp.float32),
        lax.psum(grad_conv_bc, "tp").astype(jnp.float32),
        lax.psum(grad_conv_bc_bias, "tp").astype(jnp.float32),
    )
    grad_bc_low = bc_sum.astype(jnp.bfloat16)
    grad_normed = input_sum + dot_back(grad_bc_low, bc_full)
    hidden_rows = kept["hidden_rows"]
    inv_norm = kept["inv_norm"]
    weighted_norm = grad_normed * norm_gain
    grad_norm_gain = jnp.sum(grad_normed * hidden_rows * inv_norm, axis=0)
    grad_rows = (
        grad_rows
        + inv_norm * weighted_norm
        - hidden_rows * inv_norm**3 * jnp.mean(weighted_norm * hidden_rows, axis=1, keepdims=True)
    )
    normed = kept["normed"]
    proj_grads = (
        lax.psum_scatter(
            dot_left(normed, grad_gate_low).astype(jnp.bfloat16),
            ("dp", "ctx"),
            scatter_dimension=0,
            tiled=True,
        ).astype(jnp.float32),
        lax.psum_scatter(
            dot_left(normed, grad_value_low).astype(jnp.bfloat16),
            ("dp", "ctx"),
            scatter_dimension=0,
            tiled=True,
        ).astype(jnp.float32),
        lax.psum_scatter(
            dot_left(normed, grad_bc_low).astype(jnp.bfloat16),
            ("dp", "ctx"),
            scatter_dimension=0,
            tiled=True,
        ).astype(jnp.float32),
        lax.psum_scatter(
            dot_left(normed, grad_step_low).astype(jnp.bfloat16),
            ("dp", "ctx"),
            scatter_dimension=0,
            tiled=True,
        ).astype(jnp.float32),
        lax.psum_scatter(
            grad_out_proj.astype(jnp.bfloat16), ("dp", "ctx"), scatter_dimension=1, tiled=True
        ).astype(jnp.float32),
    )
    small_grads = lax.psum(
        (
            grad_norm_gain,
            grad_conv_value.astype(jnp.float32),
            grad_conv_value_bias.astype(jnp.float32),
            conv_bc_sum,
            conv_bc_bias_sum,
            grad_decay_log,
            grad_step_bias,
            grad_skip,
            grad_out_gain,
        ),
        ("dp", "ctx"),
    )
    return (grad_rows.reshape(seq_count, tokens, model_width), proj_grads, small_grads)


def stack_layers(groups, member):
    return jnp.stack([groups[layer_index][member] for layer_index in range(LAYERS)])


def local(
    hidden_in,
    segment_ids,
    cotangent,
    norm_gain,
    gate_proj,
    value_proj,
    bc_proj,
    step_proj,
    conv_value,
    conv_value_bias,
    conv_bc,
    conv_bc_bias,
    decay_log,
    step_bias,
    skip_gain,
    out_gain,
    out_proj,
):
    params = (
        norm_gain,
        gate_proj,
        value_proj,
        bc_proj,
        step_proj,
        conv_value,
        conv_value_bias,
        conv_bc,
        conv_bc_bias,
        decay_log,
        step_bias,
        skip_gain,
        out_gain,
        out_proj,
    )
    segment = segment_ids.astype(jnp.float32)
    hidden = hidden_in.astype(jnp.float32)
    kept_layers = []
    for layer_index in range(LAYERS):
        hidden, kept = layer_forward(
            hidden, segment, tuple((stacked[layer_index] for stacked in params))
        )
        kept_layers.append(kept)
    grad_hidden = cotangent.astype(jnp.float32)
    proj_list = [None] * LAYERS
    small_list = [None] * LAYERS
    for layer_index in reversed(range(LAYERS)):
        grad_hidden, proj_list[layer_index], small_list[layer_index] = layer_backward(
            grad_hidden,
            kept_layers[layer_index],
            tuple((stacked[layer_index] for stacked in params)),
        )
    return (
        hidden.astype(jnp.bfloat16),
        grad_hidden.astype(jnp.bfloat16),
        stack_layers(small_list, 0),
        stack_layers(proj_list, 0),
        stack_layers(proj_list, 1),
        stack_layers(proj_list, 2),
        stack_layers(proj_list, 3),
        stack_layers(small_list, 1),
        stack_layers(small_list, 2),
        stack_layers(small_list, 3),
        stack_layers(small_list, 4),
        stack_layers(small_list, 5),
        stack_layers(small_list, 6),
        stack_layers(small_list, 7),
        stack_layers(small_list, 8),
        stack_layers(proj_list, 4),
    )


def solution(mesh):
    in_specs = (
        P("dp", "ctx", None),
        P("dp", "ctx"),
        P("dp", "ctx", None),
        P(),
        P(None, ("dp", "ctx"), "tp"),
        P(None, ("dp", "ctx"), "tp"),
        P(None, ("dp", "ctx"), None),
        P(None, ("dp", "ctx"), "tp"),
        P(None, None, "tp"),
        P(None, "tp"),
        P(),
        P(),
        P(None, "tp"),
        P(None, "tp"),
        P(None, "tp"),
        P(None, "tp"),
        P(None, "tp", ("dp", "ctx")),
    )
    out_specs = (
        P("dp", "ctx", None),
        P("dp", "ctx", None),
        P(),
        P(None, ("dp", "ctx"), "tp"),
        P(None, ("dp", "ctx"), "tp"),
        P(None, ("dp", "ctx"), None),
        P(None, ("dp", "ctx"), "tp"),
        P(None, None, "tp"),
        P(None, "tp"),
        P(),
        P(),
        P(None, "tp"),
        P(None, "tp"),
        P(None, "tp"),
        P(None, "tp"),
        P(None, "tp", ("dp", "ctx")),
    )
    return jax.shard_map(local, mesh=mesh, in_specs=in_specs, out_specs=out_specs, check_vma=False)
```

profile of v0, /device:TPU:0, one launch (start us, length us, event | category | flops | bytes accessed | tf_op | source)
XLA Modules:
  0.0 1505.7 jit_solution(9590833574922225550)
XLA Ops:
  10.4 4.9 collective-permute-start.5
  16.9 38.2 %all-gather.1 = bf16[1,1536,256]{2,1,0:T(8,128)(2,1)S(1)} all-gather(bf16[1,192,256]{2,1,0:T(8,128)(2,1)S(1)} %get-tuple-element.1049), channel_id=3, replica_groups=mesh['dp'=2,'ctx'=4,'tp'=4] {'dp','ctx'}, dimensions={1}, use_global_device_ids=true | all-gather | bytes 884736 | tf_op jit(solution)/shard_map/all_gather | solution.py:171
  58.8 36.9 %all-gather.2 = bf16[1,1536,12]{2,0,1:T(2,128)(2,1)S(1)} all-gather(bf16[1,192,12]{2,0,1:T(2,128)(2,1)S(1)} %copy.295), channel_id=4, replica_groups=mesh['dp'=2,'ctx'=4,'tp'=4] {'dp','ctx'}, dimensions={1}, use_global_device_ids=true | all-gather | bytes 41472 | tf_op jit(solution)/shard_map/all_gather | solution.py:172
  124.0 41.3 %while.34 = (s32[]{:T(128)}, f32[1,12,64,128]{3,2,1,0:T(8,128)S(1)}, f32[1,12]{1,0:T(1,128)S(1)}, f32[1,12,64,128]{3,2,1,0:T(8,128)S(1)}, s32[]{:T(128)}) while((s32[]{:T(128)}, f32[1,12,64,128]{3,2,1,0:T(8,128)S(1)}, f32[1,12]{1,0:T(1,128)S(1)}, f32[1,12,64,128]{3,2,1,0:T(8,128)S(1)}, s32[]{:T(128)}) %tuple.262), condition=%wide.region_5.7_spmd, body=%wide.region_4.6_spmd.sunk | while | flops 196610 | bytes 2752661 | solution.py:135
  124.1 4.5 collective-permute-start
  128.6 8.9 collective-permute-done
  137.7 4.4 collective-permute-start
  142.1 10.9 collective-permute-done
  153.1 4.4 collective-permute-start
  157.5 7.7 collective-permute-done
  165.7 4.2 fusion.96
  171.3 3.7 multiply_reduce_fusion.21
  175.1 6.0 psum.224
  181.7 11.8 all-gather.21.cloned.1.call-done
  193.6 3.7 convolution_bitcast_fusion.1
  199.4 33.8 %all-gather.7 = bf16[1,1536,12]{2,0,1:T(2,128)(2,1)S(1)} all-gather(bf16[1,192,12]{2,0,1:T(2,128)(2,1)S(1)} %copy.296), channel_id=9, replica_groups=mesh['dp'=2,'ctx'=4,'tp'=4] {'dp','ctx'}, dimensions={1}, use_global_device_ids=true | all-gather | bytes 41472 | tf_op jit(solution)/shard_map/all_gather | solution.py:172
  233.7 38.2 %all-gather.6 = bf16[1,1536,256]{2,1,0:T(8,128)(2,1)} all-gather(bf16[1,192,256]{2,1,0:T(8,128)(2,1)S(1)} %copy-done.98), channel_id=8, replica_groups=mesh['dp'=2,'ctx'=4,'tp'=4] {'dp','ctx'}, dimensions={1}, use_global_device_ids=true | all-gather | bytes 884736 | tf_op jit(solution)/shard_map/all_gather | solution.py:171
  276.3 18.8 %all-gather.23.cloned.1.call-done = bf16[1,1536,768]{2,1,0:T(8,128)(2,1)} async-done(((bf16[1,192,768]{2,1,0:T(8,128)(2,1)}), bf16[1,1536,768]{2,1,0:T(8,128)(2,1)}) %all-gather.23.cloned.1.call-update) | async-done | bytes 2359312 | tf_op jit(solution)/shard_map/all_gather | solution.py:170
  332.9 60.1 %while.35 = (s32[]{:T(128)}, f32[1,12,64,128]{3,2,1,0:T(8,128)S(1)}, f32[1,12]{1,0:T(1,128)}, f32[1,12,64,128]{3,2,1,0:T(8,128)}, s32[]{:T(128)}) while((s32[]{:T(128)}, f32[1,12,64,128]{3,2,1,0:T(8,128)S(1)}, f32[1,12]{1,0:T(1,128)}, f32[1,12,64,128]{3,2,1,0:T(8,128)}, s32[]{:T(128)}) %tuple.265), condition=%wide.region_14.16_spmd, body=%wide.region_13.15_spmd.sunk | while | flops 196610 | bytes 2752661 | solution.py:135
  337.2 14.5 collective-permute-done.1
  353.6 4.3 collective-permute-start.1
  357.9 12.8 collective-permute-done.1
  372.6 7.9 collective-permute-start.1
  380.4 12.5 collective-permute-done.1
  394.2 4.5 fusion.97
  401.0 4.4 multiply_reduce_fusion.20
  405.4 6.3 psum.226
  413.0 4.4 multiply_reduce_fusion.2
  417.4 7.2 psum.228
  425.2 4.1 fusion.123
  435.3 44.0 %while.36 = (s32[]{:T(128)}, f32[1,12,64,128]{3,2,1,0:T(8,128)S(1)}, f32[1,12]{1,0:T(1,128)}, f32[1,12,64,128]{3,2,1,0:T(8,128)}, s32[]{:T(128)}, /*index=5*/s32[]{:T(128)}) while((s32[]{:T(128)}, f32[1,12,64,128]{3,2,1,0:T(8,128)S(1)}, f32[1,12]{1,0:T(1,128)}, f32[1,12,64,128]{3,2,1,0:T(8,128)}, s32[]{:T(128)}, ...), condition=%wide.region_21.23_spmd.clone, body=%wide.region_20.22_spmd.clone.sunk | while | flops 491523 | bytes 2359463 | solution.py:145
  438.3 17.4 %collective-permute-done.2 = bf16[1,12,64,128]{3,2,1,0:T(8,128)(2,1)} collective-permute-done((bf16[1,12,64,128]{3,2,1,0:T(8,128)(2,1)}, bf16[1,12,64,128]{3,2,1,0:T(8,128)(2,1)}, u32[]{:S(2)}, u32[]{:S(2)}) %collective-permute-start.2) | collective-permute-done | bytes 196640 | tf_op jit(solution)/shard_map/while/body/eval_jaxpr/ppermute | solution.py:21
  459.7 7.9 collective-permute-done.2
  471.7 6.6 collective-permute-done.2
  491.1 5.2 fusion.40
  508.9 4.5 fusion.99
  515.8 4.1 fusion.292
  549.3 3.7 fusion.22
  568.5 32.4 %all-reduce.57.cloned.1.call-done = (bf16[256,256]{1,0:T(8,128)(2,1)}, bf16[256,1536]{1,0:T(8,128)(2,1)}) async-done(((bf16[256,256]{1,0:T(8,128)(2,1)}, bf16[256,1536]{1,0:T(8,128)(2,1)}), (bf16[256,256]{1,0:T(8,128)(2,1)}, bf16[256,1536]{1,0:T(8,128)(2,1)})) %all-reduce.57.cloned.1.call-update) | async-done | bytes 917520 | tf_op jit(solution)/shard_map/psum | solution.py:318
  607.9 6.2 psum.231
  614.8 4.0 fusion.124
  627.9 30.1 %while.37 = (s32[]{:T(128)}, f32[1,12,64,128]{3,2,1,0:T(8,128)S(1)}, f32[1,12]{1,0:T(1,128)S(1)}, f32[1,12,64,128]{3,2,1,0:T(8,128)S(1)}, s32[]{:T(128)}, /*index=5*/s32[]{:T(128)}) while((s32[]{:T(128)}, f32[1,12,64,128]{3,2,1,0:T(8,128)S(1)}, f32[1,12]{1,0:T(1,128)S(1)}, f32[1,12,64,128]{3,2,1,0:T(8,128)S(1)}, s32[]{:T(128)}, ...), condition=%wide.region_42.44_spmd.clone, body=%wide.region_41.43_spmd.clone.sunk | while | flops 491523 | bytes 2359463 | solution.py:145
  630.0 7.6 collective-permute-done.3
  640.7 6.7 collective-permute-done.3
  650.5 6.6 collective-permute-done.3
  662.2 5.1 fusion.42
  677.1 4.5 fusion.101
  683.9 4.0 fusion.291
  703.7 3.9 fusion.32
  725.9 28.4 %all-reduce.55.cloned.1.call-done = (bf16[256,256]{1,0:T(8,128)(2,1)}, bf16[256,1536]{1,0:T(8,128)(2,1)}) async-done(((bf16[256,256]{1,0:T(8,128)(2,1)}, bf16[256,1536]{1,0:T(8,128)(2,1)}), (bf16[256,256]{1,0:T(8,128)(2,1)}, bf16[256,1536]{1,0:T(8,128)(2,1)})) %all-reduce.55.cloned.1.call-update) | async-done | bytes 917520 | tf_op jit(solution)/shard_map/psum | solution.py:318
  761.8 3.7 convolution_convert_fusion.1
  780.0 40.5 %reduce-scatter.33.cloned.1.call-done = bf16[192,12]{1,0:T(8,128)(2,1)} async-done(((bf16[1536,12]{1,0:T(8,128)(2,1)}), bf16[192,12]{1,0:T(8,128)(2,1)}) %reduce-scatter.33.cloned.1.call-update) | async-done | bytes 4624
  821.5 5.7 all-reduce.43
  827.8 57.9 %reduce-scatter.31.cloned.1.call-done = bf16[192,12]{1,0:T(8,128)(2,1)} async-done(((bf16[1536,12]{1,0:T(8,128)(2,1)}), bf16[192,12]{1,0:T(8,128)(2,1)}) %reduce-scatter.31.cloned.1.call-update) | async-done | bytes 4624
  887.2 42.6 %all-reduce.53.cloned.1.call-done = f32[1,256,1536]{2,1,0:T(8,128)} async-done(((f32[1,256,1536]{2,1,0:T(8,128)}), f32[1,256,1536]{2,1,0:T(8,128)}) %all-reduce.53.cloned.1.call-update) | async-done | bytes 1572880 | tf_op jit(solution)/shard_map/psum | solution.py:222
  934.4 38.4 %all-reduce.42 = (f32[1,1536]{1,0:T(1,128)S(1)}, f32[1,1536]{1,0:T(1,128)S(1)}, f32[1,4,768]{2,1,0:T(4,128)S(1)}, f32[1,4,768]{2,1,0:T(4,128)S(1)}, f32[1,768]{1...) all-reduce(f32[1,1536]{1,0:T(1,128)S(1)} %stack.152, ...), channel_id=1, replica_groups=mesh['dp'=2,'ctx'=4,'tp'=4] {'dp','ctx'}, use_global_device_ids=true, to_apply=%region_63.65 | all-reduce | flops 14920 | bytes 119360 | tf_op jit(solution)/shard_map/psum | solution.py:363
  980.9 16.3 %reduce-scatter.25.cloned.1.call-done = bf16[192,256]{1,0:T(8,128)(2,1)} async-done(((bf16[1536,256]{1,0:T(8,128)(2,1)}), bf16[192,256]{1,0:T(8,128)(2,1)}) %reduce-scatter.25.cloned.1.call-update) | async-done | bytes 98320 | tf_op jit(solution)/shard_map/reduce_scatter | solution.py:347
  997.2 66.1 %reduce-scatter.23.cloned.1.call-done = bf16[192,256]{1,0:T(8,128)(2,1)} async-done(((bf16[1536,256]{1,0:T(8,128)(2,1)}), bf16[192,256]{1,0:T(8,128)(2,1)}) %reduce-scatter.23.cloned.1.call-update) | async-done | bytes 98320 | tf_op jit(solution)/shard_map/reduce_scatter | solution.py:347
  1064.9 70.2 %reduce-scatter.29.cloned.1.call-done = bf16[768,192]{0,1:T(8,128)(2,1)} async-done(((bf16[768,1536]{0,1:T(8,128)(2,1)}), bf16[768,192]{0,1:T(8,128)(2,1)}) %reduce-scatter.29.cloned.1.call-update) | async-done | bytes 294928 | tf_op jit(solution)/shard_map/reduce_scatter | solution.py:359
  1135.2 72.2 %reduce-scatter.27.cloned.1.call-done = bf16[768,192]{0,1:T(8,128)(2,1)} async-done(((bf16[768,1536]{0,1:T(8,128)(2,1)}), bf16[768,192]{0,1:T(8,128)(2,1)}) %reduce-scatter.27.cloned.1.call-update) | async-done | bytes 294928 | tf_op jit(solution)/shard_map/reduce_scatter | solution.py:359
  1209.5 70.2 %reduce-scatter.17.cloned.1.call-done = bf16[192,768]{1,0:T(8,128)(2,1)} async-done(((bf16[1536,768]{1,0:T(8,128)(2,1)}), bf16[192,768]{1,0:T(8,128)(2,1)}) %reduce-scatter.17.cloned.1.call-update) | async-done | bytes 294928 | tf_op jit(solution)/shard_map/reduce_scatter | solution.py:335
  1279.7 72.1 %reduce-scatter.15.cloned.1.call-done = bf16[192,768]{1,0:T(8,128)(2,1)} async-done(((bf16[1536,768]{1,0:T(8,128)(2,1)}), bf16[192,768]{1,0:T(8,128)(2,1)}) %reduce-scatter.15.cloned.1.call-update) | async-done | bytes 294928 | tf_op jit(solution)/shard_map/reduce_scatter | solution.py:335
  1354.0 70.1 %reduce-scatter.21.cloned.1.call-done = bf16[192,768]{1,0:T(8,128)(2,1)} async-done(((bf16[1536,768]{1,0:T(8,128)(2,1)}), bf16[192,768]{1,0:T(8,128)(2,1)}) %reduce-scatter.21.cloned.1.call-update) | async-done | bytes 294928 | tf_op jit(solution)/shard_map/reduce_scatter | solution.py:341
  1424.1 72.1 %reduce-scatter.19.cloned.1.call-done = bf16[192,768]{1,0:T(8,128)(2,1)} async-done(((bf16[1536,768]{1,0:T(8,128)(2,1)}), bf16[192,768]{1,0:T(8,128)(2,1)}) %reduce-scatter.19.cloned.1.call-update) | async-done | bytes 294928 | tf_op jit(solution)/shard_map/reduce_scatter | solution.py:341
  (1008 shorter events, 304.3 us)
Async XLA Ops:
  7.2 106.0 %all-gather.17.cloned.1.call-start = ((), (), s32[]{:S(2)}) async-start(), calls=%async_computation.20 | async-start | bytes 2654208 | tf_op jit(solution)/shard_map/all_gather | solution.py:170
  9.3 162.0 %all-gather.19.cloned.1.call-start = ((), (), s32[]{:S(2)}) async-start(), calls=%async_computation.21 | async-start | bytes 2654208 | tf_op jit(solution)/shard_map/all_gather | solution.py:169
  10.2 183.3 %all-gather.21.cloned.1.call-start = ((), (), s32[]{:S(2)}) async-start(), calls=%async_computation.22 | async-start | bytes 2654208 | tf_op jit(solution)/shard_map/all_gather | solution.py:173
  10.4 94.0 %collective-permute-start.5 = (f32[1,3]{1,0:T(1,128)S(1)}, f32[1,3]{1,0:T(1,128)S(1)}, u32[]{:S(2)}, u32[]{:S(2)}) collective-permute-start(f32[1,3]{1,0:T(1,128)S(1)} %slice.555), channel_id=1, source_target_pairs={{0,4},{4,8},{8,12},{1,5},{5,9},{9,13},{2,6},{6,10},{10,14},{3,7},{... | collective-permute-start | bytes 44 | tf_op jit(solution)/shard_map/ppermute | solution.py:21
  15.4 97.9 %copy-start.192 = (f32[1536]{0:T(1024)}, f32[1536]{0:T(1024)S(1)}, u32[]{:S(2)}) copy-start(f32[1536]{0:T(1024)S(1)} %get-tuple-element.923) | copy-start | bytes 18436
  15.4 258.8 %copy-start.105 = (f32[1536]{0:T(1024)}, f32[1536]{0:T(1024)S(1)}, u32[]{:S(2)}) copy-start(f32[1536]{0:T(1024)S(1)} %get-tuple-element.922) | copy-start | bytes 18436
  16.3 97.0 %copy-start.268 = (f32[256]{0:T(256)}, f32[256]{0:T(256)S(1)}, u32[]{:S(2)}) copy-start(f32[256]{0:T(256)S(1)} %get-tuple-element.1084) | copy-start | bytes 3076
  55.6 55.4 %copy-start.33 = (f32[256,256]{1,0:T(8,128)}, f32[256,256]{1,0:T(8,128)S(1)}, u32[]{:S(2)}) copy-start(f32[256,256]{1,0:T(8,128)S(1)} %fusion.131) | copy-start | bytes 786436
  55.6 55.4 %collective-permute-start.6 = (f32[1,3,256]{2,1,0:T(4,128)S(1)}, f32[1,3,256]{2,1,0:T(4,128)S(1)}, u32[]{:S(2)}, u32[]{:S(2)}) collective-permute-start(f32[1,3,256]{2,1,0:T(4,128)S(1)} %slice.562), channel_id=1, source_target_pairs={{0,4},{4,8},{8,12},{1,5},{5,9},{9,13},{2,6},{6,10},{10,14},{3,7},{... | collective-permute-start | bytes 9224 | tf_op jit(solution)/shard_map/ppermute | solution.py:21
  57.9 214.0 %all-reduce.51.cloned.1.call-start = ((), (), s32[]{:S(2)}) async-start(), calls=%async_computation.10 | async-start | bytes 3145728 | tf_op jit(solution)/shard_map/psum | solution.py:222
  103.8 89.7 %copy-start.139 = (f32[768]{0:T(1024)}, f32[768]{0:T(1024)S(1)}, u32[]{:S(2)}) copy-start(f32[768]{0:T(1024)S(1)} %get-tuple-element.925) | copy-start | bytes 9220
  112.0 53.3 %copy-start.49 = (bf16[1,256,256]{2,1,0:T(8,128)(2,1)}, bf16[1,256,256]{2,1,0:T(8,128)(2,1)S(1)}, u32[]{:S(2)}) copy-start(bf16[1,256,256]{2,1,0:T(8,128)(2,1)S(1)} %get-tuple-element.1016) | copy-start | bytes 393220
  115.8 2.9 collective-permute-start.4
  117.3 48.4 %copy-start.104 = (f32[256,256]{1,0:T(8,128)}, f32[256,256]{1,0:T(8,128)S(1)}, u32[]{:S(2)}) copy-start(f32[256,256]{1,0:T(8,128)S(1)} %fusion.190) | copy-start | bytes 786436
  124.1 13.5 collective-permute-start
  137.7 15.3 %collective-permute-start = (f32[1,12,64,128]{3,2,1,0:T(8,128)S(1)}, f32[1,12,64,128]{3,2,1,0:T(8,128)S(1)}, u32[]{:S(2)}, u32[]{:S(2)}) collective-permute-start(f32[1,12,64,128]{3,2,1,0:T(8,128)S(1)} %multiply_add_fusion.4), channel_id=1, source_target_pairs={{0,4},{4,8},{8,12},{1,5},{5,9},{9,13},{2,6},{6,10},{10,14},{3,7},{... | collective-permute-start | bytes 1179656 | tf_op jit(solution)/shard_map/while/body/eval_jaxpr/ppermute | solution.py:21
  153.1 12.2 collective-permute-start
  197.3 97.8 %all-gather.23.cloned.1.call-start = ((), (), s32[]{:S(2)}) async-start(), calls=%async_computation.23 | async-start | bytes 2654208 | tf_op jit(solution)/shard_map/all_gather | solution.py:170
  197.9 203.2 %all-gather.25.cloned.1.call-start = ((), (), s32[]{:S(2)}) async-start(), calls=%async_computation.24 | async-start | bytes 2654208 | tf_op jit(solution)/shard_map/all_gather | solution.py:169
  198.4 214.5 %all-gather.27.cloned.1.call-start = ((), (), s32[]{:S(2)}) async-start(), calls=%async_computation.25 | async-start | bytes 2654208 | tf_op jit(solution)/shard_map/all_gather | solution.py:173
  199.2 401.7 %all-reduce.57.cloned.1.call-start = ((), (), s32[]{:S(2)}) async-start(), calls=%async_computation.29 | async-start | bytes 1835008 | tf_op jit(solution)/shard_map/psum | solution.py:318
  274.8 221.5 %copy-start.82 = (f32[1,256,12]{1,2,0:T(8,128)}, f32[1,256,12]{1,2,0:T(8,128)S(1)}, u32[]{:S(2)}) copy-start(f32[1,256,12]{1,2,0:T(8,128)S(1)} %fusion.108) | copy-start | bytes 36868
  298.5 22.5 %collective-permute-start.7 = (f32[1,3,768]{2,1,0:T(4,128)S(1)}, f32[1,3,768]{2,1,0:T(4,128)S(1)}, u32[]{:S(2)}, u32[]{:S(2)}) collective-permute-start(f32[1,3,768]{2,1,0:T(4,128)S(1)} %slice.571), channel_id=1, source_target_pairs={{0,4},{4,8},{8,12},{1,5},{5,9},{9,13},{2,6},{6,10},{10,14},{3,7},{... | collective-permute-start | bytes 27656 | tf_op jit(solution)/shard_map/ppermute | solution.py:21
  302.3 15.5 %collective-permute-start.8 = (f32[1,3,256]{2,1,0:T(4,128)S(1)}, f32[1,3,256]{2,1,0:T(4,128)S(1)}, u32[]{:S(2)}, u32[]{:S(2)}) collective-permute-start(f32[1,3,256]{2,1,0:T(4,128)S(1)} %slice.576), channel_id=1, source_target_pairs={{0,4},{4,8},{8,12},{1,5},{5,9},{9,13},{2,6},{6,10},{10,14},{3,7},{... | collective-permute-start | bytes 9224 | tf_op jit(solution)/shard_map/ppermute | solution.py:21
  334.7 17.0 %collective-permute-start.1 = (f32[1,12,64,128]{3,2,1,0:T(8,128)}, f32[1,12,64,128]{3,2,1,0:T(8,128)S(1)}, u32[]{:S(2)}, u32[]{:S(2)}) collective-permute-start(f32[1,12,64,128]{3,2,1,0:T(8,128)} %multiply_add_fusion.5), channel_id=1, source_target_pairs={{0,4},{4,8},{8,12},{1,5},{5,9},{9,13},{2,6},{6,10},{10,14},{3,7},{... | collective-permute-start | bytes 1179656 | tf_op jit(solution)/shard_map/while/body/eval_jaxpr/ppermute | solution.py:21
  353.6 17.1 %collective-permute-start.1 = (f32[1,12,64,128]{3,2,1,0:T(8,128)}, f32[1,12,64,128]{3,2,1,0:T(8,128)S(1)}, u32[]{:S(2)}, u32[]{:S(2)}) collective-permute-start(f32[1,12,64,128]{3,2,1,0:T(8,128)} %multiply_add_fusion.5), channel_id=1, source_target_pairs={{0,4},{4,8},{8,12},{1,5},{5,9},{9,13},{2,6},{6,10},{10,14},{3,7},{... | collective-permute-start | bytes 1179656 | tf_op jit(solution)/shard_map/while/body/eval_jaxpr/ppermute | solution.py:21
  372.6 20.4 %collective-permute-start.1 = (f32[1,12,64,128]{3,2,1,0:T(8,128)}, f32[1,12,64,128]{3,2,1,0:T(8,128)S(1)}, u32[]{:S(2)}, u32[]{:S(2)}) collective-permute-start(f32[1,12,64,128]{3,2,1,0:T(8,128)} %multiply_add_fusion.5), channel_id=1, source_target_pairs={{0,4},{4,8},{8,12},{1,5},{5,9},{9,13},{2,6},{6,10},{10,14},{3,7},{... | collective-permute-start | bytes 1179656 | tf_op jit(solution)/shard_map/while/body/eval_jaxpr/ppermute | solution.py:21
  437.1 18.6 %collective-permute-start.2 = (bf16[1,12,64,128]{3,2,1,0:T(8,128)(2,1)}, bf16[1,12,64,128]{3,2,1,0:T(8,128)(2,1)}, u32[]{:S(2)}, u32[]{:S(2)}) collective-permute-start(bf16[1,12,64,128]{3,2,1,0:T(8,128)(2,1)} %fusion.359), channel_id=1, source_target_pairs={{4,0},{8,4},{12,8},{5,1},{9,5},{13,9},{6,2},{10,6},{14,10},{7,3},{... | collective-permute-start | bytes 589832 | tf_op jit(solution)/shard_map/while/body/eval_jaxpr/ppermute | solution.py:21
  458.5 9.2 collective-permute-start.2
  470.4 7.9 collective-permute-start.2
  544.1 11.1 collective-permute-start.9
  546.2 7.6 collective-permute-start.10
  561.7 192.6 %all-reduce.55.cloned.1.call-start = ((), (), s32[]{:S(2)}) async-start(), calls=%async_computation.28 | async-start | bytes 1835008 | tf_op jit(solution)/shard_map/psum | solution.py:318
  628.7 8.9 collective-permute-start.3
  639.4 8.0 collective-permute-start.3
  649.2 7.9 collective-permute-start.3
  699.5 10.9 collective-permute-start.11
  701.6 7.4 collective-permute-start.12
  715.9 104.6 %reduce-scatter.33.cloned.1.call-start = ((), (), s32[]{:S(2)}) async-start(), calls=%async_computation.27 | async-start | bytes 442368
  717.3 168.3 %reduce-scatter.31.cloned.1.call-start = ((), (), s32[]{:S(2)}) async-start(), calls=%async_computation.26 | async-start | bytes 442368
  719.9 210.0 %all-reduce.53.cloned.1.call-start = ((), (), s32[]{:S(2)}) async-start(), calls=%async_computation.11 | async-start | bytes 3145728 | tf_op jit(solution)/shard_map/psum | solution.py:222
  723.7 273.5 %reduce-scatter.25.cloned.1.call-start = ((), (), s32[]{:S(2)}) async-start(), calls=%async_computation.17 | async-start | bytes 884736 | tf_op jit(solution)/shard_map/reduce_scatter | solution.py:347
  725.9 337.3 %reduce-scatter.23.cloned.1.call-start = ((), (), s32[]{:S(2)}) async-start(), calls=%async_computation.16 | async-start | bytes 884736 | tf_op jit(solution)/shard_map/reduce_scatter | solution.py:347
  756.9 378.2 %reduce-scatter.29.cloned.1.call-start = ((), (), s32[]{:S(2)}) async-start(), calls=%async_computation.19 | async-start | bytes 2654208 | tf_op jit(solution)/shard_map/reduce_scatter | solution.py:359
  760.7 446.7 %reduce-scatter.27.cloned.1.call-start = ((), (), s32[]{:S(2)}) async-start(), calls=%async_computation.18 | async-start | bytes 2654208 | tf_op jit(solution)/shard_map/reduce_scatter | solution.py:359
  765.5 514.2 %reduce-scatter.17.cloned.1.call-start = ((), (), s32[]{:S(2)}) async-start(), calls=%async_computation.13 | async-start | bytes 2654208 | tf_op jit(solution)/shard_map/reduce_scatter | solution.py:335
  768.7 583.1 %reduce-scatter.15.cloned.1.call-start = ((), (), s32[]{:S(2)}) async-start(), calls=%async_computation.12 | async-start | bytes 2654208 | tf_op jit(solution)/shard_map/reduce_scatter | solution.py:335
  772.4 651.7 %reduce-scatter.21.cloned.1.call-start = ((), (), s32[]{:S(2)}) async-start(), calls=%async_computation.15 | async-start | bytes 2654208 | tf_op jit(solution)/shard_map/reduce_scatter | solution.py:341
  775.7 720.6 %reduce-scatter.19.cloned.1.call-start = ((), (), s32[]{:S(2)}) async-start(), calls=%async_computation.14 | async-start | bytes 2654208 | tf_op jit(solution)/shard_map/reduce_scatter | solution.py:341
  779.1 48.2 %copy-start.262 = (bf16[768]{0:T(1024)(128)(2,1)S(1)}, bf16[768]{0:T(1024)(128)(2,1)}, u32[]{:S(2)}) copy-start(bf16[768]{0:T(1024)(128)(2,1)} %get-tuple-element.875) | copy-start | bytes 4612
  779.1 48.2 %copy-start.261 = (bf16[768]{0:T(1024)(128)(2,1)S(1)}, bf16[768]{0:T(1024)(128)(2,1)}, u32[]{:S(2)}) copy-start(bf16[768]{0:T(1024)(128)(2,1)} %get-tuple-element.878) | copy-start | bytes 4612
  779.1 48.2 %copy-start.260 = (bf16[768]{0:T(1024)(128)(2,1)S(1)}, bf16[768]{0:T(1024)(128)(2,1)}, u32[]{:S(2)}) copy-start(bf16[768]{0:T(1024)(128)(2,1)} %get-tuple-element.877) | copy-start | bytes 4612
  779.1 48.2 %copy-start.259 = (bf16[768]{0:T(1024)(128)(2,1)S(1)}, bf16[768]{0:T(1024)(128)(2,1)}, u32[]{:S(2)}) copy-start(bf16[768]{0:T(1024)(128)(2,1)} %get-tuple-element.876) | copy-start | bytes 4612
  779.1 48.2 %copy-start.258 = (bf16[768]{0:T(1024)(128)(2,1)S(1)}, bf16[768]{0:T(1024)(128)(2,1)}, u32[]{:S(2)}) copy-start(bf16[768]{0:T(1024)(128)(2,1)} %get-tuple-element.874) | copy-start | bytes 4612
  779.1 48.3 %copy-start.217 = (f32[768]{0:T(1024)S(1)}, f32[768]{0:T(1024)}, u32[]{:S(2)}) copy-start(f32[768]{0:T(1024)} %get-tuple-element.986) | copy-start | bytes 9220
  779.2 48.3 %copy-start.219 = (f32[768]{0:T(1024)S(1)}, f32[768]{0:T(1024)}, u32[]{:S(2)}) copy-start(f32[768]{0:T(1024)} %get-tuple-element.870) | copy-start | bytes 9220
  779.2 48.3 %copy-start.196 = (f32[1536]{0:T(1024)S(1)}, f32[1536]{0:T(1024)}, u32[]{:S(2)}) copy-start(f32[1536]{0:T(1024)} %get-tuple-element.860) | copy-start | bytes 18436
  779.2 48.5 %copy-start.236 = (f32[2,12]{1,0:T(2,128)S(1)}, f32[2,12]{1,0:T(2,128)}, u32[]{:S(2)}) copy-start(f32[2,12]{1,0:T(2,128)} %param.46) | copy-start | bytes 292
  779.2 48.5 %copy-start.283 = (f32[12]{0:T(128)S(1)}, f32[12]{0:T(128)}, u32[]{:S(2)}) copy-start(f32[12]{0:T(128)} %get-tuple-element.911) | copy-start | bytes 148
  779.2 48.5 %copy-start.284 = (f32[12]{0:T(128)S(1)}, f32[12]{0:T(128)}, u32[]{:S(2)}) copy-start(f32[12]{0:T(128)} %get-tuple-element.912) | copy-start | bytes 148
  779.2 48.5 %copy-start.285 = (f32[12]{0:T(128)S(1)}, f32[12]{0:T(128)}, u32[]{:S(2)}) copy-start(f32[12]{0:T(128)} %get-tuple-element.913) | copy-start | bytes 148
  779.2 48.5 %copy-start.287 = (f32[12]{0:T(128)S(1)}, f32[12]{0:T(128)}, u32[]{:S(2)}) copy-start(f32[12]{0:T(128)} %get-tuple-element.908) | copy-start | bytes 148
  779.2 48.5 %copy-start.288 = (f32[12]{0:T(128)S(1)}, f32[12]{0:T(128)}, u32[]{:S(2)}) copy-start(f32[12]{0:T(128)} %get-tuple-element.909) | copy-start | bytes 148
  779.2 48.5 %copy-start.289 = (f32[12]{0:T(128)S(1)}, f32[12]{0:T(128)}, u32[]{:S(2)}) copy-start(f32[12]{0:T(128)} %get-tuple-element.910) | copy-start | bytes 148
  (288 other events, 2077.9 us)
Sparse Core Ops, SparseCore 0:
  10.7 68.5 all-gather.16
  81.4 52.4 all-gather.18
  136.6 56.9 all-gather.20
  197.4 41.3 all-reduce.50
  240.8 54.2 all-gather.22
  297.1 53.9 all-gather.24
  353.1 53.7 all-gather.26
  561.8 39.0 all-reduce.56
  716.1 38.2 all-reduce.54
  758.0 62.4 reduce-scatter.32
  824.3 61.2 reduce-scatter.30
  887.9 41.9 all-reduce.52
  933.7 63.3 reduce-scatter.24
  1000.9 62.2 reduce-scatter.22
  1066.6 68.5 reduce-scatter.28
  1138.5 68.8 reduce-scatter.26
  1210.7 68.9 reduce-scatter.16
  1283.0 68.7 reduce-scatter.14
  1355.3 68.7 reduce-scatter.20
  1427.4 68.7 reduce-scatter.18
where the time goes:
time: 1520 us; the launch traced here: 1510 us
  waiting for transfers between devices  866 us (57%)
  blocking collectives  217 us (14%)
  matrix products  125 us (8%)
  other arithmetic  120 us (8%)
  local copies, waits for them, and re-layouts  103 us (7%)
  starting transfers between devices  55.9 us (4%)
  between operations  20 us (1%)
    reduce_scatter x2, waiting for transfers between devices, layer_backward(): lax.psum_scatter(grad_out_proj.astype(jnp.bfloat16), ('dp', 'ctx'), scatt...  142 us
    reduce_scatter x2, waiting for transfers between devices, layer_backward(): lax.psum_scatter(dot_left(normed, grad_gate_low).astype(jnp.bfloat16), ('...  142 us
    reduce_scatter x2, waiting for transfers between devices, layer_backward(): lax.psum_scatter(dot_left(normed, grad_value_low).astype(jnp.bfloat16), (...  142 us
    ppermute x21, waiting for transfers between devices, from_behind(): return lax.ppermute(block, axis, route)  122 us
    unnamed x22, waiting for transfers between devices  100 us
    reduce_scatter x2, waiting for transfers between devices, layer_backward(): lax.psum_scatter(dot_left(normed, grad_bc_low).astype(jnp.bfloat16), ('dp...  82.3 us
    all_gather x2, blocking collectives, layer_forward(): lax.all_gather(bc_proj, ('dp', 'ctx'), axis=0, tiled=True)  76.4 us
    all_gather x2, blocking collectives, layer_forward(): lax.all_gather(step_proj, ('dp', 'ctx'), axis=0, tiled=True)  70.7 us
  transfers between devices with their start and end apart: 41, of which 28 were waited for; matrix products, arithmetic and copies ran while one was open for 11% of the time, Pallas kernels for 0%

commit v1 on v0

--- a/solution.py
+++ b/solution.py
@@ -3,6 +3,8 @@
 import jax
 import jax.numpy as jnp
 from jax import lax
+from jax.experimental import pallas as pl
+from jax.experimental.pallas import tpu as pltpu
 from jax.sharding import PartitionSpec as P
 
 HEADDIM = 64
@@ -453,6 +455,1522 @@
     )
 
 
+MESH = pl.DeviceIdType.MESH
+PACK = 640
+
+
+def params_of(collective_id):
+    return pltpu.CompilerParams(
+        collective_id=collective_id, has_side_effects=True, vmem_limit_bytes=60 << 20
+    )
+
+
+VMEM_SPEC = pl.BlockSpec(memory_space=pltpu.VMEM)
+
+
+def greet(peers):
+    barrier = pltpu.get_barrier_semaphore()
+    for peer in peers:
+        pl.semaphore_signal(barrier, inc=1, device_id=peer, device_id_type=MESH)
+    pl.semaphore_wait(barrier, len(peers))
+
+
+def remote(source, target, send_sem, recv_sem, peer):
+    return pltpu.make_async_remote_copy(
+        src_ref=source,
+        dst_ref=target,
+        send_sem=send_sem,
+        recv_sem=recv_sem,
+        device_id=peer,
+        device_id_type=MESH,
+    )
+
+
+def other_core(t):
+    return t + 1 - 2 * lax.rem(t, 2)
+
+
+def other_chip(t):
+    return lax.rem(t + 2, 4)
+
+
+def gather_body(count, depth, pieces, fulls, send_sem, recv_sem):
+    z = lax.axis_index("ctx")
+    t = lax.axis_index("tp")
+    core, chip = {"tp": other_core(t)}, {"tp": other_chip(t)}
+    started = []
+
+    def send(a, source, slot, kind, peer):
+        copy = remote(source, fulls[a].at[slot], send_sem.at[a, kind], recv_sem.at[a, slot], peer)
+        copy.start()
+        started.append(copy)
+
+    def arrived(a, slot):
+        remote(
+            fulls[a].at[slot], fulls[a].at[slot], send_sem.at[a, 0], recv_sem.at[a, slot], core
+        ).wait_recv()
+
+    mine = z * 4 + t
+    for a in range(count):
+        for hop in range(1, depth):
+            send(a, pieces[a], mine, hop, {"ctx": lax.rem(z + hop, depth)})
+        send(a, pieces[a], mine, depth, chip)
+        send(a, pieces[a], mine, depth + 1, core)
+        fulls[a][mine] = pieces[a][...]
+    kind = depth + 2
+    for hop in range(1, depth):
+        slot = lax.rem(z + hop, depth) * 4 + t
+        for a in range(count):
+            arrived(a, slot)
+            send(a, fulls[a].at[slot], slot, kind, chip)
+            send(a, fulls[a].at[slot], slot, kind + 1, core)
+        kind += 2
+    for hop in range(depth):
+        slot = lax.rem(z + hop, depth) * 4 + other_chip(t)
+        for a in range(count):
+            arrived(a, slot)
+            send(a, fulls[a].at[slot], slot, kind, core)
+        kind += 1
+    for hop in range(depth):
+        for row in (other_core(t), other_chip(other_core(t))):
+            for a in range(count):
+                arrived(a, lax.rem(z + hop, depth) * 4 + row)
+    for copy in started:
+        copy.wait_send()
+
+
+def gather_peers(depth):
+    z = lax.axis_index("ctx")
+    t = lax.axis_index("tp")
+    return [{"ctx": lax.rem(z + hop, depth)} for hop in range(1, depth)] + [
+        {"tp": other_chip(t)},
+        {"tp": other_core(t)},
+    ]
+
+
+def gather_kernel(count, depth, *refs):
+    greet(gather_peers(depth))
+    gather_body(count, depth, refs[:count], refs[count : 2 * count], *refs[2 * count :])
+
+
+def gather_pieces(pieces, depth, collective_id):
+    count = len(pieces)
+    slots = depth * 4
+    return pl.pallas_call(
+        partial(gather_kernel, count, depth),
+        out_shape=[jax.ShapeDtypeStruct((slots,) + p.shape, p.dtype) for p in pieces],
+        in_specs=[VMEM_SPEC] * count,
+        out_specs=[VMEM_SPEC] * count,
+        scratch_shapes=[
+            pltpu.SemaphoreType.DMA((count, 4 * depth)),
+            pltpu.SemaphoreType.DMA((count, slots)),
+        ],
+        compiler_params=params_of(collective_id),
+        name="gather_pieces",
+    )(*pieces)
+
+
+def reduce_body(count, depth, parts, outs, bufs, send_sem, recv_sem):
+    z = lax.axis_index("ctx")
+    t = lax.axis_index("tp")
+    core, chip = {"tp": other_core(t)}, {"tp": other_chip(t)}
+    started = []
+    hops = list(range(1, depth)) + [0]
+
+    def send(a, source, target, kind, peer):
+        copy = remote(source, target, send_sem.at[a, kind], recv_sem.at[a, kind], peer)
+        copy.start()
+        started.append(copy)
+
+    def arrived(a, ref, kind):
+        remote(ref, ref, send_sem.at[a, kind], recv_sem.at[a, kind], core).wait_recv()
+
+    for place, hop in enumerate(hops):
+        far = lax.rem(z + hop, depth)
+        for which, row in enumerate((other_chip(other_core(t)), other_core(t))):
+            kind = place * 2 + which
+            for a in range(count):
+                send(a, parts[a].at[far * 4 + row], bufs[a].at[kind], kind, core)
+    for place, hop in enumerate(hops):
+        far = lax.rem(z + hop, depth)
+        kind = place * 2
+        for a in range(count):
+            buf = bufs[a]
+            arrived(a, buf.at[kind], kind)
+            total = parts[a][far * 4 + other_chip(t)].astype(jnp.float32) + buf[kind].astype(
+                jnp.float32
+            )
+            buf[kind] = total.astype(buf.dtype)
+            send(a, buf.at[kind], buf.at[2 * depth + place], 2 * depth + place, chip)
+    for place, hop in enumerate(hops):
+        far = lax.rem(z + hop, depth)
+        kind = place * 2 + 1
+        for a in range(count):
+            buf = bufs[a]
+            arrived(a, buf.at[kind], kind)
+            arrived(a, buf.at[2 * depth + place], 2 * depth + place)
+            total = (
+                parts[a][far * 4 + t].astype(jnp.float32)
+                + buf[kind].astype(jnp.float32)
+                + buf[2 * depth + place].astype(jnp.float32)
+            )
+            if hop:
+                buf[kind] = total.astype(buf.dtype)
+                target = 3 * depth + (depth - hop)
+                copy = remote(
+                    buf.at[kind],
+                    buf.at[target],
+                    send_sem.at[a, 3 * depth + hop],
+                    recv_sem.at[a, target],
+                    {"ctx": far},
+                )
+                copy.start()
+                started.append(copy)
+            else:
+                outs[a][...] = total
+    for hop in range(1, depth):
+        for a in range(count):
+            buf = bufs[a]
+            target = 3 * depth + hop
+            arrived(a, buf.at[target], target)
+            outs[a][...] += buf[target].astype(jnp.float32)
+    for copy in started:
+        copy.wait_send()
+
+
+def reduce_kernel(count, depth, *refs):
+    greet(gather_peers(depth))
+    reduce_body(
+        count,
+        depth,
+        refs[:count],
+        refs[count : 2 * count],
+        refs[2 * count : 3 * count],
+        *refs[3 * count :],
+    )
+
+
+def reduce_pieces(parts, depth, collective_id):
+    count = len(parts)
+    return pl.pallas_call(
+        partial(reduce_kernel, count, depth),
+        out_shape=[jax.ShapeDtypeStruct(p.shape[1:], jnp.float32) for p in parts],
+        in_specs=[VMEM_SPEC] * count,
+        out_specs=[VMEM_SPEC] * count,
+        scratch_shapes=[pltpu.VMEM((4 * depth,) + p.shape[1:], p.dtype) for p in parts]
+        + [
+            pltpu.SemaphoreType.DMA((count, 4 * depth)),
+            pltpu.SemaphoreType.DMA((count, 4 * depth)),
+        ],
+        compiler_params=params_of(collective_id),
+        name="reduce_pieces",
+    )(*parts)
+
+
+def scatter_kernel(depth, grads_ref, shared_ref, out_ref, shared_out, x_buf, x_shared, send_sem, recv_sem):
+    x = lax.axis_index("dp")
+    z = lax.axis_index("ctx")
+    far_x = {"dp": 1 - x}
+    greet([{"ctx": lax.rem(z + hop, depth)} for hop in range(1, depth)] + [far_x])
+    started = []
+
+    def send(source, target, kind, recv, peer):
+        copy = remote(source, target, send_sem.at[kind], recv_sem.at[recv], peer)
+        copy.start()
+        started.append(copy)
+
+    def arrived(ref, recv):
+        remote(ref, ref, send_sem.at[recv], recv_sem.at[recv], far_x).wait_recv()
+
+    hops = list(range(1, depth)) + [0]
+    for place, hop in enumerate(hops):
+        far = lax.rem(z + hop, depth)
+        send(grads_ref.at[(1 - x) * depth + far], x_buf.at[place], place, place, far_x)
+    send(shared_ref.at[1 - x], x_shared, depth, depth, far_x)
+    for place, hop in enumerate(hops):
+        far = lax.rem(z + hop, depth)
+        arrived(x_buf.at[place], place)
+        total = grads_ref[x * depth + far].astype(jnp.float32) + x_buf[place].astype(jnp.float32)
+        if hop:
+            x_buf[place] = total.astype(x_buf.dtype)
+            copy = remote(
+                x_buf.at[place],
+                out_ref.at[z],
+                send_sem.at[depth + hop],
+                recv_sem.at[depth + depth - hop],
+                {"ctx": far},
+            )
+            copy.start()
+            started.append(copy)
+        else:
+            out_ref[z] = total.astype(out_ref.dtype)
+    arrived(x_shared, depth)
+    shared_out[...] = shared_ref[x].astype(jnp.float32) + x_shared[...].astype(jnp.float32)
+    for hop in range(1, depth):
+        arrived(out_ref.at[lax.rem(z + hop, depth)], depth + hop)
+    for copy in started:
+        copy.wait_send()
+
+
+def scatter_grads(grads, shared, depth, collective_id):
+    return pl.pallas_call(
+        partial(scatter_kernel, depth),
+        out_shape=[
+            jax.ShapeDtypeStruct((depth,) + grads.shape[1:], grads.dtype),
+            jax.ShapeDtypeStruct(shared.shape[1:], jnp.float32),
+        ],
+        in_specs=[VMEM_SPEC] * 2,
+        out_specs=[VMEM_SPEC] * 2,
+        scratch_shapes=[
+            pltpu.VMEM((depth,) + grads.shape[1:], grads.dtype),
+            pltpu.VMEM(shared.shape[1:], shared.dtype),
+            pltpu.SemaphoreType.DMA((2 * depth,)),
+            pltpu.SemaphoreType.DMA((2 * depth,)),
+        ],
+        compiler_params=params_of(collective_id),
+        name="scatter_grads",
+    )(grads, shared)
+
+
+def mxu(left, right, left_dim, right_dim, precision=None):
+    return lax.dot_general(
+        left,
+        right,
+        (((left_dim,), (right_dim,)), ((), ())),
+        preferred_element_type=jnp.float32,
+        precision=precision,
+    )
+
+
+def iota(shape, axis):
+    return lax.broadcasted_iota(jnp.int32, shape, axis)
+
+
+def ones_where(condition, kind):
+    return jnp.where(condition, 1.0, 0.0).astype(kind)
+
+
+def sigmoid(v):
+    return 1.0 / (1.0 + jnp.exp(-v))
+
+
+exact = lax.Precision.HIGHEST
+LOW = jnp.bfloat16
+OUT_AT, VALUE_AT = 128, 384
+
+
+class BlockTerms:
+    def __init__(self, start, segc_ref, segr_ref, small_ref, value_ref, bc_ref, step_in, width):
+        self.start, self.width = start, width
+        self.segc_ref, self.small_ref = segc_ref, small_ref
+        rows = pl.ds(8 + start, BLOCK)
+        seg = segc_ref[rows, :]
+        row, col = iota((BLOCK, BLOCK), 0), iota((BLOCK, BLOCK), 1)
+        self.row, self.col = row, col
+        same = jnp.logical_and(seg == segr_ref[:, pl.ds(start, BLOCK)], row >= col)
+        self.hidden_pairs = jnp.where(same, 0.0, -1e30)
+        self.value_arg = self.conv(value_ref, 0, 4, width)
+        self.bc_arg = self.conv(bc_ref, 9, 13, bc_ref.shape[1])
+        self.value_sig = sigmoid(self.value_arg)
+        self.bc_sig = sigmoid(self.bc_arg)
+        self.values = (self.value_arg * self.value_sig).astype(LOW)
+        bc_low = (self.bc_arg * self.bc_sig).astype(LOW)
+        half = bc_ref.shape[1] // 2
+        self.b_low, self.c_low = bc_low[:, :half], bc_low[:, half:]
+        self.step = jnp.maximum(step_in, 0.0) + jnp.log1p(jnp.exp(-jnp.abs(step_in)))
+        rates = small_ref[8:9, :width]
+        self.log_decay = mxu(ones_where(row >= col, jnp.float32), self.step * rates, 1, 0, exact)
+        self.log_rows = jnp.transpose(self.log_decay)
+        self.step_rows = jnp.transpose(self.step)
+        self.scores = mxu(self.c_low, self.b_low, 1, 1)
+        seg = seg[:, :width]
+        before = segc_ref[7 + start : 8 + start, :width]
+        last = segc_ref[7 + start + BLOCK : 8 + start + BLOCK, :width]
+        self.reach = jnp.where(seg == before, jnp.exp(self.log_decay), 0.0)
+        self.reach_last = self.reach[BLOCK - 1 : BLOCK, :]
+        self.fade = jnp.where(
+            seg == last, jnp.exp(self.log_decay[BLOCK - 1 : BLOCK, :] - self.log_decay), 0.0
+        )
+        self.faded = self.fade * self.step * self.values.astype(jnp.float32)
+
+    def conv(self, ref, taps_at, bias_at, width):
+        total = self.small_ref[bias_at : bias_at + 1, :width]
+        for distance in range(4):
+            tap = self.small_ref[taps_at + 3 - distance : taps_at + 4 - distance, :width]
+            total = total + tap * self.back(ref, distance, width)
+        return total
+
+    def back(self, ref, distance, width):
+        rows = ref[pl.ds(8 + self.start - distance, BLOCK), :]
+        if not distance:
+            return rows
+        here = self.segc_ref[pl.ds(8 + self.start, BLOCK), :width]
+        there = self.segc_ref[pl.ds(8 + self.start - distance, BLOCK), :width]
+        return jnp.where(here == there, rows, 0.0)
+
+    def ahead(self, ref, distance, width):
+        rows = ref[pl.ds(self.start + distance, BLOCK), :]
+        if not distance:
+            return rows
+        here = self.segc_ref[pl.ds(8 + self.start, BLOCK), :width]
+        there = self.segc_ref[pl.ds(8 + self.start + distance, BLOCK), :width]
+        return jnp.where(here == there, rows, 0.0)
+
+    def decay_pairs(self, head):
+        at = head * HEADDIM
+        return jnp.exp(
+            self.log_decay[:, at : at + 1] - self.log_rows[at : at + 1, :] + self.hidden_pairs
+        )
+
+    def head_lanes(self, head):
+        lanes = iota((BLOCK, self.width), 1)
+        return jnp.logical_and(lanes >= head * HEADDIM, lanes < (head + 1) * HEADDIM)
+
+    def of_head(self, array, head):
+        return array * ones_where(self.head_lanes(head), array.dtype)
+
+
+def lane_shift(width):
+    return ones_where(iota((width, 256), 1) == iota((width, 256), 0) + 64, LOW)
+
+
+def two_parts(array):
+    high = array.astype(LOW)
+    return high, (array - high.astype(jnp.float32)).astype(LOW)
+
+
+def forward_kernel(
+    precise,
+    normed_ref,
+    wall_ref,
+    bcw_ref,
+    small_ref,
+    segr_ref,
+    segc_ref,
+    part_ref,
+    squares_ref,
+    gate_ref,
+    value_ref,
+    bc_ref,
+    step_ref,
+    mixed_ref,
+    state_ref,
+):
+    tokens = normed_ref.shape[0]
+    width = gate_ref.shape[1]
+    heads = width // HEADDIM
+    piece = 0 if precise else part_ref.shape[1]
+    value_ref[0:8, :] = jnp.zeros((8, width), jnp.float32)
+    bc_ref[0:8, :] = jnp.zeros((8, bc_ref.shape[1]), jnp.float32)
+    spread = ones_where(
+        iota((256, width), 0) - width == iota((256, width), 1) // HEADDIM, jnp.float32
+    )
+    shift = lane_shift(width)
+    gains, skip = small_ref[5:6, :width], small_ref[6:7, :width]
+    state = jnp.zeros(state_ref.shape[1:], jnp.float32)
+    for block in range(tokens // BLOCK):
+        start = block * BLOCK
+        rows = pl.ds(start, BLOCK)
+        normed = normed_ref[rows, :]
+        gate_pre = mxu(normed, wall_ref[:, 0:256], 1, 0)[:, :width]
+        both = mxu(normed, wall_ref[:, VALUE_AT : VALUE_AT + 256], 1, 0)
+        value_ref[pl.ds(8 + start, BLOCK), :] = both[:, :width]
+        bc_ref[pl.ds(8 + start, BLOCK), :] = mxu(normed, bcw_ref[...], 1, 0)
+        step_in = mxu(both, spread, 1, 0, exact) + small_ref[7:8, :width]
+        gate_ref[rows, :] = gate_pre
+        step_ref[rows, :] = step_in
+        terms = BlockTerms(start, segc_ref, segr_ref, small_ref, value_ref, bc_ref, step_in, width)
+        mixed = skip * terms.values.astype(jnp.float32)
+        for head in range(heads):
+            at = head * HEADDIM
+            weights = terms.scores * terms.decay_pairs(head) * terms.step_rows[at : at + 1, :]
+            own_values = terms.of_head(terms.values, head)
+            for term in two_parts(weights) if precise else (weights.astype(LOW),):
+                mixed += mxu(term, own_values, 1, 0)
+        state_ref[block] = state
+        if block:
+            for term in two_parts(state) if precise else (state.astype(LOW),):
+                mixed += terms.reach * mxu(terms.c_low, term, 1, 0)
+        state = terms.reach_last * state
+        for term in two_parts(terms.faded) if precise else (terms.faded.astype(LOW),):
+            state += mxu(terms.b_low, term, 0, 0)
+        mixed_ref[rows, :] = mixed
+        gated = mixed * gate_pre * sigmoid(gate_pre)
+        squares = gated * gated
+        if precise:
+            part_ref[rows, :] = gated
+            for at in range(0, BLOCK, 128):
+                row = (start + at) // 128
+                squares_ref[row : row + 1, :] = mxu(
+                    jnp.ones((8, width), jnp.float32), squares[at : at + 128], 1, 1, exact
+                )[0:1]
+            continue
+        for at in range(0, BLOCK, piece):
+            slot = (start + at) // piece
+            squares_ref[slot, :, 0:piece] = mxu(
+                jnp.ones((8, width), jnp.float32), squares[at : at + piece], 1, 1, exact
+            )
+        moved = mxu((gated * gains).astype(LOW), shift, 1, 0).astype(LOW)
+        part = mxu(moved, wall_ref[:, OUT_AT : OUT_AT + 256], 1, 1).astype(LOW)
+        for at in range(0, BLOCK, piece):
+            part_ref[(start + at) // piece] = part[at : at + piece]
+
+
+def local_params():
+    return pltpu.CompilerParams(vmem_limit_bytes=60 << 20)
+
+
+def split_forward(normed, wall, bcw, small, segr, segc, slots, precise):
+    tokens, model_width = normed.shape
+    piece = tokens // slots
+    width = INNER // slots
+    bc_width = bcw.shape[1]
+    f32 = jnp.float32
+    if precise:
+        first = [
+            jax.ShapeDtypeStruct((tokens, width), f32),
+            jax.ShapeDtypeStruct((tokens // 128, 128), f32),
+        ]
+    else:
+        first = [
+            jax.ShapeDtypeStruct((slots, piece, model_width), LOW),
+            jax.ShapeDtypeStruct((slots, 8, 128), f32),
+        ]
+    return pl.pallas_call(
+        partial(forward_kernel, precise),
+        out_shape=first
+        + [
+            jax.ShapeDtypeStruct((tokens, width), f32),
+            jax.ShapeDtypeStruct((tokens + 8, width), f32),
+            jax.ShapeDtypeStruct((tokens + 8, bc_width), f32),
+            jax.ShapeDtypeStruct((tokens, width), f32),
+            jax.ShapeDtypeStruct((tokens, width), f32),
+            jax.ShapeDtypeStruct((tokens // BLOCK, bc_width // 2, width), f32),
+        ],
+        in_specs=[VMEM_SPEC] * 6,
+        out_specs=[VMEM_SPEC] * 8,
+        compiler_params=local_params(),
+        name="forward_block",
+    )(normed, wall, bcw, small, segr, segc)
+
+
+def row_sum(array):
+    return jnp.sum(array, axis=0, keepdims=True)
+
+
+def backward_kernel(
+    grad_ref,
+    scalar_ref,
+    normed_ref,
+    wall_ref,
+    small_ref,
+    segr_ref,
+    segc_ref,
+    gate_ref,
+    value_ref,
+    bc_ref,
+    step_ref,
+    mixed_ref,
+    state_ref,
+    both_ref,
+    grads_ref,
+    sums_ref,
+    pre_ref,
+    scaled_ref,
+    e_ref,
+    e_bc_ref,
+):
+    tokens, model_width = normed_ref.shape
+    width = gate_ref.shape[1]
+    bc_width = bc_ref.shape[1]
+    heads = width // HEADDIM
+    piece = both_ref.shape[1]
+    blocks = tokens // BLOCK
+    f32 = jnp.float32
+    shift = lane_shift(width)
+    gains, skip, rates = (small_ref[at : at + 1, :width] for at in (5, 6, 8))
+    e_ref[tokens:, :] = jnp.zeros((8, width), f32)
+    e_bc_ref[tokens:, :] = jnp.zeros((8, bc_width), f32)
+    pre_ref[...] = jnp.zeros(pre_ref.shape, LOW)
+    eye = ones_where(iota((piece, 128), 0) == iota((piece, 128), 1), f32)
+    same_head = ones_where(
+        iota((width, width), 0) // HEADDIM == iota((width, width), 1) // HEADDIM, f32
+    )
+    tail = ones_where(iota((width, 128), 0) == iota((width, 128), 1) + 128, LOW)
+    pick = ones_where(
+        jnp.logical_and(
+            iota((width, 128), 0) == (iota((width, 128), 1) - 64) * HEADDIM, iota((width, 128), 1) >= 64
+        ),
+        LOW,
+    )
+    grad_state = jnp.zeros(state_ref.shape[1:], f32)
+    sums = {}
+
+    def add(name, term):
+        sums[name] = sums[name] + term if name in sums else term
+
+    for block in reversed(range(blocks)):
+        start = block * BLOCK
+        rows = pl.ds(start, BLOCK)
+        step_in = step_ref[rows, :]
+        terms = BlockTerms(start, segc_ref, segr_ref, small_ref, value_ref, bc_ref, step_in, width)
+        columns = jnp.concatenate(
+            [
+                mxu(eye, scalar_ref[(start + at) // piece], 1, 1, exact)
+                for at in range(0, BLOCK, piece)
+            ],
+            axis=0,
+        )
+        inv, inner = columns[:, 0:1], columns[:, 1:2]
+        grad_low = grad_ref[rows, 0:model_width]
+        grad_scaled = mxu(grad_low, wall_ref[:, OUT_AT : OUT_AT + 256], 1, 0)
+        grad_scaled = pltpu.roll(grad_scaled, 192, 1)[:, :width]
+        gate_pre, mixed = gate_ref[rows, :], mixed_ref[rows, :]
+        sig = sigmoid(gate_pre)
+        act = gate_pre * sig
+        gated = mixed * act
+        normal = gated * inv
+        scaled_ref[rows, :] = mxu((normal * gains).astype(LOW), shift, 1, 0).astype(LOW)
+        add("out_gain", row_sum(grad_scaled * normal))
+        grad_gated = inv * (grad_scaled * gains) - gated * (inv * inv * inner)
+        grad_gate = grad_gated * mixed * sig * (1.0 + gate_pre * (1.0 - sig))
+        pre_ref[rows, 0:width] = grad_gate.astype(LOW)
+        grad_mixed = grad_gated * act
+        grad_mixed_low = grad_mixed.astype(LOW)
+        values = terms.values.astype(f32)
+        add("skip", row_sum(grad_mixed * values))
+        grad_values = skip * grad_mixed
+        direct = jnp.zeros((BLOCK, width), f32)
+        between = jnp.zeros((BLOCK, width), f32)
+        pair_sum = jnp.zeros((BLOCK, BLOCK), f32)
+        from_here = ones_where(terms.col >= terms.row, LOW)
+        for head in range(heads):
+            at = head * HEADDIM
+            decay = terms.decay_pairs(head)
+            step_row = terms.step_rows[at : at + 1, :]
+            grad_head = terms.of_head(grad_mixed_low, head)
+            head_ones = ones_where(terms.head_lanes(head), LOW)
+            products = mxu(grad_head, terms.values, 1, 1)
+            scored = terms.scores * decay
+            grad_values += mxu((scored * step_row).astype(LOW), grad_head, 0, 0)
+            pair_sum += decay * step_row * products
+            unstepped = scored * products
+            direct += mxu(unstepped.astype(LOW), head_ones, 0, 0)
+            later = mxu(from_here, (unstepped * step_row).astype(LOW), 1, 0)
+            later = jnp.where(terms.col < terms.row, later, 0.0)
+            between += mxu(later.astype(LOW), head_ones, 1, 0)
+        pair_low = pair_sum.astype(LOW)
+        grad_b = mxu(pair_low, terms.c_low, 0, 0)
+        grad_c = mxu(pair_low, terms.b_low, 1, 0)
+        across = jnp.zeros((BLOCK, width), f32)
+        if block < blocks - 1:
+            state_low = grad_state.astype(LOW)
+            to_state = mxu(terms.b_low, state_low, 1, 0)
+            grad_values += terms.fade * terms.step * to_state
+            by_step = terms.fade * to_state * values
+            direct += mxu(by_step, same_head, 1, 0, exact)
+            grad_b += mxu(terms.faded.astype(LOW), state_low, 1, 1)
+            across += mxu(
+                ones_where(terms.col < terms.row, f32), terms.step * by_step, 1, 0, exact
+            )
+        if block:
+            entering = state_ref[block]
+            entering_low = entering.astype(LOW)
+            carried = terms.reach * mxu(terms.c_low, entering_low, 1, 0)
+            across += mxu(
+                ones_where(terms.col >= terms.row, f32), grad_mixed * carried, 1, 0, exact
+            )
+            reached = (terms.reach * grad_mixed).astype(LOW)
+            grad_c += mxu(reached, entering_low, 1, 1)
+            if block < blocks - 1:
+                across += row_sum(grad_state * terms.reach_last * entering)
+            grad_state = terms.reach_last * grad_state + mxu(terms.c_low, reached, 0, 0)
+        between += mxu(across, same_head, 1, 0, exact)
+        grad_step = direct + rates * between
+        add("rates", row_sum(terms.step * between))
+        grad_step_in = grad_step * sigmoid(step_in)
+        add("step_bias", row_sum(grad_step_in))
+        e = grad_values * (terms.value_sig * (1.0 + terms.value_arg * (1.0 - terms.value_sig)))
+        e_ref[rows, :] = e
+        e_bc = jnp.concatenate([grad_b, grad_c], axis=1) * (
+            terms.bc_sig * (1.0 + terms.bc_arg * (1.0 - terms.bc_sig))
+        )
+        e_bc_ref[rows, :] = e_bc
+        add("value_bias", row_sum(e))
+        add("bc_bias", row_sum(e_bc))
+        grad_value = jnp.zeros((BLOCK, width), f32)
+        grad_bc = jnp.zeros((BLOCK, bc_width), f32)
+        for distance in range(4):
+            tap = 3 - distance
+            add(("value", tap), row_sum(e * terms.back(value_ref, distance, width)))
+            add(("bc", tap), row_sum(e_bc * terms.back(bc_ref, distance, bc_width)))
+            grad_value += small_ref[tap : tap + 1, :width] * terms.ahead(e_ref, distance, width)
+            grad_bc += small_ref[9 + tap : 10 + tap, :] * terms.ahead(e_bc_ref, distance, bc_width)
+        value_low = grad_value.astype(LOW)
+        pre_ref[rows, VALUE_AT : VALUE_AT + 128] = value_low[:, 0:128]
+        pre_ref[rows, VALUE_AT + 128 : VALUE_AT + 256] = (
+            mxu(value_low, tail, 1, 0) + mxu(grad_step_in.astype(LOW), pick, 1, 0)
+        ).astype(LOW)
+        part = mxu(pre_ref[rows, :], wall_ref[...], 1, 1).astype(LOW)
+        grad_bc = grad_bc.astype(LOW)
+        for at in range(0, BLOCK, piece):
+            slot = (start + at) // piece
+            both_ref[slot, :, 0:model_width] = part[at : at + piece]
+            both_ref[slot, :, model_width:] = grad_bc[at : at + piece]
+
+    k_rows = grads_ref.shape[1]
+    for pair in range(grads_ref.shape[0] // 2):
+        lanes = pl.ds(pair * 2 * k_rows, 2 * k_rows)
+        total = mxu(normed_ref[:, lanes], pre_ref[...], 0, 0)
+        out = mxu(grad_ref[:, lanes], scaled_ref[...], 0, 0)
+        for at in range(2):
+            k_slice = slice(at * k_rows, (at + 1) * k_rows)
+            slot = 2 * pair + at
+            grads_ref[slot, :, 0:OUT_AT] = total[k_slice, 0:OUT_AT].astype(LOW)
+            grads_ref[slot, :, OUT_AT:VALUE_AT] = (
+                total[k_slice, OUT_AT:VALUE_AT] + out[k_slice]
+            ).astype(LOW)
+            grads_ref[slot, :, VALUE_AT:] = total[k_slice, VALUE_AT:].astype(LOW)
+
+    sums_ref[...] = jnp.zeros(sums_ref.shape, f32)
+    head_sums = mxu(
+        jnp.concatenate([sums["skip"], jnp.zeros((7, width), f32)], axis=0), same_head, 1, 0, exact
+    )
+    for tap in range(4):
+        sums_ref[tap : tap + 1, 0:width] = sums["value", tap]
+        sums_ref[9 + tap : 10 + tap, :] = sums["bc", tap]
+    sums_ref[4:5, 0:width] = sums["value_bias"]
+    sums_ref[5:6, 0:width] = sums["out_gain"]
+    sums_ref[6:7, 0:width] = head_sums[0:1]
+    sums_ref[7:8, 0:width] = sums["step_bias"]
+    sums_ref[8:9, 0:width] = sums["rates"] * rates
+    sums_ref[13:14, :] = sums["bc_bias"]
+
+
+def split_backward(grad, scalars, normed, wall, small, segr, segc, kept, slots):
+    tokens, model_width = normed.shape
+    piece = tokens // slots
+    width = kept[0].shape[1]
+    bc_width = kept[2].shape[1]
+    k_slots = slots // 2
+    return pl.pallas_call(
+        backward_kernel,
+        out_shape=[
+            jax.ShapeDtypeStruct((slots, piece, model_width + bc_width), LOW),
+            jax.ShapeDtypeStruct((k_slots, model_width // k_slots, PACK), LOW),
+            jax.ShapeDtypeStruct((16, 256), jnp.float32),
+        ],
+        in_specs=[VMEM_SPEC] * 13,
+        out_specs=[VMEM_SPEC] * 3,
+        scratch_shapes=[
+            pltpu.VMEM((tokens, PACK), LOW),
+            pltpu.VMEM((tokens, 256), LOW),
+            pltpu.VMEM((tokens + 8, width), jnp.float32),
+            pltpu.VMEM((tokens + 8, bc_width), jnp.float32),
+        ],
+        compiler_params=local_params(),
+        name="backward_block",
+    )(grad, scalars, normed, wall, small, segr, segc, *kept)
+
+
+def lane_rows(columns, slots):
+    rows = jnp.stack([c.reshape(slots, -1) for c in columns], axis=1)
+    return jnp.pad(rows, ((0, 0), (0, 8 - rows.shape[1]), (0, 128 - rows.shape[2])))
+
+
+def norm_rows(hidden, gain):
+    inv = lax.rsqrt(jnp.mean(hidden * hidden, axis=1, keepdims=True) + epsilon)
+    return inv, (hidden * inv * gain).astype(jnp.bfloat16)
+
+
+HALVES = 2
+
+
+class Links:
+    def __init__(self, depth):
+        self.depth = depth
+        self.x, self.z, self.t = (lax.axis_index(name) for name in ("dp", "ctx", "tp"))
+        self.core, self.chip = {"tp": other_core(self.t)}, {"tp": other_chip(self.t)}
+        self.far_x = {"dp": 1 - self.x}
+        self.left = {"ctx": lax.rem(self.z + depth - 1, depth)}
+        self.right = {"ctx": lax.rem(self.z + 1, depth)}
+        self.sent = []
+
+    def send(self, source, target, send_sem, recv_sem, peer, when=None):
+        copy = remote(source, target, send_sem, recv_sem, peer)
+        self.sent.append((copy, when))
+        if when is None:
+            copy.start()
+        else:
+            pl.when(when)(copy.start)
+
+    def wait(self, ref, send_sem, recv_sem, when=None):
+        copy = remote(ref, ref, send_sem, recv_sem, self.core)
+        if when is None:
+            copy.wait_recv()
+        else:
+            pl.when(when)(copy.wait_recv)
+
+    def finish(self):
+        for copy, when in self.sent:
+            if when is None:
+                copy.wait_send()
+            else:
+                pl.when(when)(copy.wait_send)
+
+    def near_first(self):
+        z = self.z
+        first = z + 1 - 2 * lax.rem(z, 2)
+        third = 3 - 3 * (z // 2)
+        return [first, 6 - z - first - third, third]
+
+    def far_first(self):
+        z = self.z
+        odd = lax.rem(z, 2)
+        first = 3 - 3 * (z // 2)
+        second = (1 - odd) * (2 + z // 2) + odd * (z // 2)
+        return [first, second, 6 - z - first - second]
+
+
+def everyone(depth):
+    z, t = lax.axis_index("ctx"), lax.axis_index("tp")
+    return [
+        {"ctx": lax.rem(z + hop, depth), "tp": lax.rem(t + turn, 4)}
+        for hop in range(depth)
+        for turn in range(4)
+        if hop or turn
+    ]
+
+
+def half(ref, part):
+    rows = ref.shape[0] // HALVES
+    return ref.at[pl.ds(part * rows, rows)]
+
+
+def gather_task(links, pieces, fulls, send_sem, recv_sem):
+    z, t = links.z, links.t
+    last = links.depth - 1
+    own = z * 4 + t
+
+    def pass_on(a, ref, slot, part, to_left, to_right, chip=True):
+        target = half(fulls[a].at[slot], part)
+        recv = recv_sem.at[a, slot, part]
+
+        def go(way, peer, when=None):
+            links.send(ref, target, send_sem.at[a, slot, part, way], recv, peer, when)
+
+        if chip:
+            go(0, links.left, to_left)
+            go(1, links.right, to_right)
+            go(2, links.chip)
+        go(3, links.core)
+
+    def arrived(a, slot, part):
+        ref = half(fulls[a].at[slot], part)
+        links.wait(ref, send_sem.at[a, slot, part, 0], recv_sem.at[a, slot, part])
+        return ref
+
+    every = range(len(pieces))
+    for part in range(HALVES):
+        for a in every:
+            pass_on(a, half(pieces[a], part), own, part, z > 0, z < last)
+    for a in every:
+        fulls[a][own] = pieces[a][...]
+    yield
+    column = other_chip(t)
+    order = links.near_first()
+    for place, far in enumerate(order):
+        slot = far * 4 + t
+        for part in range(HALVES):
+            for a in every:
+                ref = arrived(a, slot, part)
+                to_left = jnp.logical_and(far > z, z > 0)
+                to_right = jnp.logical_and(far < z, z < last)
+                pass_on(a, ref, slot, part, to_left, to_right)
+        yield
+        slot = (order[place - 1] if place else z) * 4 + column
+        for part in range(HALVES):
+            for a in every:
+                pass_on(a, arrived(a, slot, part), slot, part, None, None, False)
+        yield
+    for part in range(HALVES):
+        for a in every:
+            slot = order[-1] * 4 + column
+            pass_on(a, arrived(a, slot, part), slot, part, None, None, False)
+    yield
+    for far in [z] + order:
+        for row in (other_core(t), other_chip(other_core(t))):
+            for part in range(HALVES):
+                for a in every:
+                    arrived(a, far * 4 + row, part)
+
+
+def gather_sems(count, slots):
+    return [
+        pltpu.SemaphoreType.DMA((count, slots, HALVES, 4)),
+        pltpu.SemaphoreType.DMA((count, slots, HALVES)),
+    ]
+
+
+def reduce_task(links, produce, parts, outs, bufs, send_sem, recv_sem):
+    z, t = links.z, links.t
+    depth = links.depth
+    last = depth - 1
+    order = links.far_first() + [z]
+    every = range(len(parts))
+
+    def rows_of(ref, part):
+        rows = ref.shape[0] // HALVES
+        return slice(part * rows, (part + 1) * rows)
+
+    def sems(a, at, part):
+        return send_sem.at[a, at, part], recv_sem.at[a, at, part]
+
+    def loaded(a, at, part):
+        return bufs[a][at, rows_of(bufs[a].at[at], part), :].astype(jnp.float32)
+
+    def mine(a, slot, part):
+        return parts[a][slot, rows_of(parts[a].at[slot], part), :].astype(jnp.float32)
+
+    def wait(a, at, part, when=None):
+        links.wait(half(bufs[a].at[at], part), *sems(a, at, part), when)
+
+    def stage1(far):
+        produce(far)
+        for which, row in enumerate((other_chip(other_core(t)), other_core(t))):
+            for part in range(HALVES):
+                for a in every:
+                    at = far * 2 + which
+                    links.send(
+                        half(parts[a].at[far * 4 + row], part),
+                        half(bufs[a].at[at], part),
+                        *sems(a, at, part),
+                        links.core,
+                    )
+
+    def stage2(far):
+        for part in range(HALVES):
+            for a in every:
+                at = far * 2
+                wait(a, at, part)
+                total = mine(a, far * 4 + other_chip(t), part) + loaded(a, at, part)
+                bufs[a][at, rows_of(bufs[a].at[at], part), :] = total.astype(bufs[a].dtype)
+                to = 2 * depth + far
+                links.send(
+                    half(bufs[a].at[at], part), half(bufs[a].at[to], part), *sems(a, to, part), links.chip
+                )
+
+    def stage3(far):
+        at = far * 2 + 1
+        for part in range(HALVES):
+            for a in every:
+                wait(a, at, part)
+                wait(a, 2 * depth + far, part)
+                total = mine(a, far * 4 + t, part) + loaded(a, at, part) + loaded(a, 2 * depth + far, part)
+                out = outs[a]
+                rows = rows_of(out, part)
+                if far is z:
+                    out[rows, :] = total
+                    continue
+                ref = bufs[a]
+                here = (at, rows_of(ref.at[at], part), slice(None))
+                for way, (peer, when, first) in enumerate(
+                    ((links.right, far > z, z == 0), (links.left, far < z, z == last))
+                ):
+                    chain = 3 * depth + way * depth + far
+
+                    def go(total=total, chain=chain, here=here, ref=ref, first=first, a=a, part=part):
+                        @pl.when(first)
+                        def _():
+                            ref[here] = total.astype(ref.dtype)
+
+                        @pl.when(jnp.logical_not(first))
+                        def _():
+                            wait(a, chain, part)
+                            ref[here] = (total + loaded(a, chain, part)).astype(ref.dtype)
+
+                    pl.when(when)(go)
+                    links.send(
+                        half(ref.at[at], part), half(ref.at[chain], part), *sems(a, chain, part), peer, when
+                    )
+
+    count = len(order)
+    for place in range(count + 2):
+        if place < count:
+            stage1(order[place])
+        if 1 <= place <= count:
+            stage2(order[place - 1])
+        if 2 <= place:
+            stage3(order[place - 2])
+        yield
+    for way, when in enumerate((z > 0, z < last)):
+        chain = 3 * depth + way * depth + z
+        for part in range(HALVES):
+            for a in every:
+
+                @pl.when(when)
+                def _(a=a, part=part, chain=chain):
+                    wait(a, chain, part)
+                    outs[a][rows_of(outs[a], part), :] += loaded(a, chain, part)
+
+
+def reduce_scratch(shapes, dtypes, depth):
+    return [pltpu.VMEM((5 * depth,) + s, d) for s, d in zip(shapes, dtypes)] + [
+        pltpu.SemaphoreType.DMA((len(shapes), 5 * depth, HALVES)),
+        pltpu.SemaphoreType.DMA((len(shapes), 5 * depth, HALVES)),
+    ]
+
+
+def run_tasks(*tasks):
+    tasks = list(tasks)
+    while tasks:
+        for task in list(tasks):
+            try:
+                next(task)
+            except StopIteration:
+                tasks.remove(task)
+
+
+def share_task(links, own, full, send_sem, recv_sem):
+    depth = links.depth
+    slot = links.z * 4 + links.t
+    for at, peer in enumerate(everyone(depth)):
+        links.send(own, full.at[slot], send_sem.at[at], recv_sem.at[slot], peer)
+    full[slot] = own[...]
+    yield
+    for hop in range(depth):
+        for turn in range(4):
+            if hop or turn:
+                source = lax.rem(links.z + hop, depth) * 4 + lax.rem(links.t + turn, 4)
+                links.wait(full.at[source], send_sem.at[0], recv_sem.at[source])
+
+
+def spread_rows(rows):
+    size = rows.shape[1]
+    eye = ones_where(iota((size, size), 0) == iota((size, size), 1), jnp.float32)
+    return mxu(eye, rows, 1, 1, exact)
+
+
+def turn_forward_kernel(
+    depth,
+    gated_ref,
+    squares_ref,
+    small_ref,
+    wall_ref,
+    hidden_ref,
+    gain_ref,
+    hidden_out,
+    total_out,
+    inv_out,
+    full_out,
+    parts,
+    normed,
+    shared,
+    share_send,
+    share_recv,
+    bufs,
+    reduce_send,
+    reduce_recv,
+    gather_send,
+    gather_recv,
+):
+    links = Links(depth)
+    greet(everyone(depth))
+    width = gated_ref.shape[1]
+    piece = hidden_ref.shape[0]
+    block = 4 * piece
+    run_tasks(share_task(links, squares_ref, shared, share_send, share_recv))
+    total = shared[0]
+    for slot in range(1, 4 * depth):
+        total = total + shared[slot]
+    inv_rows = lax.rsqrt(total / INNER + epsilon)
+    inv_out[...] = inv_rows
+    columns = spread_rows(inv_rows)
+    shift = lane_shift(width)
+    gains = small_ref[5:6, :width]
+    which = iota((block, columns.shape[1]), 1)
+
+    def produce(far):
+        at = far * (block // 128)
+        both = jnp.concatenate([columns] * (block // 128), axis=0)
+        low = iota((block, columns.shape[1]), 0) // 128 + at
+        inv = jnp.sum(jnp.where(which == low, both, 0.0), axis=1, keepdims=True)
+        rows = pl.ds(pl.multiple_of(far * block, block), block)
+        scaled = (gated_ref[rows, :] * inv * gains).astype(LOW)
+        moved = mxu(scaled, shift, 1, 0).astype(LOW)
+        part = mxu(moved, wall_ref[:, OUT_AT : OUT_AT + 256], 1, 1)
+        for row in range(4):
+            parts[far * 4 + row] = part[row * piece : (row + 1) * piece].astype(parts.dtype)
+
+    run_tasks(
+        reduce_task(links, produce, [parts], [total_out], [bufs], reduce_send, reduce_recv)
+    )
+    hidden = hidden_ref[...].astype(jnp.float32) + total_out[...]
+    hidden_out[...] = hidden
+    inv = lax.rsqrt(jnp.mean(hidden * hidden, axis=1, keepdims=True) + epsilon)
+    normed[...] = (hidden * inv * gain_ref[...]).astype(LOW)
+    run_tasks(gather_task(links, [normed], [full_out], gather_send, gather_recv))
+    links.finish()
+
+
+def turn_forward(gated, squares, small, wall, hidden, gain, depth, collective_id):
+    piece, model_width = hidden.shape
+    slots = 4 * depth
+    f32 = jnp.float32
+    return pl.pallas_call(
+        partial(turn_forward_kernel, depth),
+        out_shape=[
+            jax.ShapeDtypeStruct((piece, model_width), f32),
+            jax.ShapeDtypeStruct((piece, model_width), f32),
+            jax.ShapeDtypeStruct(squares.shape, f32),
+            jax.ShapeDtypeStruct((slots, piece, model_width), LOW),
+        ],
+        in_specs=[VMEM_SPEC] * 6,
+        out_specs=[VMEM_SPEC] * 4,
+        scratch_shapes=[
+            pltpu.VMEM((slots, piece, model_width), f32),
+            pltpu.VMEM((piece, model_width), LOW),
+            pltpu.VMEM((slots,) + squares.shape, f32),
+            pltpu.SemaphoreType.DMA((slots,)),
+            pltpu.SemaphoreType.DMA((slots,)),
+        ]
+        + reduce_scratch([(piece, model_width)], [f32], depth)
+        + gather_sems(1, slots),
+        compiler_params=params_of(collective_id),
+        name="turn_forward",
+    )(gated, squares, small, wall, hidden, gain)
+
+
+def turn_backward_kernel(
+    depth,
+    last,
+    both_ref,
+    grad_ref,
+    hidden_ref,
+    gain_ref,
+    bcw_ref,
+    total_ref,
+    scalar_ref,
+    grad_out,
+    gain_out,
+    low_out,
+    *refs,
+):
+    links = Links(depth)
+    greet(everyone(depth))
+    if last:
+        full_out, total, piece_low, bufs, reduce_send, reduce_recv, gather_send, gather_recv = refs
+    else:
+        full_out, scalar_out, total, piece_low, scalars, bufs, reduce_send, reduce_recv, gather_send, gather_recv = refs
+    model_width = hidden_ref.shape[1]
+    piece = hidden_ref.shape[0]
+    run_tasks(
+        reduce_task(
+            links, lambda far: None, [both_ref], [total], [bufs], reduce_send, reduce_recv
+        )
+    )
+    bc_low = total[:, model_width:].astype(LOW)
+    grad_normed = total[:, :model_width] + mxu(bc_low, bcw_ref[...], 1, 1)
+    hidden = hidden_ref[...].astype(jnp.float32)
+    inv = lax.rsqrt(jnp.mean(hidden * hidden, axis=1, keepdims=True) + epsilon)
+    weighted = grad_normed * gain_ref[...]
+    gain_out[...] = row_sum(grad_normed * hidden * inv)
+    grad = (
+        grad_ref[...].astype(jnp.float32)
+        + inv * weighted
+        - hidden * (inv * inv * inv) * jnp.mean(weighted * hidden, axis=1, keepdims=True)
+    )
+    grad_low = grad.astype(LOW)
+    low_out[...] = grad_low
+    grad_out[...] = grad
+    if last:
+        piece_low[...] = bc_low
+        run_tasks(gather_task(links, [piece_low], [full_out], gather_send, gather_recv))
+    else:
+        piece_low[:, :model_width] = grad_low
+        piece_low[:, model_width:] = bc_low
+        inner = jnp.sum(grad_low.astype(jnp.float32) * total_ref[...], axis=1, keepdims=True) / INNER
+        eye = ones_where(iota((piece, 128), 0) == iota((piece, 128), 1), jnp.float32)
+        row = mxu(jnp.broadcast_to(inner, (piece, 8)), eye, 0, 0, exact)
+        scalars[...] = jnp.where(iota((8, 128), 0) == 1, row, scalar_ref[...])
+        run_tasks(
+            gather_task(links, [piece_low, scalars], [full_out, scalar_out], gather_send, gather_recv)
+        )
+    links.finish()
+
+
+def turn_backward(both, grad, hidden, gain, bcw, total, scalars, last, depth, collective_id):
+    piece, model_width = hidden.shape
+    slots, _, whole_width = both.shape
+    f32 = jnp.float32
+    low_width = whole_width - model_width if last else whole_width
+    fulls = [jax.ShapeDtypeStruct((slots, piece, low_width), LOW)]
+    own = [pltpu.VMEM((piece, low_width), LOW)]
+    if not last:
+        fulls.append(jax.ShapeDtypeStruct((slots, 8, 128), f32))
+        own.append(pltpu.VMEM((8, 128), f32))
+    return pl.pallas_call(
+        partial(turn_backward_kernel, depth, last),
+        out_shape=[
+            jax.ShapeDtypeStruct((piece, model_width), f32),
+            jax.ShapeDtypeStruct((1, model_width), f32),
+            jax.ShapeDtypeStruct((piece, model_width), LOW),
+        ]
+        + fulls,
+        in_specs=[VMEM_SPEC] * 7,
+        out_specs=[VMEM_SPEC] * (3 + len(fulls)),
+        scratch_shapes=[pltpu.VMEM((piece, whole_width), f32)]
+        + own
+        + reduce_scratch([(piece, whole_width)], [LOW], depth)
+        + gather_sems(len(fulls), slots),
+        compiler_params=params_of(collective_id),
+        name="turn_backward",
+    )(both, grad, hidden, gain, bcw, total, scalars)
+
+
+def weights_task(links, packs, fulls, send_sem, recv_sem):
+    x, z, depth = links.x, links.z, links.depth
+    every = range(len(packs))
+
+    def source(a, far, part):
+        ref = packs[a]
+        return half(ref.at[far] if len(ref.shape) == len(fulls[a].shape) else ref, part)
+
+    def send(a, ref, slot, part, kind, peer):
+        links.send(
+            ref, half(fulls[a].at[slot], part), send_sem.at[a, kind, part], recv_sem.at[a, slot, part], peer
+        )
+
+    def arrived(a, slot, part):
+        ref = half(fulls[a].at[slot], part)
+        links.wait(ref, send_sem.at[a, 0, part], recv_sem.at[a, slot, part])
+        return ref
+
+    mine = x * depth + z
+    for a in every:
+        for part in range(HALVES):
+            send(a, source(a, z, part), mine, part, 0, links.far_x)
+    for place, far in enumerate(links.far_first()):
+        for a in every:
+            for part in range(HALVES):
+                send(a, source(a, far, part), mine, part, 1 + place, {"ctx": far})
+    for a in every:
+        ref = packs[a]
+        fulls[a][mine] = ref[z] if len(ref.shape) == len(fulls[a].shape) else ref[...]
+    yield
+    for place, far in enumerate(links.near_first()):
+        for part in range(HALVES):
+            for a in every:
+                slot = x * depth + far
+                send(a, arrived(a, slot, part), slot, part, depth + place, links.far_x)
+        yield
+    for far in [z] + links.near_first():
+        for part in range(HALVES):
+            for a in every:
+                arrived(a, (1 - x) * depth + far, part)
+
+
+def weights_sems(count, depth):
+    return [
+        pltpu.SemaphoreType.DMA((count, 2 * depth, HALVES)),
+        pltpu.SemaphoreType.DMA((count, 2 * depth, HALVES)),
+    ]
+
+
+def prepare_kernel(depth, count, *refs):
+    pieces, packs = refs[:count], refs[count : count + 2]
+    refs = refs[count + 2 :]
+    fulls, full_packs = refs[:count], refs[count : count + 2]
+    gather_send, gather_recv, pack_send, pack_recv = refs[count + 2 :]
+    links = Links(depth)
+    greet(everyone(depth) + [links.far_x])
+    run_tasks(
+        gather_task(links, pieces, fulls, gather_send, gather_recv),
+        weights_task(links, packs, full_packs, pack_send, pack_recv),
+    )
+    links.finish()
+
+
+def prepare(pieces, packs, depth, collective_id):
+    count = len(pieces)
+    slots = 4 * depth
+    return pl.pallas_call(
+        partial(prepare_kernel, depth, count),
+        out_shape=[jax.ShapeDtypeStruct((slots,) + p.shape, p.dtype) for p in pieces]
+        + [jax.ShapeDtypeStruct((2 * depth,) + p.shape[-2:], p.dtype) for p in packs],
+        in_specs=[VMEM_SPEC] * (count + 2),
+        out_specs=[VMEM_SPEC] * (count + 2),
+        scratch_shapes=gather_sems(count, slots) + weights_sems(2, depth),
+        compiler_params=params_of(collective_id),
+        name="prepare",
+    )(*pieces, *packs)
+
+
+def finish_kernel(depth, channel_rows, sums_ref, hidden_ref, grad_ref, by_z_out, sum_out, hidden_out, grad_out, work, total, arrived_ref, send_sem, recv_sem, row_send, row_recv):
+    links = Links(depth)
+    z, t = links.z, links.t
+    greet(everyone(depth) + [links.far_x])
+
+    def rows():
+        outs = (hidden_out, grad_out)
+        for a, ref in enumerate((hidden_ref, grad_ref)):
+            for way, peer in enumerate((links.chip, links.core)):
+                links.send(ref, outs[a].at[t], row_send.at[a, way], row_recv.at[a, t], peer)
+            outs[a][t] = ref[...]
+        yield
+        for a in range(2):
+            column = other_chip(t)
+            ref = outs[a].at[column]
+            links.wait(ref, row_send.at[a, 0], row_recv.at[a, column])
+            links.send(ref, ref, row_send.at[a, 2], row_recv.at[a, column], links.core)
+        yield
+        for a in range(2):
+            for column in (other_core(t), other_chip(other_core(t))):
+                links.wait(outs[a].at[column], row_send.at[a, 0], row_recv.at[a, column])
+
+    def sums():
+        links.send(sums_ref, arrived_ref.at[0], send_sem.at[0], recv_sem.at[0], links.far_x)
+        yield
+        links.wait(arrived_ref.at[0], send_sem.at[0], recv_sem.at[0])
+        work[...] = sums_ref[...] + arrived_ref[0]
+        links.send(work, arrived_ref.at[1], send_sem.at[1], recv_sem.at[1], links.core)
+        yield
+        links.wait(arrived_ref.at[1], send_sem.at[1], recv_sem.at[1])
+        total[0] = work[...] + arrived_ref[1]
+        links.send(total.at[0], arrived_ref.at[2], send_sem.at[2], recv_sem.at[2], links.chip)
+        yield
+        links.wait(arrived_ref.at[2], send_sem.at[2], recv_sem.at[2])
+        row = iota(work.shape, 0)
+        own = jnp.logical_and(row < 16 * LAYERS, lax.rem(row, 16) < channel_rows)
+        total[1] = jnp.where(own, work[...], total[0] + arrived_ref[2])
+        for hop in range(1, depth):
+            links.send(
+                total.at[1], by_z_out.at[z], send_sem.at[2 + hop], recv_sem.at[3 + z], {"ctx": lax.rem(z + hop, depth)}
+            )
+        by_z_out[z] = total[1]
+        yield
+        for hop in range(1, depth):
+            far = lax.rem(z + hop, depth)
+            links.wait(by_z_out.at[far], send_sem.at[0], recv_sem.at[3 + far])
+        whole = by_z_out[0]
+        for far in range(1, depth):
+            whole = whole + by_z_out[far]
+        sum_out[...] = whole
+
+    run_tasks(rows(), sums())
+    links.finish()
+
+
+def finish(sums, hidden, grad, depth, collective_id):
+    f32 = jnp.float32
+    return pl.pallas_call(
+        partial(finish_kernel, depth, 9),
+        out_shape=[
+            jax.ShapeDtypeStruct((depth,) + sums.shape, f32),
+            jax.ShapeDtypeStruct(sums.shape, f32),
+            jax.ShapeDtypeStruct((4,) + hidden.shape, hidden.dtype),
+            jax.ShapeDtypeStruct((4,) + grad.shape, grad.dtype),
+        ],
+        in_specs=[VMEM_SPEC] * 3,
+        out_specs=[VMEM_SPEC] * 4,
+        scratch_shapes=[
+            pltpu.VMEM(sums.shape, f32),
+            pltpu.VMEM((2,) + sums.shape, f32),
+            pltpu.VMEM((3,) + sums.shape, f32),
+            pltpu.SemaphoreType.DMA((3 + depth,)),
+            pltpu.SemaphoreType.DMA((3 + depth,)),
+            pltpu.SemaphoreType.DMA((2, 3)),
+            pltpu.SemaphoreType.DMA((2, 4)),
+        ],
+        compiler_params=params_of(collective_id),
+        name="finish",
+    )(sums, hidden, grad)
+
+
+def split_local(
+    depth,
+    hidden_in,
+    segment_ids,
+    cotangent,
+    norm_gain,
+    gate_proj,
+    value_proj,
+    bc_proj,
+    step_proj,
+    conv_value,
+    conv_value_bias,
+    conv_bc,
+    conv_bc_bias,
+    decay_log,
+    step_bias,
+    skip_gain,
+    out_gain,
+    out_proj,
+):
+    tokens, model_width = hidden_in.shape[1:]
+    slots = depth * 4
+    piece = tokens // 4
+    width = gate_proj.shape[2] // depth
+    heads = step_proj.shape[2] // depth
+    k_rows = gate_proj.shape[1]
+    f32 = jnp.float32
+    t = lax.axis_index("tp")
+    z = lax.axis_index("ctx")
+
+    def own_piece(array):
+        return lax.dynamic_slice_in_dim(array, t * piece, piece, 0)
+
+    my_hidden = own_piece(hidden_in[0])
+    my_cotangent = own_piece(cotangent[0])
+    gains = [norm_gain[layer].astype(f32) for layer in range(LAYERS)]
+
+    def by_z(block):
+        return block.reshape(block.shape[0], depth, -1).transpose(1, 0, 2)
+
+    packs, shared = [], []
+    for layer in range(LAYERS):
+        pack = jnp.concatenate(
+            [
+                by_z(gate_proj[layer]),
+                by_z(out_proj[layer].T),
+                by_z(value_proj[layer]),
+                by_z(step_proj[layer]),
+            ],
+            axis=2,
+        )
+        packs.append(jnp.pad(pack, ((0, 0), (0, 0), (0, PACK - pack.shape[2]))))
+        shared.append(bc_proj[layer])
+    hidden0 = my_hidden.astype(f32)
+    _, my_normed0 = norm_rows(hidden0, gains[0])
+    seg_rows = lane_rows([own_piece(segment_ids[0]).astype(f32)[None]], 1)[0]
+    normed0, seg_full, pack0, shared0 = prepare([my_normed0, seg_rows], [packs[0], shared[0]], depth, 1)
+    cotangent_full, pack1, shared1 = prepare([my_cotangent], [packs[1], shared[1]], depth, 2)
+    walls = [pack0.reshape(-1, PACK), pack1.reshape(-1, PACK)]
+    bc_walls = [shared0.reshape(-1, shared0.shape[2]), shared1.reshape(-1, shared1.shape[2])]
+    normed0 = normed0.reshape(-1, model_width)
+    cotangent_full = cotangent_full.reshape(-1, model_width)
+    segment = seg_full[:, 0, :piece].reshape(-1)
+    segr = segment[None]
+    segc = jnp.broadcast_to(jnp.pad(segment, 8, constant_values=-1.0)[:, None], (segment.size + 16, 256))
+
+    def per_lane(by_head):
+        return jnp.repeat(by_head, HEADDIM, axis=1)[:, None]
+
+    per_channel = jnp.concatenate(
+        [
+            conv_value.astype(f32),
+            conv_value_bias.astype(f32)[:, None],
+            out_gain.astype(f32)[:, None],
+            per_lane(skip_gain),
+            per_lane(step_bias),
+            per_lane(-jnp.exp(decay_log)),
+        ],
+        axis=1,
+    )
+    per_channel = lax.dynamic_slice_in_dim(per_channel, z * width, width, 2)
+    per_channel = jnp.pad(per_channel, ((0, 0), (0, 0), (0, 256 - width)))
+    smalls = jnp.concatenate(
+        [per_channel, conv_bc.astype(f32), conv_bc_bias.astype(f32)[:, None], jnp.zeros((LAYERS, 2, 256), f32)],
+        axis=1,
+    )
+
+    def forward(layer, normed, precise):
+        return split_forward(
+            normed, walls[layer], bc_walls[layer], smalls[layer], segr, segc, slots, precise
+        )
+
+    def backward(layer, grad, scalars, normed, kept):
+        return split_backward(
+            grad, scalars, normed, walls[layer], smalls[layer], segr, segc, kept, slots
+        )
+
+    gated0, squares0, *kept0 = forward(0, normed0, True)
+    hidden1, total0, inv_rows0, normed1 = turn_forward(
+        gated0, squares0, smalls[0], walls[0], my_hidden, gains[1][None], depth, 3
+    )
+    inv0 = lax.dynamic_slice_in_dim(inv_rows0.reshape(-1), (z * 4 + t) * piece, piece, 0)
+    normed1 = normed1.reshape(-1, model_width)
+    part1, squares1, *kept1 = forward(1, normed1, False)
+    total1, square_rows1 = reduce_pieces([part1, squares1], depth, 5)
+    inv1 = lax.rsqrt(square_rows1[0, :piece] / INNER + epsilon)
+    total1 = total1 * inv1[:, None]
+    hidden_out = (hidden1 + total1).astype(LOW)
+
+    def bc_grad(normed, bc_low):
+        return jnp.stack(
+            [
+                dot_left(
+                    lax.dynamic_slice_in_dim(normed, (far_x * depth + z) * k_rows, k_rows, 1), bc_low
+                ).astype(LOW)
+                for far_x in range(2)
+            ]
+        )
+
+    def scalar_rows(inv, inner):
+        return lane_rows([inv[None], inner[None] / INNER], 1)[0]
+
+    inner1 = jnp.sum(my_cotangent.astype(f32) * total1, axis=1)
+    (scalars1,) = gather_pieces([scalar_rows(inv1, inner1)], depth, 8)
+    both1, grads1, sums1 = backward(1, cotangent_full, scalars1, normed1, kept1)
+    grad1, gain_grad1, _, full0, scalars0 = turn_backward(
+        both1,
+        my_cotangent,
+        hidden1,
+        gains[1][None],
+        bc_walls[1],
+        total0,
+        scalar_rows(inv0, jnp.zeros_like(inv0)),
+        False,
+        depth,
+        6,
+    )
+    full0 = full0.reshape(-1, full0.shape[2])
+    out1, bc_out1 = scatter_grads(grads1, bc_grad(normed1, full0[:, model_width:]), depth, 10)
+    both0, grads0, sums0 = backward(0, full0, scalars0, normed0, kept0)
+    _, gain_grad0, grad_low0, bc_all0 = turn_backward(
+        both0, grad1, my_hidden, gains[0][None], bc_walls[0], total0, scalars0[0], True, depth, 7
+    )
+    out0, bc_out0 = scatter_grads(
+        grads0, bc_grad(normed0, bc_all0.reshape(-1, bc_all0.shape[2])), depth, 12
+    )
+
+    outs = jnp.stack([out0, out1]).astype(f32)
+
+    def channels(lo, hi):
+        return outs[..., lo:hi].transpose(0, 2, 1, 3).reshape(LAYERS, k_rows, -1)
+
+    gain_rows = jnp.concatenate([gain_grad0, gain_grad1], axis=0).reshape(-1, 256)
+    gain_count = gain_rows.shape[0]
+    sums = jnp.concatenate([sums0, sums1, gain_rows, jnp.zeros((16 - gain_count, 256), f32)], axis=0)
+    by_z, whole, hidden_out, grad_hidden = finish(sums, hidden_out, grad_low0, depth, 13)
+    by_channel = jnp.stack([by_z[:, 16 * layer : 16 * layer + 9, :width] for layer in range(LAYERS)])
+    by_channel = by_channel.transpose(0, 2, 1, 3).reshape(LAYERS, 9, -1)
+    bc_sums = jnp.stack([whole[16 * layer + 9 : 16 * layer + 14] for layer in range(LAYERS)])
+    gain_grad = whole[16 * LAYERS : 16 * LAYERS + gain_count].reshape(LAYERS, model_width)
+
+    def by_head(row):
+        return by_channel[:, row].reshape(LAYERS, -1, HEADDIM)[:, :, 0]
+
+    return (
+        hidden_out.reshape(1, tokens, model_width),
+        grad_hidden.reshape(1, tokens, model_width),
+        gain_grad,
+        channels(0, width),
+        channels(2 * width, 3 * width),
+        jnp.stack([bc_out0, bc_out1]),
+        channels(3 * width, 3 * width + heads),
+        by_channel[:, :4],
+        by_channel[:, 4],
+        bc_sums[:, :4],
+        bc_sums[:, 4],
+        by_head(8),
+        by_head(7),
+        by_head(6),
+        by_channel[:, 5],
+        channels(width, 2 * width).transpose(0, 2, 1),
+    )
+
+
 def solution(mesh):
     in_specs = (
         P("dp", "ctx", None),
@@ -491,4 +2009,8 @@
         P(None, "tp"),
         P(None, "tp", ("dp", "ctx")),
     )
-    return jax.shard_map(local, mesh=mesh, in_specs=in_specs, out_specs=out_specs, check_vma=False)
+    depth = mesh.shape["ctx"]
+    heads = 48 // mesh.shape["tp"]
+    fits = mesh.shape["tp"] == 4 and mesh.shape["dp"] == 2 and depth == 4 and heads % depth == 0
+    body = partial(split_local, depth) if fits else local
+    return jax.shard_map(body, mesh=mesh, in_specs=in_specs, out_specs=out_specs, check_vma=False)

time: 1520 us -> 626 us (0.41)
  waiting for transfers between devices: 866 us -> 0 us
  Pallas kernels: 0 us -> 544 us
  blocking collectives: 217 us -> 0 us
  matrix products: 125 us -> 7.26 us
  other arithmetic: 120 us -> 18.7 us
  local copies, waits for them, and re-layouts: 103 us -> 44.2 us
  starting transfers between devices: 55.9 us -> 0 us
  between operations: 20 us -> 1.32 us
    pallas_call x0 -> x14, Pallas kernels: none -> 544 us  [the longest x2 136 us: prepare(): pl.pallas_call(partial(prepare_kernel, depth, count), out_shape=[jax.Shap...]
    reduce_scatter x8 -> x0, waiting for transfers between devices: 509 us -> none  [the longest x2 142 us: layer_backward(): lax.psum_scatter(grad_out_proj.astype(jnp.bfloat16), ('dp', 'ctx'), scatt...]
    all_gather x4 -> x0, blocking collectives: 147 us -> none  [the longest x2 76.4 us: layer_forward(): lax.all_gather(bc_proj, ('dp', 'ctx'), axis=0, tiled=True)]
    ppermute x21 -> x0, waiting for transfers between devices: 122 us -> none  [from_behind(): return lax.ppermute(block, axis, route)]
    psum x4 -> x0, waiting for transfers between devices: 103 us -> none  [the longest x2 60.8 us: layer_backward(): lax.psum(grad_bc_pre.reshape(row_count, -1).astype(jnp.bfloat16), 'tp')]
    dot_general x48 -> x0, matrix products: 103 us -> none  [the longest x6 27.9 us: block_step(): intra_out = jnp.einsum('tsh,shp->thp', scores, values, precision=precise)]
    unnamed x22 -> x0, waiting for transfers between devices: 100 us -> none
    psum x6 -> x0, blocking collectives: 69.9 us -> none  [the longest x1 38.4 us: layer_backward(): lax.psum((grad_norm_gain, grad_conv_value.astype(jnp.float32), grad_conv_...]
  transfers between devices with their start and end apart: 41 -> 0, of which waited for: 28 -> 0; matrix products, arithmetic and copies ran while one was open for 11% -> 0% of each run, Pallas kernels for 0% -> 0%
where the time goes in v1:
time: 626 us; the launch traced here: 616 us
  Pallas kernels  544 us (87%)
  local copies, waits for them, and re-layouts  44.2 us (7%)
  other arithmetic  18.7 us (3%)
  matrix products  7.26 us (1%)
    pallas_call x2, Pallas kernels, prepare(): pl.pallas_call(partial(prepare_kernel, depth, count), out_shape=[jax.Shap...  136 us
    pallas_call x2, Pallas kernels, turn_backward(): pl.pallas_call(partial(turn_backward_kernel, depth, last), out_shape=[jax...  102 us
    pallas_call x1, Pallas kernels, turn_forward(): pl.pallas_call(partial(turn_forward_kernel, depth), out_shape=[jax.ShapeD...  72.4 us
    pallas_call x2, Pallas kernels, scatter_grads(): pl.pallas_call(partial(scatter_kernel, depth), out_shape=[jax.ShapeDtypeS...  68.1 us
    pallas_call x2, Pallas kernels, split_backward(): pl.pallas_call(backward_kernel, out_shape=[jax.ShapeDtypeStruct((slots, p...  64 us
    pallas_call x2, Pallas kernels, split_forward(): pl.pallas_call(partial(forward_kernel, precise), out_shape=first + [jax.S...  34 us
    pallas_call x1, Pallas kernels, reduce_pieces(): pl.pallas_call(partial(reduce_kernel, count, depth), out_shape=[jax.Shape...  32 us
    pallas_call x1, Pallas kernels, finish(): pl.pallas_call(partial(finish_kernel, depth, 9), out_shape=[jax.ShapeDtyp...  24.9 us

profile of v1, /device:TPU:0, one launch (start us, length us, event | category | flops | bytes accessed | tf_op | source)
XLA Modules:
  0.0 616.0 jit_solution(7430273573500651964)
XLA Ops:
  0.7 0.8 fusion.36
  1.6 0.7 exponential_negate_fusion
  2.3 0.7 reshape.185
  3.6 0.7 reshape.183
  4.3 0.7 reshape.184
  5.0 0.7 convert_element_type.73
  5.6 0.7 fusion.39
  6.4 1.4 slice_convert_fusion.1
  7.9 0.8 broadcast_in_dim.51
  8.7 0.8 broadcast_in_dim.50
  9.6 0.8 slice_reduce_fusion.3
  10.4 0.8 concatenate.20
  12.4 1.6 dynamic-slice_bitcast_fusion.1.refs_0_.grad_ref
  14.0 1.6 slice_bitcast_fusion.5
  15.6 1.1 fusion.24
  16.7 0.8 fusion.26.refs_0_
  19.4 1.1 slice_bitcast_fusion.3
  21.0 1.4 fusion.14.refs_2_
  22.8 1.4 fusion.17.refs_1_
  24.2 71.5 %prepare.3 = (bf16[16,64,1536]{2,1,0:T(8,128)(2,1)}, f32[16,8,128]{2,1,0:T(8,128)}, bf16[8,192,640]{2,1,0:T(8,128)(2,1)}, bf16[8,192,256]{2,1,0:T(8,128)(2,1)}) custom-call(bf16[64,1536]{1,0:T(8,128)(2,1)} %fusion.26.refs_0_, f32[8,128]{1,0:T(8,128)} %pad_bitcast_fusion.1.refs_1_, bf16[4,192,640]{2,1,0:T(8,128)(2,1)} %fusion.14.refs_2_, ...), custom_call_target="tpu_custom_call" | custom-call | tf_op jit(solution)/shard_map/prepare/pallas_call | solution.py:1697
  95.7 0.9 fusion.42
  96.7 0.7 broadcast_in_dim_reshape_squeeze.3.segr_ref
  97.4 1.2 broadcast_in_dim.56.segc_ref
  98.6 64.8 %prepare.2 = (bf16[16,64,1536]{2,1,0:T(8,128)(2,1)}, bf16[8,192,640]{2,1,0:T(8,128)(2,1)}, bf16[8,192,256]{2,1,0:T(8,128)(2,1)}) custom-call(bf16[64,1536]{1,0:T(8,128)(2,1)} %dynamic-slice_bitcast_fusion.1.refs_0_.grad_ref, bf16[4,192,640]{2,1,0:T(8,128)(2,1)} %fusion.17.refs_1_, bf16[192,256]{1,0:T(8,128)(2,1)} %get-tuple-element.182.refs_2_), custom_call_target="tpu_custom_call" | custom-call | tf_op jit(solution)/shard_map/prepare/pallas_call | solution.py:1697
  163.4 16.5 %forward_block.2 = (f32[1024,192]{1,0:T(8,128)}, f32[8,128]{1,0:T(8,128)}, f32[1024,192]{1,0:T(8,128)}, f32[1032,192]{1,0:T(8,128)}, f32[1032,256]{1,0:T(8,128)}...) custom-call(bf16[1024,1536]{1,0:T(8,128)(2,1)} %bitcast.126, bf16[1536,640]{1,0:T(8,128)(2,1)} %bitcast.123, ...), custom_call_target="tpu_custom_call" | custom-call | tf_op jit(solution)/shard_map/forward_block/pallas_call | solution.py:939
  179.9 72.4 %turn_forward.1 = (f32[64,1536]{1,0:T(8,128)}, f32[64,1536]{1,0:T(8,128)}, f32[8,128]{1,0:T(8,128)}, bf16[16,64,1536]{2,1,0:T(8,128)(2,1)}) custom-call(f32[1024,192]{1,0:T(8,128)} %get-tuple-element.71.gated_ref, f32[8,128]{1,0:T(8,128)} %get-tuple-element.72.squares_ref, f32[16,256]{1,0:T(8,128)} %get-tuple-element.193.small_ref, ...), custom_call_target="tpu_custom_call" | custom-call | tf_op jit(solution)/shard_map/turn_forward/pallas_call | solution.py:1520
  252.3 0.8 dynamic-slice_bitcast_fusion.2
  253.6 17.6 %forward_block.3 = (bf16[16,64,1536]{2,1,0:T(8,128)(2,1)}, f32[16,8,128]{2,1,0:T(8,128)}, f32[1024,192]{1,0:T(8,128)}, f32[1032,192]{1,0:T(8,128)}, f32[1032,256...) custom-call(bf16[1024,1536]{1,0:T(8,128)(2,1)} %bitcast.130, ...), custom_call_target="tpu_custom_call" | custom-call | tf_op jit(solution)/shard_map/forward_block/pallas_call | solution.py:939
  271.2 32.0 %reduce_pieces.1 = (f32[64,1536]{1,0:T(8,128)}, f32[8,128]{1,0:T(8,128)}) custom-call(bf16[16,64,1536]{2,1,0:T(8,128)(2,1)} %get-tuple-element.76.refs_0_, f32[16,8,128]{2,1,0:T(8,128)} %get-tuple-element.77.refs_1_), custom_call_target="tpu_custom_call" | custom-call | tf_op jit(solution)/shard_map/reduce_pieces/pallas_call | solution.py:655
  303.2 0.7 fusion.38
  303.9 2.0 add_convert_fusion
  306.5 10.9 %gather_pieces.1.scalar_ref = f32[16,8,128]{2,1,0:T(8,128)} custom-call(f32[8,128]{1,0:T(8,128)} %fusion.30.refs_0_), custom_call_target="tpu_custom_call" | custom-call | tf_op jit(solution)/shard_map/gather_pieces/pallas_call | solution.py:559
  317.3 31.9 %backward_block.2 = (bf16[16,64,1792]{2,1,0:T(8,128)(2,1)}, bf16[8,192,640]{2,1,0:T(8,128)(2,1)}, f32[16,256]{1,0:T(8,128)}) custom-call(bf16[1024,1536]{1,0:T(8,128)(2,1)} %bitcast.143, f32[16,8,128]{2,1,0:T(8,128)} %gather_pieces.1.scalar_ref, bf16[1024,1536]{1,0:T(8,128)(2,1)} %bitcast.131, bf16[1536,640]{1,0:T(8,128)(2,1)} %bitcast.135, ...), custom_call_target="tpu_custom_call" | custom-call | tf_op jit(solution)/shard_map/backward_block/pallas_call | solution.py:1156
  349.2 57.6 %turn_backward.2 = (f32[64,1536]{1,0:T(8,128)}, f32[1,1536]{1,0:T(1,128)}, bf16[64,1536]{1,0:T(8,128)(2,1)}, bf16[16,64,1792]{2,1,0:T(8,128)(2,1)}, f32[16,8,128]{2,1,0:T(8,128)}) custom-call(bf16[16,64,1792]{2,1,0:T(8,128)(2,1)} %get-tuple-element.86.both_ref, bf16[64,1536]{1,0:T(8,128)(2,1)} %dynamic-slice_bitcast_fusion.1.refs_0_.grad_ref, ...), custom_call_target="tpu_custom_call" | custom-call | tf_op jit(solution)/shard_map/turn_backward/pallas_call | solution.py:1612
  406.8 32.1 %backward_block.3 = (bf16[16,64,1792]{2,1,0:T(8,128)(2,1)}, bf16[8,192,640]{2,1,0:T(8,128)(2,1)}, f32[16,256]{1,0:T(8,128)}) custom-call(bf16[1024,1792]{1,0:T(8,128)(2,1)} %bitcast.140, f32[16,8,128]{2,1,0:T(8,128)} %get-tuple-element.91.scalar_ref, bf16[1024,1536]{1,0:T(8,128)(2,1)} %bitcast.127, bf16[1536,640]{1,0:T(8,128)(2,1)} %bitcast.125, ...), custom_call_target="tpu_custom_call" | custom-call | tf_op jit(solution)/shard_map/backward_block/pallas_call | solution.py:1156
  438.9 1.3 slice_bitcast_fusion.15.scalar_ref
  440.2 44.3 %turn_backward.3 = (f32[64,1536]{1,0:T(8,128)}, f32[1,1536]{1,0:T(1,128)}, bf16[64,1536]{1,0:T(8,128)(2,1)}, bf16[16,64,256]{2,1,0:T(8,128)(2,1)}) custom-call(bf16[16,64,1792]{2,1,0:T(8,128)(2,1)} %get-tuple-element.100.both_ref, f32[64,1536]{1,0:T(8,128)} %get-tuple-element.101.grad_ref, bf16[64,1536]{1,0:T(8,128)(2,1)} %copy-done.2, ...), custom_call_target="tpu_custom_call" | custom-call | tf_op jit(solution)/shard_map/turn_backward/pallas_call | solution.py:1612
  484.5 0.7 pad_maximum_fusion.3
  485.2 0.7 maximum_maximum_fusion.sums_ref
  485.9 1.8 fusion.9
  487.7 1.8 fusion.8
  489.5 0.7 pad_maximum_fusion.1.shared_ref
  490.2 34.1 %scatter_grads.2 = (bf16[4,192,640]{2,1,0:T(8,128)(2,1)}, f32[192,256]{1,0:T(8,128)}) custom-call(bf16[8,192,640]{2,1,0:T(8,128)(2,1)} %get-tuple-element.108.grads_ref, bf16[2,192,256]{2,1,0:T(8,128)(2,1)} %pad_maximum_fusion.1.shared_ref), custom_call_target="tpu_custom_call" | custom-call | tf_op jit(solution)/shard_map/scatter_grads/pallas_call | solution.py:716
  524.4 1.8 fusion.10
  526.2 1.8 fusion.11
  528.1 0.7 pad_maximum_fusion.2.shared_ref
  528.8 34.0 %scatter_grads.3 = (bf16[4,192,640]{2,1,0:T(8,128)(2,1)}, f32[192,256]{1,0:T(8,128)}) custom-call(bf16[8,192,640]{2,1,0:T(8,128)(2,1)} %get-tuple-element.111.grads_ref, bf16[2,192,256]{2,1,0:T(8,128)(2,1)} %pad_maximum_fusion.2.shared_ref), custom_call_target="tpu_custom_call" | custom-call | tf_op jit(solution)/shard_map/scatter_grads/pallas_call | solution.py:716
  562.8 1.7 pad_maximum_fusion
  564.5 1.1 convert_bitcast_fusion
  565.6 0.9 copy.67
  566.5 24.9 %finish.1 = (f32[4,48,256]{2,1,0:T(8,128)}, f32[48,256]{1,0:T(8,128)}, bf16[4,64,1536]{2,1,0:T(8,128)(2,1)}, bf16[4,64,1536]{2,1,0:T(8,128)(2,1)}) custom-call(f32[48,256]{1,0:T(8,128)} %maximum_maximum_fusion.sums_ref, bf16[64,1536]{1,0:T(8,128)(2,1)} %get-tuple-element.177.hidden_ref, bf16[64,1536]{1,0:T(8,128)(2,1)} %get-tuple-element.104.grad_ref), custom_call_target="tpu_custom_call" | custom-call | tf_op jit(solution)/shard_map/finish/pallas_call | solution.py:1766
  591.5 0.7 slice.134
  592.2 0.7 slice_bitcast_fusion.11
  594.7 0.9 slice_bitcast_fusion.8
  597.1 0.7 slice_reduce_fusion
  599.5 0.8 slice_bitcast_fusion
  600.3 2.2 copy.69
  602.4 3.2 reshape.182
  605.7 2.2 copy.66
  607.8 3.0 reshape.179
  610.9 1.0 copy.65
  611.9 2.0 reshape.178
  614.0 0.9 copy.86
  614.8 0.9 copy.87
  (75 shorter events, 11.4 us)
Async XLA Ops:
  0.6 16.9 %copy-start.6 = (bf16[2,192,768]{2,1,0:T(8,128)(2,1)S(1)}, bf16[2,192,768]{2,1,0:T(8,128)(2,1)}, u32[]{:S(2)}) copy-start(bf16[2,192,768]{2,1,0:T(8,128)(2,1)} %param.21) | copy-start | bytes 1769476
  16.7 1.7 copy-start.2
  17.6 1.1 copy-start.7
  271.2 32.7 %copy-start.3 = (f32[64,1536]{1,0:T(8,128)S(1)}, f32[64,1536]{1,0:T(8,128)}, u32[]{:S(2)}) copy-start(f32[64,1536]{1,0:T(8,128)} %get-tuple-element.87.hidden_ref) | copy-start | bytes 1179652
  440.2 44.3 %copy-start.11 = (f32[1,1536]{1,0:T(1,128)S(1)}, f32[1,1536]{1,0:T(1,128)}, u32[]{:S(2)}) copy-start(f32[1,1536]{1,0:T(1,128)} %get-tuple-element.103) | copy-start | bytes 18436
  440.2 45.0 %copy-start.9 = (f32[16,256]{1,0:T(8,128)S(1)}, f32[16,256]{1,0:T(8,128)}, u32[]{:S(2)}) copy-start(f32[16,256]{1,0:T(8,128)} %get-tuple-element.99) | copy-start | bytes 49156
  440.2 45.0 %copy-start.10 = (f32[16,256]{1,0:T(8,128)S(1)}, f32[16,256]{1,0:T(8,128)}, u32[]{:S(2)}) copy-start(f32[16,256]{1,0:T(8,128)} %get-tuple-element.98) | copy-start | bytes 49156
  526.2 36.5 %copy-start.8 = (f32[192,256]{1,0:T(8,128)S(1)}, f32[192,256]{1,0:T(8,128)}, u32[]{:S(2)}) copy-start(f32[192,256]{1,0:T(8,128)} %get-tuple-element.113) | copy-start | bytes 589828
  528.1 36.4 %copy-start = (bf16[4,192,640]{2,1,0:T(8,128)(2,1)S(1)}, bf16[4,192,640]{2,1,0:T(8,128)(2,1)}, u32[]{:S(2)}) copy-start(bf16[4,192,640]{2,1,0:T(8,128)(2,1)} %get-tuple-element.110) | copy-start | bytes 2949124
  565.6 33.7 %copy-start.1 = (bf16[4,192,640]{2,1,0:T(8,128)(2,1)S(1)}, bf16[4,192,640]{2,1,0:T(8,128)(2,1)}, u32[]{:S(2)}) copy-start(bf16[4,192,640]{2,1,0:T(8,128)(2,1)} %get-tuple-element.112) | copy-start | bytes 2949124
  611.9 2.1 copy-start.5
  611.9 2.9 copy-start.4

commit v2 on v1

--- a/solution.py
+++ b/solution.py
@@ -494,244 +494,6 @@
     return lax.rem(t + 2, 4)
 
 
-def gather_body(count, depth, pieces, fulls, send_sem, recv_sem):
-    z = lax.axis_index("ctx")
-    t = lax.axis_index("tp")
-    core, chip = {"tp": other_core(t)}, {"tp": other_chip(t)}
-    started = []
-
-    def send(a, source, slot, kind, peer):
-        copy = remote(source, fulls[a].at[slot], send_sem.at[a, kind], recv_sem.at[a, slot], peer)
-        copy.start()
-        started.append(copy)
-
-    def arrived(a, slot):
-        remote(
-            fulls[a].at[slot], fulls[a].at[slot], send_sem.at[a, 0], recv_sem.at[a, slot], core
-        ).wait_recv()
-
-    mine = z * 4 + t
-    for a in range(count):
-        for hop in range(1, depth):
-            send(a, pieces[a], mine, hop, {"ctx": lax.rem(z + hop, depth)})
-        send(a, pieces[a], mine, depth, chip)
-        send(a, pieces[a], mine, depth + 1, core)
-        fulls[a][mine] = pieces[a][...]
-    kind = depth + 2
-    for hop in range(1, depth):
-        slot = lax.rem(z + hop, depth) * 4 + t
-        for a in range(count):
-            arrived(a, slot)
-            send(a, fulls[a].at[slot], slot, kind, chip)
-            send(a, fulls[a].at[slot], slot, kind + 1, core)
-        kind += 2
-    for hop in range(depth):
-        slot = lax.rem(z + hop, depth) * 4 + other_chip(t)
-        for a in range(count):
-            arrived(a, slot)
-            send(a, fulls[a].at[slot], slot, kind, core)
-        kind += 1
-    for hop in range(depth):
-        for row in (other_core(t), other_chip(other_core(t))):
-            for a in range(count):
-                arrived(a, lax.rem(z + hop, depth) * 4 + row)
-    for copy in started:
-        copy.wait_send()
-
-
-def gather_peers(depth):
-    z = lax.axis_index("ctx")
-    t = lax.axis_index("tp")
-    return [{"ctx": lax.rem(z + hop, depth)} for hop in range(1, depth)] + [
-        {"tp": other_chip(t)},
-        {"tp": other_core(t)},
-    ]
-
-
-def gather_kernel(count, depth, *refs):
-    greet(gather_peers(depth))
-    gather_body(count, depth, refs[:count], refs[count : 2 * count], *refs[2 * count :])
-
-
-def gather_pieces(pieces, depth, collective_id):
-    count = len(pieces)
-    slots = depth * 4
-    return pl.pallas_call(
-        partial(gather_kernel, count, depth),
-        out_shape=[jax.ShapeDtypeStruct((slots,) + p.shape, p.dtype) for p in pieces],
-        in_specs=[VMEM_SPEC] * count,
-        out_specs=[VMEM_SPEC] * count,
-        scratch_shapes=[
-            pltpu.SemaphoreType.DMA((count, 4 * depth)),
-            pltpu.SemaphoreType.DMA((count, slots)),
-        ],
-        compiler_params=params_of(collective_id),
-        name="gather_pieces",
-    )(*pieces)
-
-
-def reduce_body(count, depth, parts, outs, bufs, send_sem, recv_sem):
-    z = lax.axis_index("ctx")
-    t = lax.axis_index("tp")
-    core, chip = {"tp": other_core(t)}, {"tp": other_chip(t)}
-    started = []
-    hops = list(range(1, depth)) + [0]
-
-    def send(a, source, target, kind, peer):
-        copy = remote(source, target, send_sem.at[a, kind], recv_sem.at[a, kind], peer)
-        copy.start()
-        started.append(copy)
-
-    def arrived(a, ref, kind):
-        remote(ref, ref, send_sem.at[a, kind], recv_sem.at[a, kind], core).wait_recv()
-
-    for place, hop in enumerate(hops):
-        far = lax.rem(z + hop, depth)
-        for which, row in enumerate((other_chip(other_core(t)), other_core(t))):
-            kind = place * 2 + which
-            for a in range(count):
-                send(a, parts[a].at[far * 4 + row], bufs[a].at[kind], kind, core)
-    for place, hop in enumerate(hops):
-        far = lax.rem(z + hop, depth)
-        kind = place * 2
-        for a in range(count):
-            buf = bufs[a]
-            arrived(a, buf.at[kind], kind)
-            total = parts[a][far * 4 + other_chip(t)].astype(jnp.float32) + buf[kind].astype(
-                jnp.float32
-            )
-            buf[kind] = total.astype(buf.dtype)
-            send(a, buf.at[kind], buf.at[2 * depth + place], 2 * depth + place, chip)
-    for place, hop in enumerate(hops):
-        far = lax.rem(z + hop, depth)
-        kind = place * 2 + 1
-        for a in range(count):
-            buf = bufs[a]
-            arrived(a, buf.at[kind], kind)
-            arrived(a, buf.at[2 * depth + place], 2 * depth + place)
-            total = (
-                parts[a][far * 4 + t].astype(jnp.float32)
-                + buf[kind].astype(jnp.float32)
-                + buf[2 * depth + place].astype(jnp.float32)
-            )
-            if hop:
-                buf[kind] = total.astype(buf.dtype)
-                target = 3 * depth + (depth - hop)
-                copy = remote(
-                    buf.at[kind],
-                    buf.at[target],
-                    send_sem.at[a, 3 * depth + hop],
-                    recv_sem.at[a, target],
-                    {"ctx": far},
-                )
-                copy.start()
-                started.append(copy)
-            else:
-                outs[a][...] = total
-    for hop in range(1, depth):
-        for a in range(count):
-            buf = bufs[a]
-            target = 3 * depth + hop
-            arrived(a, buf.at[target], target)
-            outs[a][...] += buf[target].astype(jnp.float32)
-    for copy in started:
-        copy.wait_send()
-
-
-def reduce_kernel(count, depth, *refs):
-    greet(gather_peers(depth))
-    reduce_body(
-        count,
-        depth,
-        refs[:count],
-        refs[count : 2 * count],
-        refs[2 * count : 3 * count],
-        *refs[3 * count :],
-    )
-
-
-def reduce_pieces(parts, depth, collective_id):
-    count = len(parts)
-    return pl.pallas_call(
-        partial(reduce_kernel, count, depth),
-        out_shape=[jax.ShapeDtypeStruct(p.shape[1:], jnp.float32) for p in parts],
-        in_specs=[VMEM_SPEC] * count,
-        out_specs=[VMEM_SPEC] * count,
-        scratch_shapes=[pltpu.VMEM((4 * depth,) + p.shape[1:], p.dtype) for p in parts]
-        + [
-            pltpu.SemaphoreType.DMA((count, 4 * depth)),
-            pltpu.SemaphoreType.DMA((count, 4 * depth)),
-        ],
-        compiler_params=params_of(collective_id),
-        name="reduce_pieces",
-    )(*parts)
-
-
-def scatter_kernel(depth, grads_ref, shared_ref, out_ref, shared_out, x_buf, x_shared, send_sem, recv_sem):
-    x = lax.axis_index("dp")
-    z = lax.axis_index("ctx")
-    far_x = {"dp": 1 - x}
-    greet([{"ctx": lax.rem(z + hop, depth)} for hop in range(1, depth)] + [far_x])
-    started = []
-
-    def send(source, target, kind, recv, peer):
-        copy = remote(source, target, send_sem.at[kind], recv_sem.at[recv], peer)
-        copy.start()
-        started.append(copy)
-
-    def arrived(ref, recv):
-        remote(ref, ref, send_sem.at[recv], recv_sem.at[recv], far_x).wait_recv()
-
-    hops = list(range(1, depth)) + [0]
-    for place, hop in enumerate(hops):
-        far = lax.rem(z + hop, depth)
-        send(grads_ref.at[(1 - x) * depth + far], x_buf.at[place], place, place, far_x)
-    send(shared_ref.at[1 - x], x_shared, depth, depth, far_x)
-    for place, hop in enumerate(hops):
-        far = lax.rem(z + hop, depth)
-        arrived(x_buf.at[place], place)
-        total = grads_ref[x * depth + far].astype(jnp.float32) + x_buf[place].astype(jnp.float32)
-        if hop:
-            x_buf[place] = total.astype(x_buf.dtype)
-            copy = remote(
-                x_buf.at[place],
-                out_ref.at[z],
-                send_sem.at[depth + hop],
-                recv_sem.at[depth + depth - hop],
-                {"ctx": far},
-            )
-            copy.start()
-            started.append(copy)
-        else:
-            out_ref[z] = total.astype(out_ref.dtype)
-    arrived(x_shared, depth)
-    shared_out[...] = shared_ref[x].astype(jnp.float32) + x_shared[...].astype(jnp.float32)
-    for hop in range(1, depth):
-        arrived(out_ref.at[lax.rem(z + hop, depth)], depth + hop)
-    for copy in started:
-        copy.wait_send()
-
-
-def scatter_grads(grads, shared, depth, collective_id):
-    return pl.pallas_call(
-        partial(scatter_kernel, depth),
-        out_shape=[
-            jax.ShapeDtypeStruct((depth,) + grads.shape[1:], grads.dtype),
-            jax.ShapeDtypeStruct(shared.shape[1:], jnp.float32),
-        ],
-        in_specs=[VMEM_SPEC] * 2,
-        out_specs=[VMEM_SPEC] * 2,
-        scratch_shapes=[
-            pltpu.VMEM((depth,) + grads.shape[1:], grads.dtype),
-            pltpu.VMEM(shared.shape[1:], shared.dtype),
-            pltpu.SemaphoreType.DMA((2 * depth,)),
-            pltpu.SemaphoreType.DMA((2 * depth,)),
-        ],
-        compiler_params=params_of(collective_id),
-        name="scatter_grads",
-    )(grads, shared)
-
-
 def mxu(left, right, left_dim, right_dim, precision=None):
     return lax.dot_general(
         left,
@@ -839,8 +601,9 @@
     return high, (array - high.astype(jnp.float32)).astype(LOW)
 
 
-def forward_kernel(
+def forward_body(
     precise,
+    plan,
     normed_ref,
     wall_ref,
     bcw_ref,
@@ -887,6 +650,7 @@
             own_values = terms.of_head(terms.values, head)
             for term in two_parts(weights) if precise else (weights.astype(LOW),):
                 mixed += mxu(term, own_values, 1, 0)
+            plan(block, head)
         state_ref[block] = state
         if block:
             for term in two_parts(state) if precise else (state.astype(LOW),):
@@ -897,70 +661,56 @@
         mixed_ref[rows, :] = mixed
         gated = mixed * gate_pre * sigmoid(gate_pre)
         squares = gated * gated
+        for at in range(0, BLOCK, 128):
+            row = (start + at) // 128
+            squares_ref[row : row + 1, :] = mxu(
+                jnp.ones((8, width), jnp.float32), squares[at : at + 128], 1, 1, exact
+            )[0:1]
         if precise:
             part_ref[rows, :] = gated
-            for at in range(0, BLOCK, 128):
-                row = (start + at) // 128
-                squares_ref[row : row + 1, :] = mxu(
-                    jnp.ones((8, width), jnp.float32), squares[at : at + 128], 1, 1, exact
-                )[0:1]
+            plan(block, 3)
             continue
-        for at in range(0, BLOCK, piece):
-            slot = (start + at) // piece
-            squares_ref[slot, :, 0:piece] = mxu(
-                jnp.ones((8, width), jnp.float32), squares[at : at + piece], 1, 1, exact
-            )
         moved = mxu((gated * gains).astype(LOW), shift, 1, 0).astype(LOW)
         part = mxu(moved, wall_ref[:, OUT_AT : OUT_AT + 256], 1, 1).astype(LOW)
         for at in range(0, BLOCK, piece):
             part_ref[(start + at) // piece] = part[at : at + piece]
+        plan(block, 3)
 
 
 def local_params():
     return pltpu.CompilerParams(vmem_limit_bytes=60 << 20)
 
 
-def split_forward(normed, wall, bcw, small, segr, segc, slots, precise):
+def forward_shapes(normed, bcw, slots, precise):
     tokens, model_width = normed.shape
-    piece = tokens // slots
     width = INNER // slots
     bc_width = bcw.shape[1]
     f32 = jnp.float32
     if precise:
-        first = [
-            jax.ShapeDtypeStruct((tokens, width), f32),
-            jax.ShapeDtypeStruct((tokens // 128, 128), f32),
-        ]
+        first = jax.ShapeDtypeStruct((tokens, width), f32)
     else:
-        first = [
-            jax.ShapeDtypeStruct((slots, piece, model_width), LOW),
-            jax.ShapeDtypeStruct((slots, 8, 128), f32),
-        ]
-    return pl.pallas_call(
-        partial(forward_kernel, precise),
-        out_shape=first
-        + [
-            jax.ShapeDtypeStruct((tokens, width), f32),
-            jax.ShapeDtypeStruct((tokens + 8, width), f32),
-            jax.ShapeDtypeStruct((tokens + 8, bc_width), f32),
-            jax.ShapeDtypeStruct((tokens, width), f32),
-            jax.ShapeDtypeStruct((tokens, width), f32),
-            jax.ShapeDtypeStruct((tokens // BLOCK, bc_width // 2, width), f32),
-        ],
-        in_specs=[VMEM_SPEC] * 6,
-        out_specs=[VMEM_SPEC] * 8,
-        compiler_params=local_params(),
-        name="forward_block",
-    )(normed, wall, bcw, small, segr, segc)
+        first = jax.ShapeDtypeStruct((slots, tokens // slots, model_width), LOW)
+    return [
+        first,
+        jax.ShapeDtypeStruct((tokens // 128, 128), f32),
+        jax.ShapeDtypeStruct((tokens, width), f32),
+        jax.ShapeDtypeStruct((tokens + 8, width), f32),
+        jax.ShapeDtypeStruct((tokens + 8, bc_width), f32),
+        jax.ShapeDtypeStruct((tokens, width), f32),
+        jax.ShapeDtypeStruct((tokens, width), f32),
+        jax.ShapeDtypeStruct((tokens // BLOCK, bc_width // 2, width), f32),
+    ]
 
 
 def row_sum(array):
     return jnp.sum(array, axis=0, keepdims=True)
 
 
-def backward_kernel(
+def backward_body(
+    plan,
     grad_ref,
-    scalar_ref,
+    inv_ref,
+    inner_ref,
     normed_ref,
     wall_ref,
     small_ref,
@@ -973,12 +723,14 @@
     mixed_ref,
     state_ref,
     both_ref,
-    grads_ref,
+    early_ref,
+    late_ref,
     sums_ref,
     pre_ref,
     scaled_ref,
     e_ref,
     e_bc_ref,
+    grad_mixed_ref,
 ):
     tokens, model_width = normed_ref.shape
     width = gate_ref.shape[1]
@@ -992,7 +744,7 @@
     e_ref[tokens:, :] = jnp.zeros((8, width), f32)
     e_bc_ref[tokens:, :] = jnp.zeros((8, bc_width), f32)
     pre_ref[...] = jnp.zeros(pre_ref.shape, LOW)
-    eye = ones_where(iota((piece, 128), 0) == iota((piece, 128), 1), f32)
+    inv_columns, inner_columns = spread_rows(inv_ref[...]), spread_rows(inner_ref[...])
     same_head = ones_where(
         iota((width, width), 0) // HEADDIM == iota((width, width), 1) // HEADDIM, f32
     )
@@ -1009,19 +761,13 @@
     def add(name, term):
         sums[name] = sums[name] + term if name in sums else term
 
-    for block in reversed(range(blocks)):
+    for block in range(blocks):
         start = block * BLOCK
         rows = pl.ds(start, BLOCK)
-        step_in = step_ref[rows, :]
-        terms = BlockTerms(start, segc_ref, segr_ref, small_ref, value_ref, bc_ref, step_in, width)
-        columns = jnp.concatenate(
-            [
-                mxu(eye, scalar_ref[(start + at) // piece], 1, 1, exact)
-                for at in range(0, BLOCK, piece)
-            ],
-            axis=0,
+        inv, inner = (
+            jnp.concatenate([c[:, at : at + 1] for at in range(start // 128, (start + BLOCK) // 128)], axis=0)
+            for c in (inv_columns, inner_columns)
         )
-        inv, inner = columns[:, 0:1], columns[:, 1:2]
         grad_low = grad_ref[rows, 0:model_width]
         grad_scaled = mxu(grad_low, wall_ref[:, OUT_AT : OUT_AT + 256], 1, 0)
         grad_scaled = pltpu.roll(grad_scaled, 192, 1)[:, :width]
@@ -1035,7 +781,31 @@
         grad_gated = inv * (grad_scaled * gains) - gated * (inv * inv * inner)
         grad_gate = grad_gated * mixed * sig * (1.0 + gate_pre * (1.0 - sig))
         pre_ref[rows, 0:width] = grad_gate.astype(LOW)
-        grad_mixed = grad_gated * act
+        grad_mixed_ref[rows, :] = grad_gated * act
+    plan(-1, 0)
+    k_rows = early_ref.shape[1]
+
+    def by_slices(pair):
+        lanes = pl.ds(pair * 2 * k_rows, 2 * k_rows)
+        return lanes, ((2 * pair + at, slice(at * k_rows, (at + 1) * k_rows)) for at in range(2))
+
+    for pair in range(early_ref.shape[0] // 2):
+        lanes, slices = by_slices(pair)
+        total = mxu(normed_ref[:, lanes], pre_ref[:, 0:256], 0, 0)
+        out = mxu(grad_ref[:, lanes], scaled_ref[...], 0, 0)
+        for slot, k_slice in slices:
+            early_ref[slot, :, 0:OUT_AT] = total[k_slice, 0:OUT_AT].astype(LOW)
+            early_ref[slot, :, OUT_AT:256] = (
+                total[k_slice, OUT_AT:256] + out[k_slice, 0 : 256 - OUT_AT]
+            ).astype(LOW)
+            early_ref[slot, :, 256:VALUE_AT] = out[k_slice, 256 - OUT_AT :].astype(LOW)
+    plan(-1, 1)
+    for turn, block in enumerate(reversed(range(blocks))):
+        start = block * BLOCK
+        rows = pl.ds(start, BLOCK)
+        step_in = step_ref[rows, :]
+        terms = BlockTerms(start, segc_ref, segr_ref, small_ref, value_ref, bc_ref, step_in, width)
+        grad_mixed = grad_mixed_ref[rows, :]
         grad_mixed_low = grad_mixed.astype(LOW)
         values = terms.values.astype(f32)
         add("skip", row_sum(grad_mixed * values))
@@ -1059,6 +829,7 @@
             later = mxu(from_here, (unstepped * step_row).astype(LOW), 1, 0)
             later = jnp.where(terms.col < terms.row, later, 0.0)
             between += mxu(later.astype(LOW), head_ones, 1, 0)
+            plan(turn, head)
         pair_low = pair_sum.astype(LOW)
         grad_b = mxu(pair_low, terms.c_low, 0, 0)
         grad_c = mxu(pair_low, terms.b_low, 1, 0)
@@ -1117,20 +888,14 @@
             slot = (start + at) // piece
             both_ref[slot, :, 0:model_width] = part[at : at + piece]
             both_ref[slot, :, model_width:] = grad_bc[at : at + piece]
-
-    k_rows = grads_ref.shape[1]
-    for pair in range(grads_ref.shape[0] // 2):
-        lanes = pl.ds(pair * 2 * k_rows, 2 * k_rows)
-        total = mxu(normed_ref[:, lanes], pre_ref[...], 0, 0)
-        out = mxu(grad_ref[:, lanes], scaled_ref[...], 0, 0)
-        for at in range(2):
-            k_slice = slice(at * k_rows, (at + 1) * k_rows)
-            slot = 2 * pair + at
-            grads_ref[slot, :, 0:OUT_AT] = total[k_slice, 0:OUT_AT].astype(LOW)
-            grads_ref[slot, :, OUT_AT:VALUE_AT] = (
-                total[k_slice, OUT_AT:VALUE_AT] + out[k_slice]
-            ).astype(LOW)
-            grads_ref[slot, :, VALUE_AT:] = total[k_slice, VALUE_AT:].astype(LOW)
+        plan(turn, 3)
+
+    for pair in range(late_ref.shape[0] // 2):
+        lanes, slices = by_slices(pair)
+        total = mxu(normed_ref[:, lanes], pre_ref[:, VALUE_AT:], 0, 0)
+        for slot, k_slice in slices:
+            late_ref[slot] = total[k_slice].astype(LOW)
+        plan(blocks, pair)
 
     sums_ref[...] = jnp.zeros(sums_ref.shape, f32)
     head_sums = mxu(
@@ -1147,35 +912,25 @@
     sums_ref[13:14, :] = sums["bc_bias"]
 
 
-def split_backward(grad, scalars, normed, wall, small, segr, segc, kept, slots):
+def backward_shapes(normed, kept, slots):
     tokens, model_width = normed.shape
-    piece = tokens // slots
     width = kept[0].shape[1]
     bc_width = kept[2].shape[1]
     k_slots = slots // 2
-    return pl.pallas_call(
-        backward_kernel,
-        out_shape=[
-            jax.ShapeDtypeStruct((slots, piece, model_width + bc_width), LOW),
-            jax.ShapeDtypeStruct((k_slots, model_width // k_slots, PACK), LOW),
-            jax.ShapeDtypeStruct((16, 256), jnp.float32),
-        ],
-        in_specs=[VMEM_SPEC] * 13,
-        out_specs=[VMEM_SPEC] * 3,
-        scratch_shapes=[
-            pltpu.VMEM((tokens, PACK), LOW),
-            pltpu.VMEM((tokens, 256), LOW),
-            pltpu.VMEM((tokens + 8, width), jnp.float32),
-            pltpu.VMEM((tokens + 8, bc_width), jnp.float32),
-        ],
-        compiler_params=local_params(),
-        name="backward_block",
-    )(grad, scalars, normed, wall, small, segr, segc, *kept)
-
-
-def lane_rows(columns, slots):
-    rows = jnp.stack([c.reshape(slots, -1) for c in columns], axis=1)
-    return jnp.pad(rows, ((0, 0), (0, 8 - rows.shape[1]), (0, 128 - rows.shape[2])))
+    shapes = [
+        jax.ShapeDtypeStruct((slots, tokens // slots, model_width + bc_width), LOW),
+        jax.ShapeDtypeStruct((k_slots, model_width // k_slots, VALUE_AT), LOW),
+        jax.ShapeDtypeStruct((k_slots, model_width // k_slots, PACK - VALUE_AT), LOW),
+        jax.ShapeDtypeStruct((16, 256), jnp.float32),
+    ]
+    work = [
+        pltpu.VMEM((tokens, PACK), LOW),
+        pltpu.VMEM((tokens, 256), LOW),
+        pltpu.VMEM((tokens + 8, width), jnp.float32),
+        pltpu.VMEM((tokens + 8, bc_width), jnp.float32),
+        pltpu.VMEM((tokens, width), jnp.float32),
+    ]
+    return shapes, work
 
 
 def norm_rows(hidden, gain):
@@ -1287,7 +1042,6 @@
                 to_left = jnp.logical_and(far > z, z > 0)
                 to_right = jnp.logical_and(far < z, z < last)
                 pass_on(a, ref, slot, part, to_left, to_right)
-        yield
         slot = (order[place - 1] if place else z) * 4 + column
         for part in range(HALVES):
             for a in every:
@@ -1459,10 +1213,15 @@
     wall_ref,
     hidden_ref,
     gain_ref,
+    pack_ref,
+    early_ref,
+    bc_ref,
     hidden_out,
     total_out,
     inv_out,
     full_out,
+    full_pack,
+    full_bc,
     parts,
     normed,
     shared,
@@ -1473,13 +1232,25 @@
     reduce_recv,
     gather_send,
     gather_recv,
+    pack_send,
+    pack_recv,
+    bc_send,
+    bc_recv,
 ):
     links = Links(depth)
-    greet(everyone(depth))
+    greet(everyone(depth) + [links.far_x])
     width = gated_ref.shape[1]
-    piece = hidden_ref.shape[0]
+    piece = hidden_ref.shape[1] // 4
     block = 4 * piece
-    run_tasks(share_task(links, squares_ref, shared, share_send, share_recv))
+    share = share_task(links, squares_ref, shared, share_send, share_recv)
+    next(share, None)
+    weights = Weights(links, pack_ref, full_pack, pack_send, pack_recv)
+    here = [links.z, weights.order[0], weights.order[1]]
+    for far in here:
+        full_pack[weights.base + far] = early_ref[weights.base + far]
+    other = (1 - links.x) * depth + links.z
+    full_pack[other] = early_ref[other]
+    run_tasks(share)
     total = shared[0]
     for slot in range(1, 4 * depth):
         total = total + shared[slot]
@@ -1502,19 +1273,34 @@
         for row in range(4):
             parts[far * 4 + row] = part[row * piece : (row + 1) * piece].astype(parts.dtype)
 
+    def background():
+        weights.over(0, False)
+        yield
+        weights.along(2)
+        yield
+        weights.over(1, False)
+        yield
+        yield
+        weights.over(2)
+
+    shared_bc = shared_task(links, bc_ref.at[1], full_bc, bc_send, bc_recv)
     run_tasks(
-        reduce_task(links, produce, [parts], [total_out], [bufs], reduce_send, reduce_recv)
-    )
-    hidden = hidden_ref[...].astype(jnp.float32) + total_out[...]
+        reduce_task(links, produce, [parts], [total_out], [bufs], reduce_send, reduce_recv),
+        background(),
+        shared_bc,
+    )
+    rows = pl.ds(pl.multiple_of(links.t * piece, piece), piece)
+    hidden = hidden_ref[0, rows, :].astype(jnp.float32) + total_out[...]
     hidden_out[...] = hidden
-    inv = lax.rsqrt(jnp.mean(hidden * hidden, axis=1, keepdims=True) + epsilon)
-    normed[...] = (hidden * inv * gain_ref[...]).astype(LOW)
+    _, normed[...] = norm_rows(hidden, gain_ref[...].astype(jnp.float32)[1:2])
     run_tasks(gather_task(links, [normed], [full_out], gather_send, gather_recv))
+    for far in weights.order:
+        weights.over_landed(far)
     links.finish()
 
 
-def turn_forward(gated, squares, small, wall, hidden, gain, depth, collective_id):
-    piece, model_width = hidden.shape
+def turn_forward(gated, squares, small, wall, hidden, gain, pack, early, bc, depth, collective_id):
+    piece, model_width = hidden.shape[1] // 4, hidden.shape[2]
     slots = 4 * depth
     f32 = jnp.float32
     return pl.pallas_call(
@@ -1524,9 +1310,10 @@
             jax.ShapeDtypeStruct((piece, model_width), f32),
             jax.ShapeDtypeStruct(squares.shape, f32),
             jax.ShapeDtypeStruct((slots, piece, model_width), LOW),
-        ],
-        in_specs=[VMEM_SPEC] * 6,
-        out_specs=[VMEM_SPEC] * 4,
+        ]
+        + pack_shapes(depth, pack.shape[1], bc.shape[2]),
+        in_specs=[VMEM_SPEC] * 9,
+        out_specs=[VMEM_SPEC] * 6,
         scratch_shapes=[
             pltpu.VMEM((slots, piece, model_width), f32),
             pltpu.VMEM((piece, model_width), LOW),
@@ -1535,256 +1322,1082 @@
             pltpu.SemaphoreType.DMA((slots,)),
         ]
         + reduce_scratch([(piece, model_width)], [f32], depth)
-        + gather_sems(1, slots),
+        + gather_sems(1, slots)
+        + weights_sems(depth)
+        + shared_sems(depth),
         compiler_params=params_of(collective_id),
         name="turn_forward",
-    )(gated, squares, small, wall, hidden, gain)
-
-
-def turn_backward_kernel(
+    )(gated, squares, small, wall, hidden, gain, pack, early, bc)
+
+
+def partners(links):
+    z = links.z
+    return [lax.rem(z + 2, 4), z + 1 - 2 * lax.rem(z, 2), 3 - z]
+
+
+class Weights:
+    def __init__(self, links, pack, full, send_sem, recv_sem):
+        self.links, self.pack, self.full = links, pack, full
+        self.send_sem, self.recv_sem = send_sem, recv_sem
+        self.order = partners(links)
+        self.base = links.x * links.depth
+        self.mine = self.base + links.z
+
+    def send(self, ref, slot, part, kind, peer):
+        self.links.send(
+            ref,
+            half(self.full.at[slot], part),
+            self.send_sem.at[kind, part],
+            self.recv_sem.at[slot, part],
+            peer,
+        )
+
+    def arrived(self, slot, part):
+        ref = half(self.full.at[slot], part)
+        self.links.wait(ref, self.send_sem.at[0, part], self.recv_sem.at[slot, part])
+        return ref
+
+    def keep(self):
+        self.full[self.mine] = self.pack[self.links.z]
+
+    def own_over(self):
+        for part in range(HALVES):
+            self.send(half(self.pack.at[self.links.z], part), self.mine, part, 0, self.links.far_x)
+
+    def along(self, place):
+        far = self.order[place]
+        for part in range(HALVES):
+            self.send(half(self.pack.at[far], part), self.mine, part, 1 + place, {"ctx": far})
+
+    def landed(self, place):
+        for part in range(HALVES):
+            self.arrived(self.base + self.order[place], part)
+
+    def over(self, place, wait=True):
+        slot = self.base + self.order[place]
+        for part in range(HALVES):
+            ref = self.arrived(slot, part) if wait else half(self.full.at[slot], part)
+            self.send(ref, slot, part, self.links.depth + place, self.links.far_x)
+
+    def own_over_landed(self):
+        self.over_landed(self.links.z)
+
+    def over_landed(self, far):
+        slot = (1 - self.links.x) * self.links.depth + far
+        for part in range(HALVES):
+            self.arrived(slot, part)
+
+    def task(self):
+        self.own_over()
+        self.keep()
+        yield
+        self.along(1)
+        yield
+        self.along(0)
+        yield
+        self.over(1)
+        yield
+        self.along(2)
+        self.over(0)
+        yield
+        self.over(2)
+        yield
+        for far in [self.links.z] + self.order:
+            self.over_landed(far)
+
+
+def weights_sems(depth):
+    return [
+        pltpu.SemaphoreType.DMA((2 * depth, HALVES)),
+        pltpu.SemaphoreType.DMA((2 * depth, HALVES)),
+    ]
+
+
+def shared_task(links, own, full, send_sem, recv_sem):
+    x, z, t, depth = links.x, links.z, links.t, links.depth
+    quarter = own.at[pl.ds(t * full.shape[2], full.shape[2])]
+    mine = x * depth + z
+
+    def send(ref, slot, column, kind, peer):
+        links.send(ref, full.at[slot, column], send_sem.at[slot, column, kind], recv_sem.at[slot, column], peer)
+
+    def arrived(slot, column):
+        ref = full.at[slot, column]
+        links.wait(ref, send_sem.at[slot, column, 0], recv_sem.at[slot, column])
+        return ref
+
+    order = partners(links)
+    for place, far in enumerate(order):
+        send(quarter, mine, t, place, {"ctx": far})
+    send(quarter, mine, t, 3, links.far_x)
+    full[mine] = own[...].reshape(full.shape[1:])
+    yield
+    for place in (1, 0, 2):
+        slot = x * depth + order[place]
+        ref = arrived(slot, t)
+        send(ref, slot, t, 3, links.far_x)
+        send(ref, slot, t, 4, links.chip)
+        send(ref, slot, t, 5, links.core)
+    yield
+    for far in [z] + order:
+        slot = (1 - x) * depth + far
+        ref = arrived(slot, t)
+        send(ref, slot, t, 4, links.chip)
+        send(ref, slot, t, 5, links.core)
+    others = [x * depth + far for far in order] + [(1 - x) * depth + far for far in [z] + order]
+    yield
+    for slot in others:
+        send(arrived(slot, other_chip(t)), slot, other_chip(t), 5, links.core)
+    yield
+    for slot in others:
+        for column in (other_core(t), other_chip(other_core(t))):
+            arrived(slot, column)
+
+
+def shared_sems(depth):
+    return [
+        pltpu.SemaphoreType.DMA((2 * depth, 4, 6)),
+        pltpu.SemaphoreType.DMA((2 * depth, 4)),
+    ]
+
+
+def scatter_task(links, grads, out, bufs, send_sem, recv_sem):
+    x, z, depth = links.x, links.z, links.depth
+    order = partners(links) + [z]
+
+    def rows_of(ref, part):
+        rows = ref.shape[0] // HALVES
+        return slice(part * rows, (part + 1) * rows)
+
+    def over(place):
+        for part in range(HALVES):
+            links.send(
+                half(grads.at[(1 - x) * depth + order[place]], part),
+                half(bufs.at[place], part),
+                send_sem.at[place, part],
+                recv_sem.at[place, part],
+                links.far_x,
+            )
+
+    over(0)
+    over(1)
+    yield
+    for place, far in enumerate(order):
+        for part in range(HALVES):
+            ref = half(bufs.at[place], part)
+            links.wait(ref, send_sem.at[place, part], recv_sem.at[place, part])
+            rows = rows_of(out.at[0], part)
+            total = grads[x * depth + far, rows, :].astype(jnp.float32) + bufs[place, rows, :].astype(
+                jnp.float32
+            )
+            if place < 3:
+                bufs[place, rows, :] = total.astype(LOW)
+                links.send(
+                    ref,
+                    half(out.at[z], part),
+                    send_sem.at[depth + place, part],
+                    recv_sem.at[depth + z, part],
+                    {"ctx": far},
+                )
+            else:
+                out[z, rows, :] = total.astype(LOW)
+        if place < 2:
+            over(place + 2)
+        yield
+    for far in order[:3]:
+        for part in range(HALVES):
+            links.wait(half(out.at[far], part), send_sem.at[0, part], recv_sem.at[depth + far, part])
+
+
+def scatter_scratch(shape, depth, keep=True):
+    return [pltpu.VMEM((depth,) + shape, LOW)] * (2 if keep else 1) + [
+        pltpu.SemaphoreType.DMA((2 * depth, HALVES)),
+        pltpu.SemaphoreType.DMA((2 * depth, HALVES)),
+    ]
+
+
+def placed(far, width, whole):
+    window, lane = iota((256, whole), 0), iota((256, whole), 1)
+    return ones_where(jnp.logical_and(lane == window + far * width, window < width), LOW)
+
+
+def unpack_early(early, width, layer, gate_out, proj_out):
+    take = ones_where(iota((256, width), 0) == iota((256, width), 1) + 64, LOW)
+    gate = 0.0
+    for far in range(early.shape[0]):
+        gate += mxu(early[far, :, 0:256], placed(far, width, gate_out.shape[2]), 1, 0)
+        proj_out[layer, far * width : (far + 1) * width, :] = mxu(
+            take, early[far, :, OUT_AT : OUT_AT + 256], 0, 1
+        )
+    gate_out[layer] = gate
+
+
+def bc_products(normed_ref, bc_low, slots_ref):
+    rows = slots_ref.shape[1]
+    for pair in range(slots_ref.shape[0] // 2):
+        total = mxu(normed_ref[:, pair * 2 * rows : (pair + 1) * 2 * rows], bc_low, 0, 0)
+        slots_ref[2 * pair] = total[:rows].astype(LOW)
+        slots_ref[2 * pair + 1] = total[rows:].astype(LOW)
+
+
+def bc_task(links, slots_ref, arrived_ref, out_ref, layer, send_sem, recv_sem):
+    x, z, depth = links.x, links.z, links.depth
+    links.send(slots_ref.at[(1 - x) * depth + z], arrived_ref, send_sem, recv_sem, links.far_x)
+    yield
+    links.wait(arrived_ref, send_sem, recv_sem)
+    out_ref[layer] = slots_ref[x * depth + z].astype(jnp.float32) + arrived_ref[...].astype(jnp.float32)
+
+
+def rows_task(links, ref, out, send_sem, recv_sem):
+    t = links.t
+    for way, peer in enumerate((links.chip, links.core)):
+        links.send(ref, out.at[t], send_sem.at[way], recv_sem.at[t], peer)
+    out[t] = ref[...]
+    yield
+    column = other_chip(t)
+    links.wait(out.at[column], send_sem.at[0], recv_sem.at[column])
+    links.send(out.at[column], out.at[column], send_sem.at[2], recv_sem.at[column], links.core)
+    yield
+    for column in (other_core(t), other_chip(other_core(t))):
+        links.wait(out.at[column], send_sem.at[0], recv_sem.at[column])
+
+
+ROWS_SEMS = [pltpu.SemaphoreType.DMA((3,)), pltpu.SemaphoreType.DMA((4,))]
+
+
+def sums_task(links, own, arrived_ref, work, by_z, sum_out, send_sem, recv_sem, channel_rows=9):
+    z, depth = links.z, links.depth
+    links.send(own, arrived_ref.at[0], send_sem.at[0], recv_sem.at[0], links.far_x)
+    yield
+    links.wait(arrived_ref.at[0], send_sem.at[0], recv_sem.at[0])
+    over_dp = own[...] + arrived_ref[0]
+    work[0] = over_dp
+    links.send(work.at[0], arrived_ref.at[1], send_sem.at[1], recv_sem.at[1], links.core)
+    yield
+    links.wait(arrived_ref.at[1], send_sem.at[1], recv_sem.at[1])
+    work[1] = work[0] + arrived_ref[1]
+    links.send(work.at[1], arrived_ref.at[2], send_sem.at[2], recv_sem.at[2], links.chip)
+    yield
+    links.wait(arrived_ref.at[2], send_sem.at[2], recv_sem.at[2])
+    row = iota(own.shape, 0)
+    kept = jnp.logical_and(row < 16 * LAYERS, lax.rem(row, 16) < channel_rows)
+    work[2] = jnp.where(kept, work[0], work[1] + arrived_ref[2])
+    for hop in range(1, depth):
+        links.send(
+            work.at[2], by_z.at[z], send_sem.at[2 + hop], recv_sem.at[3 + z], {"ctx": lax.rem(z + hop, depth)}
+        )
+    by_z[z] = work[2]
+    yield
+    for hop in range(1, depth):
+        far = lax.rem(z + hop, depth)
+        links.wait(by_z.at[far], send_sem.at[0], recv_sem.at[3 + far])
+    whole = by_z[0]
+    for far in range(1, depth):
+        whole = whole + by_z[far]
+    sum_out[...] = whole
+
+
+def sums_scratch(shape, depth):
+    return [
+        pltpu.VMEM((3,) + shape, jnp.float32),
+        pltpu.VMEM((3,) + shape, jnp.float32),
+        pltpu.SemaphoreType.DMA((3 + depth,)),
+        pltpu.SemaphoreType.DMA((3 + depth,)),
+    ]
+
+
+ANY_SPEC = pl.BlockSpec(memory_space=pl.ANY)
+
+
+class Fetch:
+    def __init__(self, sources, targets, sems):
+        self.copies = [
+            pltpu.make_async_copy(source, target, sems.at[at])
+            for at, (source, target) in enumerate(zip(sources, targets))
+        ]
+        self.waiting = set(range(len(self.copies)))
+        for copy in self.copies:
+            copy.start()
+
+    def wait(self, *which):
+        for at in which or range(len(self.copies)):
+            if at in self.waiting:
+                self.waiting.remove(at)
+                self.copies[at].wait()
+
+
+def build_pack(pack, gate, value, step, proj):
+    depth, rows, _ = pack.shape
+    width, heads = gate.shape[1] // depth, step.shape[1] // depth
+    shift = lane_shift(width)
+    blank = jnp.zeros((rows, 128), jnp.float32)
+    inside = iota((rows, 256), 1) < width
+
+    def own_lanes(ref, far):
+        at = far * width // 128 * 128
+        window = ref[:, at : at + 256].astype(jnp.float32)
+        if far * width > at:
+            window = pltpu.roll(window, 256 - (far * width - at), 1)
+        return jnp.where(inside, window, 0.0)
+
+    for far in range(depth):
+        gate_lanes, value_lanes = own_lanes(gate, far), own_lanes(value, far)
+        pack[far, :, 0:128] = gate_lanes[:, 0:128].astype(LOW)
+        out = mxu(proj[far * width : (far + 1) * width, :], shift, 0, 0)
+        pack[far, :, OUT_AT:VALUE_AT] = (
+            out + jnp.concatenate([gate_lanes[:, 128:256], blank], axis=1)
+        ).astype(LOW)
+        pack[far, :, VALUE_AT : VALUE_AT + 128] = value_lanes[:, 0:128].astype(LOW)
+        head = iota((depth * heads, 128), 0) - far * heads
+        chosen = jnp.logical_and(jnp.logical_and(head >= 0, head < heads), iota(head.shape, 1) == head + 64)
+        pack[far, :, VALUE_AT + 128 :] = (
+            value_lanes[:, 128:256] + mxu(step[...], ones_where(chosen, LOW), 1, 0)
+        ).astype(LOW)
+
+
+def raw_scratch(gate, step, proj):
+    return [pltpu.VMEM(a.shape[1:], LOW) for a in (gate, gate, step, proj)] + [pltpu.SemaphoreType.DMA((4,))]
+
+
+def prepare_kernel(
     depth,
-    last,
-    both_ref,
-    grad_ref,
     hidden_ref,
+    seg_ref,
     gain_ref,
-    bcw_ref,
-    total_ref,
-    scalar_ref,
-    grad_out,
-    gain_out,
-    low_out,
-    *refs,
+    gate_ref,
+    value_ref,
+    step_ref,
+    proj_ref,
+    bc_ref,
+    taps_ref,
+    tap_bias_ref,
+    out_gain_ref,
+    skip_ref,
+    step_bias_ref,
+    decay_ref,
+    bc_taps_ref,
+    bc_bias_ref,
+    full_out,
+    pack_out,
+    bc_out,
+    smalls_out,
+    segr_out,
+    segc_out,
+    normed,
+    seg_piece,
+    seg_full,
+    pack,
+    raw_gate,
+    raw_value,
+    raw_step,
+    raw_proj,
+    raw_sems,
+    gather_send,
+    gather_recv,
+    pack_send,
+    pack_recv,
+    bc_send,
+    bc_recv,
 ):
+    f32 = jnp.float32
+    links = Links(depth)
+    raw = (raw_gate, raw_value, raw_step, raw_proj)
+    fetch = Fetch([r.at[0] for r in (gate_ref, value_ref, step_ref, proj_ref)], raw, raw_sems)
+    piece, model_width = normed.shape
+    rows = pl.ds(pl.multiple_of(links.t * piece, piece), piece)
+    _, normed[...] = norm_rows(hidden_ref[0, rows, :].astype(f32), gain_ref[0:1, :].astype(f32))
+    tokens = seg_ref.shape[1]
+    lane, place = iota((tokens, 128), 0) - links.t * piece, iota((tokens, 128), 1)
+    pick = ones_where(jnp.logical_and(lane == place, place < piece), f32)
+    seg_piece[...] = mxu(jnp.broadcast_to(seg_ref[...].astype(f32), (8, tokens)), pick, 1, 0, exact)
+    greet(everyone(depth) + [links.far_x])
+    gather = gather_task(links, [normed, seg_piece], [full_out, seg_full], gather_send, gather_recv)
+    next(gather, None)
+    shared = shared_task(links, bc_ref.at[0], bc_out, bc_send, bc_recv)
+    fetch.wait()
+    build_pack(pack, *raw)
+    weights = Weights(links, pack, pack_out, pack_send, pack_recv)
+    weights.own_over()
+    weights.keep()
+    next(gather, None)
+    weights.along(1)
+    next(gather, None)
+    weights.along(0)
+    next(shared, None)
+    width = taps_ref.shape[2] // depth
+    lane, place = iota((taps_ref.shape[2], 256), 0) - links.z * width, iota((taps_ref.shape[2], 256), 1)
+    own = ones_where(jnp.logical_and(lane == place, place < width), f32)
+    heads = skip_ref.shape[1] // depth
+    head, place = iota((skip_ref.shape[1], 256), 0) - links.z * heads, iota((skip_ref.shape[1], 256), 1)
+    spread = ones_where(jnp.logical_and(head == place // HEADDIM, place < width), f32)
+    smalls_out[...] = jnp.zeros(smalls_out.shape, f32)
+    for layer in range(LAYERS):
+        one = slice(layer, layer + 1)
+        smalls_out[layer, 0:4, :] = mxu(taps_ref[layer].astype(f32), own, 1, 0, exact)
+        by_channel = jnp.concatenate(
+            [tap_bias_ref[...].astype(f32)[one], out_gain_ref[...].astype(f32)[one]] * 4, axis=0
+        )
+        smalls_out[layer, 4:6, :] = mxu(by_channel, own, 1, 0, exact)[0:2]
+        by_head = jnp.concatenate(
+            [skip_ref[one, :], step_bias_ref[one, :], -jnp.exp(decay_ref[one, :])] + [skip_ref[one, :]] * 5,
+            axis=0,
+        )
+        smalls_out[layer, 6:9, :] = mxu(by_head, spread, 1, 0, exact)[0:3]
+        smalls_out[layer, 9:13, :] = bc_taps_ref[layer].astype(f32)
+        smalls_out[layer, 13:14, :] = bc_bias_ref[...].astype(f32)[one]
+    next(gather, None)
+    weights.over(1)
+    weights.along(2)
+    next(gather, None)
+    weights.over(0)
+    next(gather, None)
+    per = 128 // piece
+    segc_out[...] = jnp.full(segc_out.shape, -1.0, f32)
+    for row in range(4 * depth // per):
+        lanes = iota((8, 128), 1)
+        total = jnp.zeros((8, 128), f32)
+        for at in range(per):
+            part = seg_full[row * per + at]
+            total = jnp.where(lanes // piece == at, pltpu.roll(part, at * piece, 1) if at else part, total)
+        segr_out[:, row * 128 : (row + 1) * 128] = total[0:1]
+        column = spread_rows(total)[:, 0:1]
+        segc_out[8 + row * 128 : 8 + (row + 1) * 128, :] = jnp.broadcast_to(column, (128, 256))
+    weights.over(2)
+    run_tasks(shared)
+    for far in [links.z] + weights.order:
+        weights.over_landed(far)
+    links.finish()
+
+
+def pack_shapes(depth, rows, bc_width):
+    return [
+        jax.ShapeDtypeStruct((2 * depth, rows, PACK), LOW),
+        jax.ShapeDtypeStruct((2 * depth, 4, rows // 4, bc_width), LOW),
+    ]
+
+
+def piece_shapes(pieces, depth):
+    return [jax.ShapeDtypeStruct((4 * depth,) + p.shape, p.dtype) for p in pieces]
+
+
+def prepare(hidden, segment, gain, gate, value, step, proj, bc, small, depth, collective_id):
+    f32 = jnp.float32
+    _, tokens, model_width = hidden.shape
+    piece, slots = tokens // 4, 4 * depth
+    rows = gate.shape[1]
+    shapes = [
+        jax.ShapeDtypeStruct((slots, piece, model_width), LOW),
+        *pack_shapes(depth, rows, bc.shape[2]),
+        jax.ShapeDtypeStruct((LAYERS, 16, 256), f32),
+        jax.ShapeDtypeStruct((1, depth * tokens), f32),
+        jax.ShapeDtypeStruct((depth * tokens + 16, 256), f32),
+    ]
+    return pl.pallas_call(
+        partial(prepare_kernel, depth),
+        out_shape=shapes,
+        in_specs=[VMEM_SPEC] * 3 + [ANY_SPEC] * 4 + [VMEM_SPEC] * (1 + len(small)),
+        out_specs=[VMEM_SPEC] * len(shapes),
+        scratch_shapes=[
+            pltpu.VMEM((piece, model_width), LOW),
+            pltpu.VMEM((8, 128), f32),
+            pltpu.VMEM((slots, 8, 128), f32),
+            pltpu.VMEM((depth, rows, PACK), LOW),
+        ]
+        + raw_scratch(gate, step, proj)
+        + gather_sems(2, slots)
+        + weights_sems(depth)
+        + shared_sems(depth),
+        compiler_params=params_of(collective_id),
+        name="prepare",
+    )(hidden, segment, gain, gate, value, step, proj, bc, *small)
+
+
+class SumStream:
+    def __init__(self, links, parts, out, bufs, send_sem, recv_sem, low=0, high=4):
+        self.links, self.parts, self.out, self.bufs = links, parts, out, bufs
+        self.send_sem, self.recv_sem = send_sem, recv_sem
+        self.receives = jnp.logical_and(links.z >= low, links.z < high)
+
+    def rows(self, part):
+        size = self.out.shape[0] // HALVES
+        return slice(part * size, (part + 1) * size)
+
+    def sems(self, at, part):
+        return self.send_sem.at[at, part], self.recv_sem.at[at, part]
+
+    def wait(self, at, part):
+        self.links.wait(half(self.bufs.at[at], part), *self.sems(at, part))
+
+    def loaded(self, at, part):
+        return self.bufs[at, self.rows(part), :].astype(jnp.float32)
+
+    def mine(self, slot, part):
+        return self.parts[slot, self.rows(part), :].astype(jnp.float32)
+
+    def first(self, far):
+        t = self.links.t
+        for which, row in enumerate((other_chip(other_core(t)), other_core(t))):
+            for part in range(HALVES):
+                at = far * 2 + which
+                self.links.send(
+                    half(self.parts.at[far * 4 + row], part),
+                    half(self.bufs.at[at], part),
+                    *self.sems(at, part),
+                    self.links.core,
+                )
+
+    def second(self, far):
+        at = far * 2
+        for part in range(HALVES):
+            self.wait(at, part)
+            total = self.mine(far * 4 + other_chip(self.links.t), part) + self.loaded(at, part)
+            self.bufs[at, self.rows(part), :] = total.astype(self.bufs.dtype)
+            self.links.send(
+                half(self.bufs.at[at], part),
+                half(self.bufs.at[8 + far], part),
+                *self.sems(8 + far, part),
+                self.links.chip,
+            )
+
+    def third(self, far):
+        at = far * 2 + 1
+        z = self.links.z
+        for part in range(HALVES):
+            self.wait(at, part)
+            self.wait(8 + far, part)
+            total = (
+                self.mine(far * 4 + self.links.t, part) + self.loaded(at, part) + self.loaded(8 + far, part)
+            )
+            rows = self.rows(part)
+
+            @pl.when(z == far)
+            def _(total=total, rows=rows):
+                self.out[rows, :] = total
+
+            @pl.when(z != far)
+            def _(total=total, rows=rows):
+                self.bufs[at, rows, :] = total.astype(self.bufs.dtype)
+
+            self.links.send(
+                half(self.bufs.at[at], part),
+                half(self.bufs.at[12 + z], part),
+                self.send_sem.at[12 + far, part],
+                self.recv_sem.at[12 + z, part],
+                {"ctx": far},
+                z != far,
+            )
+
+    def end(self):
+        @pl.when(self.receives)
+        def _():
+            for hop in range(1, self.links.depth):
+                far = lax.rem(self.links.z + hop, self.links.depth)
+                for part in range(HALVES):
+                    self.wait(12 + far, part)
+                    self.out[self.rows(part), :] += self.loaded(12 + far, part)
+
+
+def stream_scratch(shape, dtype):
+    return [
+        pltpu.VMEM((16,) + shape, dtype),
+        pltpu.SemaphoreType.DMA((16, HALVES)),
+        pltpu.SemaphoreType.DMA((16, HALVES)),
+    ]
+
+
+class Plan:
+    def __init__(self, calls):
+        self.calls = calls
+
+    def __call__(self, turn, point):
+        for call in self.calls.get((turn, point), ()):
+            call()
+
+
+def advance(task):
+    def step():
+        next(task, None)
+
+    return step
+
+
+def forward_first_kernel(depth, *refs):
+    compute, weights_in, results, (pack, full_pack) = refs[:6], refs[6:10], refs[10:18], refs[18:20]
+    *raw, raw_sems, pack_send, pack_recv = refs[20:]
+    links = Links(depth)
+    fetch = Fetch([r.at[1] for r in weights_in], raw, raw_sems)
+    greet(everyone(depth) + [links.far_x])
+    fetch.wait()
+    build_pack(pack, *raw)
+    weights = Weights(links, pack, full_pack, pack_send, pack_recv)
+    weights.along(0)
+    weights.own_over()
+    weights.keep()
+    plan = Plan({(1, 1): [partial(weights.along, 1)]})
+    forward_body(True, plan, *compute, *results)
+    weights.landed(0)
+    weights.landed(1)
+    weights.own_over_landed()
+    links.finish()
+
+
+def forward_first(normed, wall, bcw, small, segr, segc, slots, gate, value, step, proj, depth, collective_id):
+    rows = gate.shape[1]
+    shapes = forward_shapes(normed, bcw, slots, True) + [
+        jax.ShapeDtypeStruct((depth, rows, PACK), LOW),
+        jax.ShapeDtypeStruct((2 * depth, rows, PACK), LOW),
+    ]
+    return pl.pallas_call(
+        partial(forward_first_kernel, depth),
+        out_shape=shapes,
+        in_specs=[VMEM_SPEC] * 6 + [ANY_SPEC] * 4,
+        out_specs=[VMEM_SPEC] * len(shapes),
+        scratch_shapes=raw_scratch(gate, step, proj) + weights_sems(depth),
+        compiler_params=params_of(collective_id),
+        name="forward_first",
+    )(normed, wall, bcw, small, segr, segc, gate, value, step, proj)
+
+
+def forward_second_kernel(depth, *refs):
+    compute, cotangent, results, (full, inv_out, inner_out), scratch = (
+        refs[:6],
+        refs[6],
+        refs[7:15],
+        refs[15:18],
+        refs[18:],
+    )
+    gather_send, gather_recv, own, shared, share_send, share_recv = scratch
     links = Links(depth)
     greet(everyone(depth))
-    if last:
-        full_out, total, piece_low, bufs, reduce_send, reduce_recv, gather_send, gather_recv = refs
-    else:
-        full_out, scalar_out, total, piece_low, scalars, bufs, reduce_send, reduce_recv, gather_send, gather_recv = refs
+    piece = full.shape[1]
+    mine = cotangent.at[0, pl.ds(pl.multiple_of(links.t * piece, piece), piece)]
+    gather = gather_task(links, [mine], [full], gather_send, gather_recv)
+    next(gather, None)
+    go = [advance(gather)]
+    forward_body(False, Plan({(1, 0): go, (2, 0): go, (3, 0): go}), *compute, *results)
+    run_tasks(gather)
+    _, wall_ref, _, small_ref = compute[:4]
+    squares_ref, gate_ref, mixed_ref = results[1], results[2], results[6]
+    width = gate_ref.shape[1]
+    rows = squares_ref.shape[0]
+    own[0:rows, :] = squares_ref[...]
+    gains = small_ref[5:6, :width]
+    per = 128 // piece
+    for row in range(rows):
+        grad = full[per * row : per * (row + 1)].reshape(128, full.shape[2])
+        grad_scaled = mxu(grad, wall_ref[:, OUT_AT : OUT_AT + 256], 1, 0)
+        grad_scaled = pltpu.roll(grad_scaled, 192, 1)[:, :width]
+        at = pl.ds(row * 128, 128)
+        gate_pre = gate_ref[at, :]
+        terms = grad_scaled * gains * mixed_ref[at, :] * gate_pre * sigmoid(gate_pre)
+        own[rows + row : rows + row + 1, :] = mxu(
+            jnp.ones((8, width), jnp.float32), terms, 1, 1, exact
+        )[0:1]
+    run_tasks(share_task(links, own, shared, share_send, share_recv))
+    summed = shared[0]
+    for slot in range(1, 4 * depth):
+        summed = summed + shared[slot]
+    inv = lax.rsqrt(summed[0:rows] / INNER + epsilon)
+    inv_out[...] = inv
+    inner_out[...] = inv * summed[rows:] / INNER
+    links.finish()
+
+
+def forward_second(normed, wall, bcw, small, segr, segc, slots, cotangent, depth, collective_id):
+    shapes = forward_shapes(normed, bcw, slots, False)
+    rows = shapes[1].shape
+    shapes = (
+        shapes
+        + [jax.ShapeDtypeStruct((4 * depth, cotangent.shape[1] // 4, cotangent.shape[2]), LOW)]
+        + [jax.ShapeDtypeStruct(rows, jnp.float32)] * 2
+    )
+    return pl.pallas_call(
+        partial(forward_second_kernel, depth),
+        out_shape=shapes,
+        in_specs=[VMEM_SPEC] * 7,
+        out_specs=[VMEM_SPEC] * len(shapes),
+        scratch_shapes=gather_sems(1, 4 * depth)
+        + [
+            pltpu.VMEM((2 * rows[0], 128), jnp.float32),
+            pltpu.VMEM((4 * depth, 2 * rows[0], 128), jnp.float32),
+            pltpu.SemaphoreType.DMA((4 * depth,)),
+            pltpu.SemaphoreType.DMA((4 * depth,)),
+        ],
+        compiler_params=params_of(collective_id),
+        name="forward_second",
+    )(normed, wall, bcw, small, segr, segc, cotangent)
+
+
+def own_column(rows, slot, piece):
+    per = 128 // piece
+    columns = spread_rows(rows)
+    lane = iota(columns.shape, 1)
+    column = jnp.sum(jnp.where(lane == slot // per, columns, 0.0), axis=1, keepdims=True)
+    at = iota((piece, 128), 0) + lax.rem(slot, per) * piece
+    pick = ones_where(at == iota((piece, 128), 1), jnp.float32)
+    return mxu(pick, jnp.broadcast_to(column, (128, 128)), 1, 0, exact)[:, 0:1]
+
+
+def norm_gradient(grad_rows, grad_normed, hidden, gain):
+    inv = lax.rsqrt(jnp.mean(hidden * hidden, axis=1, keepdims=True) + epsilon)
+    weighted = grad_normed * gain
+    grad = (
+        grad_rows
+        + inv * weighted
+        - hidden * (inv * inv * inv) * jnp.mean(weighted * hidden, axis=1, keepdims=True)
+    )
+    return grad, row_sum(grad_normed * hidden * inv)
+
+
+def owner_norm(total, grad, hidden_ref, gain_ref, bcw_ref):
     model_width = hidden_ref.shape[1]
-    piece = hidden_ref.shape[0]
-    run_tasks(
-        reduce_task(
-            links, lambda far: None, [both_ref], [total], [bufs], reduce_send, reduce_recv
-        )
-    )
     bc_low = total[:, model_width:].astype(LOW)
     grad_normed = total[:, :model_width] + mxu(bc_low, bcw_ref[...], 1, 1)
-    hidden = hidden_ref[...].astype(jnp.float32)
-    inv = lax.rsqrt(jnp.mean(hidden * hidden, axis=1, keepdims=True) + epsilon)
-    weighted = grad_normed * gain_ref[...]
-    gain_out[...] = row_sum(grad_normed * hidden * inv)
-    grad = (
-        grad_ref[...].astype(jnp.float32)
-        + inv * weighted
-        - hidden * (inv * inv * inv) * jnp.mean(weighted * hidden, axis=1, keepdims=True)
-    )
-    grad_low = grad.astype(LOW)
-    low_out[...] = grad_low
-    grad_out[...] = grad
-    if last:
-        piece_low[...] = bc_low
-        run_tasks(gather_task(links, [piece_low], [full_out], gather_send, gather_recv))
-    else:
-        piece_low[:, :model_width] = grad_low
-        piece_low[:, model_width:] = bc_low
-        inner = jnp.sum(grad_low.astype(jnp.float32) * total_ref[...], axis=1, keepdims=True) / INNER
-        eye = ones_where(iota((piece, 128), 0) == iota((piece, 128), 1), jnp.float32)
-        row = mxu(jnp.broadcast_to(inner, (piece, 8)), eye, 0, 0, exact)
-        scalars[...] = jnp.where(iota((8, 128), 0) == 1, row, scalar_ref[...])
-        run_tasks(
-            gather_task(links, [piece_low, scalars], [full_out, scalar_out], gather_send, gather_recv)
-        )
-    links.finish()
-
-
-def turn_backward(both, grad, hidden, gain, bcw, total, scalars, last, depth, collective_id):
-    piece, model_width = hidden.shape
-    slots, _, whole_width = both.shape
-    f32 = jnp.float32
-    low_width = whole_width - model_width if last else whole_width
-    fulls = [jax.ShapeDtypeStruct((slots, piece, low_width), LOW)]
-    own = [pltpu.VMEM((piece, low_width), LOW)]
-    if not last:
-        fulls.append(jax.ShapeDtypeStruct((slots, 8, 128), f32))
-        own.append(pltpu.VMEM((8, 128), f32))
-    return pl.pallas_call(
-        partial(turn_backward_kernel, depth, last),
-        out_shape=[
-            jax.ShapeDtypeStruct((piece, model_width), f32),
-            jax.ShapeDtypeStruct((1, model_width), f32),
-            jax.ShapeDtypeStruct((piece, model_width), LOW),
-        ]
-        + fulls,
-        in_specs=[VMEM_SPEC] * 7,
-        out_specs=[VMEM_SPEC] * (3 + len(fulls)),
-        scratch_shapes=[pltpu.VMEM((piece, whole_width), f32)]
-        + own
-        + reduce_scratch([(piece, whole_width)], [LOW], depth)
-        + gather_sems(len(fulls), slots),
-        compiler_params=params_of(collective_id),
-        name="turn_backward",
-    )(both, grad, hidden, gain, bcw, total, scalars)
-
-
-def weights_task(links, packs, fulls, send_sem, recv_sem):
-    x, z, depth = links.x, links.z, links.depth
-    every = range(len(packs))
-
-    def source(a, far, part):
-        ref = packs[a]
-        return half(ref.at[far] if len(ref.shape) == len(fulls[a].shape) else ref, part)
-
-    def send(a, ref, slot, part, kind, peer):
-        links.send(
-            ref, half(fulls[a].at[slot], part), send_sem.at[a, kind, part], recv_sem.at[a, slot, part], peer
-        )
-
-    def arrived(a, slot, part):
-        ref = half(fulls[a].at[slot], part)
-        links.wait(ref, send_sem.at[a, 0, part], recv_sem.at[a, slot, part])
-        return ref
-
-    mine = x * depth + z
-    for a in every:
-        for part in range(HALVES):
-            send(a, source(a, z, part), mine, part, 0, links.far_x)
-    for place, far in enumerate(links.far_first()):
-        for a in every:
-            for part in range(HALVES):
-                send(a, source(a, far, part), mine, part, 1 + place, {"ctx": far})
-    for a in every:
-        ref = packs[a]
-        fulls[a][mine] = ref[z] if len(ref.shape) == len(fulls[a].shape) else ref[...]
-    yield
-    for place, far in enumerate(links.near_first()):
-        for part in range(HALVES):
-            for a in every:
-                slot = x * depth + far
-                send(a, arrived(a, slot, part), slot, part, depth + place, links.far_x)
-        yield
-    for far in [z] + links.near_first():
-        for part in range(HALVES):
-            for a in every:
-                arrived(a, (1 - x) * depth + far, part)
-
-
-def weights_sems(count, depth):
-    return [
-        pltpu.SemaphoreType.DMA((count, 2 * depth, HALVES)),
-        pltpu.SemaphoreType.DMA((count, 2 * depth, HALVES)),
-    ]
-
-
-def prepare_kernel(depth, count, *refs):
-    pieces, packs = refs[:count], refs[count : count + 2]
-    refs = refs[count + 2 :]
-    fulls, full_packs = refs[:count], refs[count : count + 2]
-    gather_send, gather_recv, pack_send, pack_recv = refs[count + 2 :]
+    grad, gain = norm_gradient(grad, grad_normed, hidden_ref[...].astype(jnp.float32), gain_ref[...])
+    return bc_low, grad, gain
+
+
+def backward_second_kernel(depth, *refs):
+    compute, (cotangent, hidden_ref, gain_ref, bcw_ref, before_ref) = refs[:14], refs[14:19]
+    late, sums, grad_out, gain_out, full_out, inner_out, early_out = refs[19:26]
+    both, early, *work = refs[26:33]
+    (
+        early_bufs, early_send, early_recv,
+        back_total, piece_low, scalars, scalars_full, back_bufs, back_send, back_recv,
+        gather_send, gather_recv,
+    ) = refs[33:]
     links = Links(depth)
     greet(everyone(depth) + [links.far_x])
+    piece, model_width = hidden_ref.shape
+    scatter = scatter_task(links, early, early_out, early_bufs, early_send, early_recv)
+    go = advance(scatter)
+    stream = SumStream(links, both, back_total, back_bufs, back_send, back_recv)
+
+    def call(method, far):
+        return partial(method, far)
+
+    plan = Plan(
+        {
+            (-1, 1): [go],
+            (0, 3): [call(stream.first, 3)],
+            (1, 0): [call(stream.second, 3)],
+            (1, 2): [go],
+            (1, 3): [call(stream.first, 2)],
+            (2, 0): [call(stream.second, 2), call(stream.third, 3)],
+            (2, 2): [go],
+            (2, 3): [call(stream.first, 1)],
+            (3, 0): [call(stream.second, 1), call(stream.third, 2)],
+            (3, 3): [call(stream.first, 0)],
+            (4, 0): [call(stream.second, 0), call(stream.third, 1)],
+        }
+    )
+    backward_body(plan, *compute, both, early, late, sums, *work)
+    stream.third(0)
+    stream.end()
+    rows = pl.ds(pl.multiple_of(links.t * piece, piece), piece)
+    bc_low, grad, gain_out[...] = owner_norm(
+        back_total,
+        cotangent[0, rows, :].astype(jnp.float32),
+        hidden_ref,
+        gain_ref[...].astype(jnp.float32)[1:2],
+        bcw_ref,
+    )
+    grad_low = grad.astype(LOW)
+    piece_low[:, :model_width] = grad_low
+    piece_low[:, model_width:] = bc_low
+    inner = jnp.sum(grad_low.astype(jnp.float32) * before_ref[...], axis=1, keepdims=True) / INNER
+    slot, per = links.z * 4 + links.t, 128 // piece
+    lane = iota((piece, 128), 0) + lax.rem(slot, per) * piece
+    place = ones_where(lane == iota((piece, 128), 1), jnp.float32)
+    inner_rows = mxu(jnp.broadcast_to(inner, (piece, 8)), place, 0, 0, exact)
+    scalars[...] = jnp.where(iota(inner_rows.shape, 0) == slot // per, inner_rows, 0.0)
+    grad_out[...] = grad
     run_tasks(
-        gather_task(links, pieces, fulls, gather_send, gather_recv),
-        weights_task(links, packs, full_packs, pack_send, pack_recv),
-    )
+        gather_task(links, [piece_low, scalars], [full_out, scalars_full], gather_send, gather_recv),
+        scatter,
+    )
+    inner_rows = scalars_full[0]
+    for other in range(1, 4 * depth):
+        inner_rows = inner_rows + scalars_full[other]
+    inner_out[...] = inner_rows
     links.finish()
 
 
-def prepare(pieces, packs, depth, collective_id):
-    count = len(pieces)
-    slots = 4 * depth
+def backward_second(
+    grad, inv, inner, normed, wall, small, segr, segc, kept, slots, cotangent, hidden, gain, bcw, before, depth, collective_id
+):
+    f32 = jnp.float32
+    piece, model_width = hidden.shape
+    (both, early, late, sums), work = backward_shapes(normed, kept, slots)
+    whole_width = both.shape[2]
+    shapes = [
+        late,
+        sums,
+        jax.ShapeDtypeStruct((piece, model_width), f32),
+        jax.ShapeDtypeStruct((1, model_width), f32),
+        jax.ShapeDtypeStruct(both.shape, LOW),
+        jax.ShapeDtypeStruct(inv.shape, f32),
+        jax.ShapeDtypeStruct((depth,) + early.shape[1:], LOW),
+    ]
     return pl.pallas_call(
-        partial(prepare_kernel, depth, count),
-        out_shape=[jax.ShapeDtypeStruct((slots,) + p.shape, p.dtype) for p in pieces]
-        + [jax.ShapeDtypeStruct((2 * depth,) + p.shape[-2:], p.dtype) for p in packs],
-        in_specs=[VMEM_SPEC] * (count + 2),
-        out_specs=[VMEM_SPEC] * (count + 2),
-        scratch_shapes=gather_sems(count, slots) + weights_sems(2, depth),
+        partial(backward_second_kernel, depth),
+        out_shape=shapes,
+        in_specs=[VMEM_SPEC] * 19,
+        out_specs=[VMEM_SPEC] * len(shapes),
+        scratch_shapes=[pltpu.VMEM(both.shape, LOW), pltpu.VMEM(early.shape, LOW)]
+        + work
+        + scatter_scratch(early.shape[1:], depth, False)
+        + [
+            pltpu.VMEM((piece, whole_width), f32),
+            pltpu.VMEM((piece, whole_width), LOW),
+            pltpu.VMEM(inv.shape, f32),
+            pltpu.VMEM((slots,) + inv.shape, f32),
+        ]
+        + stream_scratch((piece, whole_width), LOW)
+        + gather_sems(2, slots),
         compiler_params=params_of(collective_id),
-        name="prepare",
-    )(*pieces, *packs)
-
-
-def finish_kernel(depth, channel_rows, sums_ref, hidden_ref, grad_ref, by_z_out, sum_out, hidden_out, grad_out, work, total, arrived_ref, send_sem, recv_sem, row_send, row_recv):
+        name="backward_second",
+    )(grad, inv, inner, normed, wall, small, segr, segc, *kept, cotangent, hidden, gain, bcw, before)
+
+
+def backward_first_kernel(depth, *refs):
+    compute, (late1, normed1, grad_in, hidden_ref, gain_ref, bcw_ref, sums1, gain1, part, hidden1, inv1) = (
+        refs[:14],
+        refs[14:25],
+    )
+    late1_out, early0_out, late0_out, bc_out, by_z_out, sum_out, hidden_grad_out, hidden_out = refs[25:33]
+    both, early, late, sums, *work = refs[33:42]
+    (
+        out_total, out_low, out_bufs, out_send, out_recv, out_row_send, out_row_recv,
+        total, low, bc_piece, bc_full, own,
+        bufs, stream_send, stream_recv,
+        gather_send, gather_recv,
+        late1_bufs, late1_send, late1_recv,
+        early0_bufs, early0_send, early0_recv,
+        late0_bufs, late0_send, late0_recv,
+        bc_slots, bc_arrived, bc_send, bc_recv,
+        sums_arrived, sums_work, sums_send, sums_recv,
+        row_send, row_recv,
+    ) = refs[42:]
     links = Links(depth)
-    z, t = links.z, links.t
     greet(everyone(depth) + [links.far_x])
-
-    def rows():
-        outs = (hidden_out, grad_out)
-        for a, ref in enumerate((hidden_ref, grad_ref)):
-            for way, peer in enumerate((links.chip, links.core)):
-                links.send(ref, outs[a].at[t], row_send.at[a, way], row_recv.at[a, t], peer)
-            outs[a][t] = ref[...]
-        yield
-        for a in range(2):
-            column = other_chip(t)
-            ref = outs[a].at[column]
-            links.wait(ref, row_send.at[a, 0], row_recv.at[a, column])
-            links.send(ref, ref, row_send.at[a, 2], row_recv.at[a, column], links.core)
-        yield
-        for a in range(2):
-            for column in (other_core(t), other_chip(other_core(t))):
-                links.wait(outs[a].at[column], row_send.at[a, 0], row_recv.at[a, column])
-
-    def sums():
-        links.send(sums_ref, arrived_ref.at[0], send_sem.at[0], recv_sem.at[0], links.far_x)
-        yield
-        links.wait(arrived_ref.at[0], send_sem.at[0], recv_sem.at[0])
-        work[...] = sums_ref[...] + arrived_ref[0]
-        links.send(work, arrived_ref.at[1], send_sem.at[1], recv_sem.at[1], links.core)
-        yield
-        links.wait(arrived_ref.at[1], send_sem.at[1], recv_sem.at[1])
-        total[0] = work[...] + arrived_ref[1]
-        links.send(total.at[0], arrived_ref.at[2], send_sem.at[2], recv_sem.at[2], links.chip)
-        yield
-        links.wait(arrived_ref.at[2], send_sem.at[2], recv_sem.at[2])
-        row = iota(work.shape, 0)
-        own = jnp.logical_and(row < 16 * LAYERS, lax.rem(row, 16) < channel_rows)
-        total[1] = jnp.where(own, work[...], total[0] + arrived_ref[2])
-        for hop in range(1, depth):
-            links.send(
-                total.at[1], by_z_out.at[z], send_sem.at[2 + hop], recv_sem.at[3 + z], {"ctx": lax.rem(z + hop, depth)}
+    piece, model_width = grad_in.shape
+    normed_ref, grad_ref = compute[3], compute[0]
+    output = SumStream(links, part, out_total, out_bufs, out_send, out_recv)
+    stream = SumStream(links, both, total, bufs, stream_send, stream_recv)
+    late_task1 = scatter_task(links, late1, late1_out, late1_bufs, late1_send, late1_recv)
+    early_task0 = scatter_task(links, early, early0_out, early0_bufs, early0_send, early0_recv)
+    late_task0 = scatter_task(links, late, late0_out, late0_bufs, late0_send, late0_recv)
+    bc1 = bc_task(links, bc_slots.at[1], bc_arrived.at[1], bc_out, 1, bc_send.at[1], bc_recv.at[1])
+    next(late_task1, None)
+    for far in (3, 2, 1, 0):
+        output.first(far)
+
+    def call(method, far):
+        return partial(method, far)
+
+    def output_rows():
+        output.end()
+        inv = own_column(inv1[...], links.z * 4 + links.t, piece)
+        out_low[...] = (hidden1[...] + out_total[...] * inv).astype(LOW)
+        yield from rows_task(links, out_low, hidden_out, out_row_send, out_row_recv)
+
+    def bc_first():
+        bc_products(normed1, grad_ref[:, model_width:], bc_slots.at[1])
+        next(bc1, None)
+
+    go1, go0 = advance(late_task1), advance(early_task0)
+    plan = Plan(
+        {
+            (-1, 0): [go1, call(output.second, 3)],
+            (-1, 1): [go0, go1, call(output.second, 2)],
+            (0, 1): [call(output.third, 3), go1],
+            (0, 3): [call(stream.first, 3), go1, call(output.third, 2)],
+            (1, 0): [call(stream.second, 3), go0],
+            (1, 2): [call(output.second, 1)],
+            (1, 3): [call(stream.first, 2), go0],
+            (2, 0): [call(stream.second, 2), call(stream.third, 3), go1],
+            (2, 2): [call(output.third, 1), call(output.second, 0)],
+            (2, 3): [call(stream.first, 1), go0],
+            (3, 0): [call(stream.second, 1), call(stream.third, 2)],
+            (3, 2): [call(output.third, 0)],
+            (3, 3): [call(stream.first, 0), go0],
+            (4, 0): [call(stream.second, 0), call(stream.third, 1)],
+        }
+    )
+    backward_body(plan, *compute, both, early, late, sums, *work)
+    next(late_task0, None)
+    bc_first()
+    stream.third(0)
+    next(late_task0, None)
+    stream.end()
+    rows = pl.ds(pl.multiple_of(links.t * piece, piece), piece)
+    bc_low, grad, gain = owner_norm(
+        total, grad_in[...], hidden_ref.at[0, rows], gain_ref[...].astype(jnp.float32)[0:1], bcw_ref
+    )
+    bc_piece[...] = bc_low
+    low[...] = grad.astype(LOW)
+    own[...] = jnp.zeros(own.shape, jnp.float32)
+    own[0:16, :] = sums[...]
+    own[16:32, :] = sums1[...]
+    count = model_width // 256
+    for layer, row in enumerate((gain, gain1[...])):
+        for at in range(count):
+            to = 16 * LAYERS + layer * count + at
+            own[to : to + 1, :] = row[:, at * 256 : (at + 1) * 256]
+    run_tasks(
+        gather_task(links, [bc_piece], [bc_full], gather_send, gather_recv),
+        sums_task(links, own, sums_arrived, sums_work, by_z_out, sum_out, sums_send, sums_recv),
+        rows_task(links, low, hidden_grad_out, row_send, row_recv),
+        late_task0,
+        output_rows(),
+        early_task0,
+        late_task1,
+        bc1,
+    )
+    tokens = bc_full.shape[0] * bc_full.shape[1]
+    bc_products(normed_ref, bc_full[...].reshape(tokens, bc_full.shape[2]), bc_slots.at[0])
+    bc0 = bc_task(links, bc_slots.at[0], bc_arrived.at[0], bc_out, 0, bc_send.at[0], bc_recv.at[0])
+    run_tasks(bc0)
+    links.finish()
+
+
+def backward_first(
+    grad, inv, inner, normed, wall, small, segr, segc, kept, slots, late1, normed1, grad_in, hidden, gain, bcw, sums1, gain1, part, hidden1, inv1, depth, collective_id
+):
+    f32 = jnp.float32
+    piece, model_width = grad_in.shape
+    (both, early, late, sums), work = backward_shapes(normed, kept, slots)
+    whole_width = both.shape[2]
+    k_slots, k_rows, _ = late1.shape
+    bc_width = kept[2].shape[1]
+    small_sums = (16 * LAYERS + 16, 256)
+    shapes = [
+        jax.ShapeDtypeStruct((depth,) + late.shape[1:], LOW),
+        jax.ShapeDtypeStruct((depth,) + early.shape[1:], LOW),
+        jax.ShapeDtypeStruct((depth,) + late.shape[1:], LOW),
+        jax.ShapeDtypeStruct((LAYERS, k_rows, bc_width), f32),
+        jax.ShapeDtypeStruct((depth,) + small_sums, f32),
+        jax.ShapeDtypeStruct(small_sums, f32),
+        jax.ShapeDtypeStruct((4, piece, model_width), LOW),
+        jax.ShapeDtypeStruct((4, piece, model_width), LOW),
+    ]
+    return pl.pallas_call(
+        partial(backward_first_kernel, depth),
+        out_shape=shapes,
+        in_specs=[VMEM_SPEC] * 25,
+        out_specs=[VMEM_SPEC] * len(shapes),
+        scratch_shapes=[pltpu.VMEM(a.shape, a.dtype) for a in (both, early, late, sums)]
+        + work
+        + [pltpu.VMEM((piece, model_width), f32), pltpu.VMEM((piece, model_width), LOW)]
+        + stream_scratch((piece, model_width), LOW)
+        + ROWS_SEMS
+        + [
+            pltpu.VMEM((piece, whole_width), f32),
+            pltpu.VMEM((piece, model_width), LOW),
+            pltpu.VMEM((piece, bc_width), LOW),
+            pltpu.VMEM((slots, piece, bc_width), LOW),
+            pltpu.VMEM(small_sums, f32),
+        ]
+        + stream_scratch((piece, whole_width), LOW)
+        + gather_sems(1, slots)
+        + scatter_scratch(late.shape[1:], depth, False)
+        + scatter_scratch(early.shape[1:], depth, False)
+        + scatter_scratch(late.shape[1:], depth, False)
+        + [
+            pltpu.VMEM((LAYERS, k_slots, k_rows, bc_width), LOW),
+            pltpu.VMEM((LAYERS, k_rows, bc_width), LOW),
+            pltpu.SemaphoreType.DMA((LAYERS,)),
+            pltpu.SemaphoreType.DMA((LAYERS,)),
+        ]
+        + sums_scratch(small_sums, depth)
+        + ROWS_SEMS,
+        compiler_params=params_of(collective_id),
+        name="backward_first",
+    )(grad, inv, inner, normed, wall, small, segr, segc, *kept, late1, normed1, grad_in, hidden, gain, bcw, sums1, gain1, part, hidden1, inv1)
+
+
+def emit_kernel(
+    hidden_ref, grad_ref, early0, late0, early1, late1, bc_ref, by_z, whole,
+    hidden_out, grad_out, gain_out, gate_out, value_out, bc_out, step_out,
+    taps_out, tap_bias_out, bc_taps_out, bc_bias_out, decay_out, step_bias_out, skip_out, out_gain_out, proj_out,
+):
+    piece = hidden_ref.shape[1]
+    depth, _, _ = by_z.shape
+    channels, heads_whole = taps_out.shape[2], skip_out.shape[1]
+    width, heads = channels // depth, heads_whole // depth
+    for at in range(4):
+        hidden_out[0, at * piece : (at + 1) * piece, :] = hidden_ref[at]
+        grad_out[0, at * piece : (at + 1) * piece, :] = grad_ref[at]
+    bc_out[...] = bc_ref[...]
+    count = gain_out.shape[1] // 256
+    for layer, (early, late) in enumerate(((early0, late0), (early1, late1))):
+        one = slice(layer, layer + 1)
+        unpack_early(early, width, layer, gate_out, proj_out)
+        value = step = by_channel = by_head = 0.0
+        rows = slice(16 * layer, 16 * layer + 16)
+        for far in range(depth):
+            place = placed(far, width, channels)
+            value += mxu(late[far], place, 1, 0)
+            window, head = iota((256, 16), 0), iota((256, 16), 1) - far * heads
+            mine = jnp.logical_and(head >= 0, head < heads)
+            step += mxu(ones_where(jnp.logical_and(mine, window == width + head), LOW), late[far], 0, 1)
+            by_channel += mxu(by_z[far, rows, :], place.astype(jnp.float32), 1, 0, exact)
+            window, head = iota((256, 128), 0), iota((256, 128), 1) - far * heads
+            mine = jnp.logical_and(head >= 0, head < heads)
+            by_head += mxu(
+                by_z[far, rows, :],
+                ones_where(jnp.logical_and(mine, window == head * HEADDIM), jnp.float32),
+                1,
+                0,
+                exact,
             )
-        by_z_out[z] = total[1]
-        yield
-        for hop in range(1, depth):
-            far = lax.rem(z + hop, depth)
-            links.wait(by_z_out.at[far], send_sem.at[0], recv_sem.at[3 + far])
-        whole = by_z_out[0]
-        for far in range(1, depth):
-            whole = whole + by_z_out[far]
-        sum_out[...] = whole
-
-    run_tasks(rows(), sums())
-    links.finish()
-
-
-def finish(sums, hidden, grad, depth, collective_id):
+        value_out[layer] = value
+        for head in range(heads_whole):
+            step_out[head, one, :] = step[head : head + 1]
+        taps_out[layer] = by_channel[0:4]
+        tap_bias_out[one, :] = by_channel[4:5]
+        out_gain_out[one, :] = by_channel[5:6]
+        skip_out[one, :] = by_head[6:7, :heads_whole]
+        step_bias_out[one, :] = by_head[7:8, :heads_whole]
+        decay_out[one, :] = by_head[8:9, :heads_whole]
+        bc_taps_out[layer] = whole[16 * layer + 9 : 16 * layer + 13, :]
+        bc_bias_out[one, :] = whole[16 * layer + 13 : 16 * layer + 14, :]
+        for at in range(count):
+            row = 16 * LAYERS + layer * count + at
+            gain_out[one, at * 256 : (at + 1) * 256] = whole[row : row + 1, :]
+
+
+def emit(hidden, grad, early0, late0, early1, late1, bc, by_z, whole, tokens, heads, channels):
     f32 = jnp.float32
+    rows, model_width = early0.shape[1], hidden.shape[2]
+    bc_width = bc.shape[2]
+    shapes = [
+        ((1, tokens, model_width), LOW),
+        ((1, tokens, model_width), LOW),
+        ((LAYERS, model_width), f32),
+        ((LAYERS, rows, channels), f32),
+        ((LAYERS, rows, channels), f32),
+        ((LAYERS, rows, bc_width), f32),
+        ((heads, LAYERS, rows), f32),
+        ((LAYERS, 4, channels), f32),
+        ((LAYERS, channels), f32),
+        ((LAYERS, 4, bc_width), f32),
+        ((LAYERS, bc_width), f32),
+        ((LAYERS, heads), f32),
+        ((LAYERS, heads), f32),
+        ((LAYERS, heads), f32),
+        ((LAYERS, channels), f32),
+        ((LAYERS, channels, rows), f32),
+    ]
     return pl.pallas_call(
-        partial(finish_kernel, depth, 9),
-        out_shape=[
-            jax.ShapeDtypeStruct((depth,) + sums.shape, f32),
-            jax.ShapeDtypeStruct(sums.shape, f32),
-            jax.ShapeDtypeStruct((4,) + hidden.shape, hidden.dtype),
-            jax.ShapeDtypeStruct((4,) + grad.shape, grad.dtype),
-        ],
-        in_specs=[VMEM_SPEC] * 3,
-        out_specs=[VMEM_SPEC] * 4,
-        scratch_shapes=[
-            pltpu.VMEM(sums.shape, f32),
-            pltpu.VMEM((2,) + sums.shape, f32),
-            pltpu.VMEM((3,) + sums.shape, f32),
-            pltpu.SemaphoreType.DMA((3 + depth,)),
-            pltpu.SemaphoreType.DMA((3 + depth,)),
-            pltpu.SemaphoreType.DMA((2, 3)),
-            pltpu.SemaphoreType.DMA((2, 4)),
-        ],
-        compiler_params=params_of(collective_id),
-        name="finish",
-    )(sums, hidden, grad)
+        emit_kernel,
+        out_shape=[jax.ShapeDtypeStruct(*shape) for shape in shapes],
+        in_specs=[VMEM_SPEC] * 9,
+        out_specs=[VMEM_SPEC] * len(shapes),
+        compiler_params=local_params(),
+        name="emit",
+    )(hidden, grad, early0, late0, early1, late1, bc, by_z, whole)
 
 
 def split_local(
@@ -1809,166 +2422,81 @@
 ):
     tokens, model_width = hidden_in.shape[1:]
     slots = depth * 4
-    piece = tokens // 4
-    width = gate_proj.shape[2] // depth
-    heads = step_proj.shape[2] // depth
-    k_rows = gate_proj.shape[1]
-    f32 = jnp.float32
-    t = lax.axis_index("tp")
-    z = lax.axis_index("ctx")
-
-    def own_piece(array):
-        return lax.dynamic_slice_in_dim(array, t * piece, piece, 0)
-
-    my_hidden = own_piece(hidden_in[0])
-    my_cotangent = own_piece(cotangent[0])
-    gains = [norm_gain[layer].astype(f32) for layer in range(LAYERS)]
-
-    def by_z(block):
-        return block.reshape(block.shape[0], depth, -1).transpose(1, 0, 2)
-
-    packs, shared = [], []
-    for layer in range(LAYERS):
-        pack = jnp.concatenate(
-            [
-                by_z(gate_proj[layer]),
-                by_z(out_proj[layer].T),
-                by_z(value_proj[layer]),
-                by_z(step_proj[layer]),
-            ],
-            axis=2,
-        )
-        packs.append(jnp.pad(pack, ((0, 0), (0, 0), (0, PACK - pack.shape[2]))))
-        shared.append(bc_proj[layer])
-    hidden0 = my_hidden.astype(f32)
-    _, my_normed0 = norm_rows(hidden0, gains[0])
-    seg_rows = lane_rows([own_piece(segment_ids[0]).astype(f32)[None]], 1)[0]
-    normed0, seg_full, pack0, shared0 = prepare([my_normed0, seg_rows], [packs[0], shared[0]], depth, 1)
-    cotangent_full, pack1, shared1 = prepare([my_cotangent], [packs[1], shared[1]], depth, 2)
-    walls = [pack0.reshape(-1, PACK), pack1.reshape(-1, PACK)]
-    bc_walls = [shared0.reshape(-1, shared0.shape[2]), shared1.reshape(-1, shared1.shape[2])]
+    heads, channels = step_proj.shape[2], gate_proj.shape[2]
+    projections = (gate_proj, value_proj, step_proj, out_proj)
+    small = (
+        conv_value,
+        conv_value_bias,
+        out_gain,
+        skip_gain,
+        step_bias,
+        decay_log,
+        conv_bc,
+        conv_bc_bias,
+    )
+    normed0, pack0, shared0, smalls, segr, segc = prepare(
+        hidden_in, segment_ids, norm_gain, *projections, bc_proj, small, depth, 1
+    )
+    seg = (segr, segc)
     normed0 = normed0.reshape(-1, model_width)
-    cotangent_full = cotangent_full.reshape(-1, model_width)
-    segment = seg_full[:, 0, :piece].reshape(-1)
-    segr = segment[None]
-    segc = jnp.broadcast_to(jnp.pad(segment, 8, constant_values=-1.0)[:, None], (segment.size + 16, 256))
-
-    def per_lane(by_head):
-        return jnp.repeat(by_head, HEADDIM, axis=1)[:, None]
-
-    per_channel = jnp.concatenate(
-        [
-            conv_value.astype(f32),
-            conv_value_bias.astype(f32)[:, None],
-            out_gain.astype(f32)[:, None],
-            per_lane(skip_gain),
-            per_lane(step_bias),
-            per_lane(-jnp.exp(decay_log)),
-        ],
-        axis=1,
-    )
-    per_channel = lax.dynamic_slice_in_dim(per_channel, z * width, width, 2)
-    per_channel = jnp.pad(per_channel, ((0, 0), (0, 0), (0, 256 - width)))
-    smalls = jnp.concatenate(
-        [per_channel, conv_bc.astype(f32), conv_bc_bias.astype(f32)[:, None], jnp.zeros((LAYERS, 2, 256), f32)],
-        axis=1,
-    )
-
-    def forward(layer, normed, precise):
-        return split_forward(
-            normed, walls[layer], bc_walls[layer], smalls[layer], segr, segc, slots, precise
-        )
-
-    def backward(layer, grad, scalars, normed, kept):
-        return split_backward(
-            grad, scalars, normed, walls[layer], smalls[layer], segr, segc, kept, slots
-        )
-
-    gated0, squares0, *kept0 = forward(0, normed0, True)
-    hidden1, total0, inv_rows0, normed1 = turn_forward(
-        gated0, squares0, smalls[0], walls[0], my_hidden, gains[1][None], depth, 3
-    )
-    inv0 = lax.dynamic_slice_in_dim(inv_rows0.reshape(-1), (z * 4 + t) * piece, piece, 0)
+    wall0, bc_wall0 = pack0.reshape(-1, PACK), shared0.reshape(model_width, -1)
+    gated0, squares0, *kept0, packs1, early = forward_first(
+        normed0, wall0, bc_wall0, smalls[0], *seg, slots, *projections, depth, 2
+    )
+    hidden1, total0, inv_rows0, normed1, pack1, shared1 = turn_forward(
+        gated0, squares0, smalls[0], wall0, hidden_in, norm_gain, packs1, early, bc_proj, depth, 3
+    )
+    wall1, bc_wall1 = pack1.reshape(-1, PACK), shared1.reshape(model_width, -1)
     normed1 = normed1.reshape(-1, model_width)
-    part1, squares1, *kept1 = forward(1, normed1, False)
-    total1, square_rows1 = reduce_pieces([part1, squares1], depth, 5)
-    inv1 = lax.rsqrt(square_rows1[0, :piece] / INNER + epsilon)
-    total1 = total1 * inv1[:, None]
-    hidden_out = (hidden1 + total1).astype(LOW)
-
-    def bc_grad(normed, bc_low):
-        return jnp.stack(
-            [
-                dot_left(
-                    lax.dynamic_slice_in_dim(normed, (far_x * depth + z) * k_rows, k_rows, 1), bc_low
-                ).astype(LOW)
-                for far_x in range(2)
-            ]
-        )
-
-    def scalar_rows(inv, inner):
-        return lane_rows([inv[None], inner[None] / INNER], 1)[0]
-
-    inner1 = jnp.sum(my_cotangent.astype(f32) * total1, axis=1)
-    (scalars1,) = gather_pieces([scalar_rows(inv1, inner1)], depth, 8)
-    both1, grads1, sums1 = backward(1, cotangent_full, scalars1, normed1, kept1)
-    grad1, gain_grad1, _, full0, scalars0 = turn_backward(
-        both1,
-        my_cotangent,
+    part1, _, *kept1, cotangent_full, inv_rows1, inner_rows1 = forward_second(
+        normed1, wall1, bc_wall1, smalls[1], *seg, slots, cotangent, depth, 4
+    )
+    late1, sums1, grad1, gain1, full0, inner_rows0, early1 = backward_second(
+        cotangent_full.reshape(-1, model_width),
+        inv_rows1,
+        inner_rows1,
+        normed1,
+        wall1,
+        smalls[1],
+        *seg,
+        kept1,
+        slots,
+        cotangent,
         hidden1,
-        gains[1][None],
-        bc_walls[1],
+        norm_gain,
+        bc_wall1,
         total0,
-        scalar_rows(inv0, jnp.zeros_like(inv0)),
-        False,
+        depth,
+        5,
+    )
+    late1, early0, late0, bc_grad, by_z, whole, grad_hidden, hidden_out = backward_first(
+        full0.reshape(-1, full0.shape[2]),
+        inv_rows0,
+        inner_rows0,
+        normed0,
+        wall0,
+        smalls[0],
+        *seg,
+        kept0,
+        slots,
+        late1,
+        normed1,
+        grad1,
+        hidden_in,
+        norm_gain,
+        bc_wall0,
+        sums1,
+        gain1,
+        part1,
+        hidden1,
+        inv_rows1,
         depth,
         6,
     )
-    full0 = full0.reshape(-1, full0.shape[2])
-    out1, bc_out1 = scatter_grads(grads1, bc_grad(normed1, full0[:, model_width:]), depth, 10)
-    both0, grads0, sums0 = backward(0, full0, scalars0, normed0, kept0)
-    _, gain_grad0, grad_low0, bc_all0 = turn_backward(
-        both0, grad1, my_hidden, gains[0][None], bc_walls[0], total0, scalars0[0], True, depth, 7
-    )
-    out0, bc_out0 = scatter_grads(
-        grads0, bc_grad(normed0, bc_all0.reshape(-1, bc_all0.shape[2])), depth, 12
-    )
-
-    outs = jnp.stack([out0, out1]).astype(f32)
-
-    def channels(lo, hi):
-        return outs[..., lo:hi].transpose(0, 2, 1, 3).reshape(LAYERS, k_rows, -1)
-
-    gain_rows = jnp.concatenate([gain_grad0, gain_grad1], axis=0).reshape(-1, 256)
-    gain_count = gain_rows.shape[0]
-    sums = jnp.concatenate([sums0, sums1, gain_rows, jnp.zeros((16 - gain_count, 256), f32)], axis=0)
-    by_z, whole, hidden_out, grad_hidden = finish(sums, hidden_out, grad_low0, depth, 13)
-    by_channel = jnp.stack([by_z[:, 16 * layer : 16 * layer + 9, :width] for layer in range(LAYERS)])
-    by_channel = by_channel.transpose(0, 2, 1, 3).reshape(LAYERS, 9, -1)
-    bc_sums = jnp.stack([whole[16 * layer + 9 : 16 * layer + 14] for layer in range(LAYERS)])
-    gain_grad = whole[16 * LAYERS : 16 * LAYERS + gain_count].reshape(LAYERS, model_width)
-
-    def by_head(row):
-        return by_channel[:, row].reshape(LAYERS, -1, HEADDIM)[:, :, 0]
-
-    return (
-        hidden_out.reshape(1, tokens, model_width),
-        grad_hidden.reshape(1, tokens, model_width),
-        gain_grad,
-        channels(0, width),
-        channels(2 * width, 3 * width),
-        jnp.stack([bc_out0, bc_out1]),
-        channels(3 * width, 3 * width + heads),
-        by_channel[:, :4],
-        by_channel[:, 4],
-        bc_sums[:, :4],
-        bc_sums[:, 4],
-        by_head(8),
-        by_head(7),
-        by_head(6),
-        by_channel[:, 5],
-        channels(width, 2 * width).transpose(0, 2, 1),
-    )
+    outs = emit(
+        hidden_out, grad_hidden, early0, late0, early1, late1, bc_grad, by_z, whole, tokens, heads, channels
+    )
+    return (*outs[:6], outs[6].transpose(1, 2, 0), *outs[7:])
 
 
 def solution(mesh):

time: 626 us -> 451 us (0.72)
  Pallas kernels: 544 us -> 433 us
  local copies, waits for them, and re-layouts: 44.2 us -> 7.92 us
  other arithmetic: 18.7 us -> 0 us
  matrix products: 7.26 us -> 0 us
    pallas_call x13 -> x6, Pallas kernels: 472 us -> 354 us  [the longest x1 116 us: backward_first(): pl.pallas_call(partial(backward_first_kernel, depth), out_shape=shapes, i...]
    reshape x8 -> x0, local copies, waits for them, and re-layouts: 9.77 us -> none  [the longest x3 8.31 us: channels(): return outs[..., lo:hi].transpose(0, 2, 1, 3).reshape(LAYERS, k_rows, -1)]
    transpose x9 -> x0, local copies, waits for them, and re-layouts: 8.43 us -> none  [the longest x5 7.07 us: channels(): return outs[..., lo:hi].transpose(0, 2, 1, 3).reshape(LAYERS, k_rows, -1)]
    dot_general x4 -> x0, matrix products: 7.26 us -> none  [dot_left(): lax.dot_general(left_rows, right_rows, (((0,), (0,)), ((), ())), preferre...]
    pallas_call x1, Pallas kernels: 72.4 us -> 79.4 us  [turn_forward(): pl.pallas_call(partial(turn_forward_kernel, depth), out_shape=[jax.ShapeD...]
    convert_element_type x7 -> x0, other arithmetic: 6.57 us -> none  [the longest x2 2.09 us: split_local(): gains = [norm_gain[layer].astype(f32) for layer in range(LAYERS)]]
where the time goes in v2:
time: 451 us; the launch traced here: 442 us
  Pallas kernels  433 us (96%)
  local copies, waits for them, and re-layouts  7.92 us (2%)
    pallas_call x1, Pallas kernels, backward_first(): pl.pallas_call(partial(backward_first_kernel, depth), out_shape=shapes, i...  116 us
    pallas_call x1, Pallas kernels, backward_second(): pl.pallas_call(partial(backward_second_kernel, depth), out_shape=shapes,...  93.5 us
    pallas_call x1, Pallas kernels, turn_forward(): pl.pallas_call(partial(turn_forward_kernel, depth), out_shape=[jax.ShapeD...  79.4 us
    pallas_call x1, Pallas kernels, prepare(): pl.pallas_call(partial(prepare_kernel, depth), out_shape=shapes, in_specs...  66 us
    pallas_call x1, Pallas kernels, forward_second(): pl.pallas_call(partial(forward_second_kernel, depth), out_shape=shapes, i...  43.6 us
    pallas_call x1, Pallas kernels, forward_first(): pl.pallas_call(partial(forward_first_kernel, depth), out_shape=shapes, in...  25.3 us

profile of v2, /device:TPU:0, one launch (start us, length us, event | category | flops | bytes accessed | tf_op | source)
XLA Modules:
  0.0 441.7 jit_solution(9721284484067533996)
XLA Ops:
  0.6 1.5 copy.33.step_ref.refs_8_
  2.1 2.2 copy.34.proj_ref.refs_9_
  4.3 66.0 %prepare.1 = (bf16[16,64,1536]{2,1,0:T(8,128)(2,1)}, bf16[8,192,640]{2,1,0:T(8,128)(2,1)}, bf16[8,4,48,256]{3,2,1,0:T(8,128)(2,1)}, f32[2,16,256]{2,1,0:T(8,128)...) custom-call(bf16[1,256,1536]{2,1,0:T(8,128)(2,1)} %refs_17_.1, s32[1,256]{1,0:T(1,128)} %seg_ref.1, bf16[2,1536]{1,0:T(2,128)(2,1)} %refs_18_.1, ...), custom_call_target="tpu_custom_call" | custom-call | tf_op jit(solution)/shard_map/prepare/pallas_call | solution.py:1795
  70.4 1.3 slice_bitcast_fusion
  71.7 25.3 %forward_first.1 = (f32[1024,192]{1,0:T(8,128)}, f32[8,128]{1,0:T(8,128)}, f32[1024,192]{1,0:T(8,128)}, f32[1032,192]{1,0:T(8,128)}, f32[1032,256]{1,0:T(8,128)}...) custom-call(bf16[1024,1536]{1,0:T(8,128)(2,1)} %bitcast.19, ...), custom_call_target="tpu_custom_call" | custom-call | tf_op jit(solution)/shard_map/forward_first/pallas_call | solution.py:1950
  97.1 79.4 %turn_forward.1 = (f32[64,1536]{1,0:T(8,128)}, f32[64,1536]{1,0:T(8,128)}, f32[8,128]{1,0:T(8,128)}, bf16[16,64,1536]{2,1,0:T(8,128)(2,1)}, bf16[8,192,640]{2,1,...) custom-call(f32[1024,192]{1,0:T(8,128)} %get-tuple-element.85.gated_ref, f32[8,128]{1,0:T(8,128)} %get-tuple-element.86.squares_ref, ...), custom_call_target="tpu_custom_call" | custom-call | tf_op jit(solution)/shard_map/turn_forward/pallas_call | solution.py:1306
  176.5 43.6 %forward_second.1 = (bf16[16,64,1536]{2,1,0:T(8,128)(2,1)}, f32[8,128]{1,0:T(8,128)}, f32[1024,192]{1,0:T(8,128)}, f32[1032,192]{1,0:T(8,128)}, f32[1032,256]{1,...) custom-call(bf16[1024,1536]{1,0:T(8,128)(2,1)} %bitcast.13, ...), custom_call_target="tpu_custom_call" | custom-call | tf_op jit(solution)/shard_map/forward_second/pallas_call | solution.py:2014
  220.1 93.5 %backward_second.1 = (bf16[8,192,256]{2,1,0:T(8,128)(2,1)}, f32[16,256]{1,0:T(8,128)}, f32[64,1536]{1,0:T(8,128)}, f32[1,1536]{1,0:T(1,128)}, bf16[16,64,1792]{2...) custom-call(bf16[1024,1536]{1,0:T(8,128)(2,1)} %bitcast.26, ...), custom_call_target="tpu_custom_call" | custom-call | tf_op jit(solution)/shard_map/backward_second/pallas_call | solution.py:2142
  313.6 116.3 %backward_first.1 = (bf16[4,192,256]{2,1,0:T(8,128)(2,1)}, bf16[4,192,384]{2,1,0:T(8,128)(2,1)}, bf16[4,192,256]{2,1,0:T(8,128)(2,1)}, f32[2,192,256]{2,1,0:T(8,...) custom-call(bf16[1024,1792]{1,0:T(8,128)(2,1)} %bitcast.23, ...), custom_call_target="tpu_custom_call" | custom-call | tf_op jit(solution)/shard_map/backward_first/pallas_call | solution.py:2285
  429.9 8.8 %emit.1 = (bf16[1,256,1536]{2,1,0:T(8,128)(2,1)}, bf16[1,256,1536]{2,1,0:T(8,128)(2,1)}, f32[2,1536]{1,0:T(2,128)}, f32[2,192,768]{2,1,0:T(8,128)}, f32[2,192,76...) custom-call(bf16[4,64,1536]{2,1,0:T(8,128)(2,1)} %get-tuple-element., ...), custom_call_target="tpu_custom_call" | custom-call | tf_op jit(solution)/shard_map/emit/pallas_call | solution.py:2393
  438.7 2.9 copy.37
